TPU v7x, 128 devices: a whole 4x4x4 slice. The times are simulated.
128 devices in a mesh: row: 8 (over z, core), col: 16 (over x, y).
Axes of the slice: x: 4, y: 4, z: 4, core: 2. Of those that a mesh axis runs over, the one named last changes fastest.
Arguments:
- hamiltonian: bfloat16 [4096, 4096], P('row', 'col'), may hold values from -0.3 to 0.3
- pattern: int32 [32, 32], replicated, may hold values from 0 to 1, as said below
- tile_lists: int32 [128, 8], replicated, may hold values from 0 to 31, as said below
- orders: int32 [128], replicated, may hold values from 6 to 8
- shift: float32 [1], replicated, may hold values from -0.5 to 0.5
Outputs:
- density: bfloat16 [4096, 4096], P('row', 'col')
- php: float32 [4096, 4096], P('row', 'col')
Inputs may be any that keep to these rules, and one draw needn't show every extreme that they name: `pattern`: Symmetric, with zeros on the diagonal. `tile_lists`: row s begins with tile s * 32 // 128; its entries lie in distinct groups of 2 consecutive tiles, and the second lies in the group that shares a group of 4 consecutive tiles with the first. Entries from position orders[s] on are not used.
All inputs are finite; a program needn't handle non-finite values.
Results may differ from a plain program's by a relative error of at most 0.0073.
Values may be sent and summed in bfloat16 or wider, within the bound.
No kernel may reach another device: no remote copies, remote signals or barrier semaphores. Data moves between devices by JAX's collectives and lax.ppermute only.
A program may use at most 64 MiB of HBM per device.

v0:
```python
import jax
import jax.numpy as jnp
from jax import lax
from jax.experimental import pallas as pl
from jax.experimental.pallas import tpu as pltpu
from jax.sharding import Mesh
from jax.sharding import PartitionSpec as P

TILE = 128
MAXT = 8
NB = 32
ROWS = 8
COLS = 16
SUBS = 128
CW = 32
N = MAXT * TILE
RT = NB // ROWS
CT = NB // COLS
WIDTH = CT * TILE
ROW = ("z", "core")
COL = ("c0", "c1")
F32 = jnp.float32
BF16 = jnp.bfloat16


class Table:
    def __init__(self, ref):
        self.lists = Part(ref, 0)
        self.orders = Part(ref, SUBS * MAXT)
        self.pattern = Part(ref, SUBS * MAXT + SUBS)
        self.ids = Part(ref, SUBS * MAXT + SUBS + NB * NB)


class Part:
    def __init__(self, ref, base):
        self.ref = ref
        self.base = base

    def __getitem__(self, index):
        return self.ref[self.base + index]


def kept(pattern, a, b):
    return (pattern[a * NB + b] > 0) | (a == b)


def ring_owner(ids, k, part):
    return (ids[0] // 2 + k) % 4 * 2 + (ids[0] + part) % 2


def join_rows(ids, blocks, whole):
    for part in range(2):
        for k in range(4):
            block = blocks[part * 4 + k]
            pieces = block if isinstance(block, tuple) else (block,)
            size = RT * TILE // len(pieces)
            start = ring_owner(ids, k, part) * RT * TILE
            for number, piece in enumerate(pieces):
                whole[pl.ds(pl.multiple_of(start + number * size, size), size), :] = piece[...]


def cyclic(j, k):
    return 1 + (j - 1 + k) % (MAXT - 1)


def pack_kernel(table, *refs):
    table = Table(table)
    ids, lists, orders = table.ids, table.lists, table.orders
    halves, blocks, (out, first, strip, sems) = refs[:2], refs[2:9], refs[9:]
    join_rows(ids, (halves, *blocks), strip)

    def send(c, k, row, lanes):
        start = pl.multiple_of(row * TILE, TILE)
        lanes = pl.ds(pl.multiple_of(lanes * TILE, TILE), TILE)
        return pltpu.make_async_copy(
            strip.at[pl.ds(start, TILE), lanes], out.at[c, k], sems.at[c, k]
        )

    def one(c, _):
        s = c * ROWS + ids[0]
        which = jnp.int32(1)
        for j in range(2, MAXT):
            hit = (lists[s * MAXT + j] // CT == ids[1]) & (j < orders[s])
            which = jnp.where(hit, j, which)
        side = lists[s * MAXT + which] % CT
        for k in range(4):
            send(c, k, lists[s * MAXT + cyclic(which, k)], side).start()
        return 0

    lax.fori_loop(0, COLS, one, 0)

    def tile(a, lanes):
        return strip[pl.ds(pl.multiple_of(a * TILE, TILE), TILE), lanes]

    own = (ids[1] * ROWS + ids[0]) * MAXT
    lanes = pl.ds(pl.multiple_of(lists[own] % CT * TILE, TILE), TILE)
    for i in range(MAXT):
        first[i] = tile(lists[own + i], lanes)

    def done(c, _):
        for k in range(4):
            send(c, k, 0, 0).wait()
        return 0

    lax.fori_loop(0, COLS, done, 0)


def solve_kernel(table, shift, tiles, first, panel, x, f, y):
    table = Table(table)
    ids, lists, pattern = table.ids, table.lists, table.pattern
    s = ids[1] * ROWS + ids[0]
    order = table.orders[s]
    potential = shift[0]
    names = [lists[s * MAXT + j] for j in range(MAXT)]
    rows = lax.broadcasted_iota(jnp.int32, (TILE, TILE), 0)
    cols = lax.broadcasted_iota(jnp.int32, (TILE, TILE), 1)
    eye = jnp.where(rows == cols, 1.0, 0.0).astype(F32)

    def put(i, j, tile):
        y[pl.ds(i * TILE, TILE), pl.ds(j * TILE, TILE)] = tile

    def masked(i, j, tile):
        both = kept(pattern, names[i], names[j]) & (i < order) & (j < order)
        return jnp.where(both, tile, jnp.zeros_like(tile))

    for i in range(MAXT):
        tile = masked(i, 0, first[i])
        put(i, 0, tile)
        if i:
            put(0, i, tile.T)
            for k in range(4):
                tile = masked(cyclic(i, k), i, tiles[names[i] // CT, k])
                put(cyclic(i, k), i, tile)
                if k:
                    put(i, cyclic(i, k), tile.T)

    def shifted(i, j):
        tile = y[pl.ds(i * TILE, TILE), pl.ds(j * TILE, TILE)].astype(F32)
        if i == j:
            tile = tile - jnp.where(i < order, potential, 0.0) * eye
        return tile

    largest = jnp.zeros((), F32)
    for i in range(MAXT):
        total = jnp.zeros((TILE, TILE), F32)
        for j in range(MAXT):
            tile = shifted(i, j)
            total = total + tile * tile
        largest = jnp.maximum(largest, jnp.max(jnp.sum(total, axis=1)))
    root = jnp.sqrt(jnp.full((8, TILE), largest + 1e-06, F32))
    inverse = (1.0 / (jnp.abs(potential) + 2.0 * root))[0:1, :]
    for i in range(MAXT):
        for j in range(MAXT):
            x[pl.ds(i * TILE, TILE), pl.ds(j * TILE, TILE)] = (shifted(i, j) * inverse).astype(BF16)

    band = 256
    brow = lax.broadcasted_iota(jnp.int32, (band, N), 0)
    bcol = lax.broadcasted_iota(jnp.int32, (band, N), 1)

    def step(source, target):
        blocks = N // band
        for b in range(blocks):
            here = slice(b * band, b * band + band)
            rest = slice(b * band, N)
            q = lax.dot_general(
                source[here, :], source[:, rest], (((1,), (0,)), ((), ())), preferred_element_type=F32
            )
            diag = jnp.where(brow[:, : N - b * band] == bcol[:, : N - b * band], 1.5, 0.0)
            part = (diag - 0.5 * q).astype(BF16)
            f[here, rest] = part
            for c in range(b + 1, blocks):
                f[c * band : c * band + band, here] = part[:, (c - b) * band : (c - b + 1) * band].T
        for b in range(blocks):
            here = slice(b * band, b * band + band)
            rest = slice(b * band, N)
            part = jnp.dot(source[here, :], f[:, rest], preferred_element_type=F32).astype(BF16)
            target[here, rest] = part
            for c in range(b + 1, blocks):
                target[c * band : c * band + band, here] = part[
                    :, (c - b) * band : (c - b + 1) * band
                ].T

    step(x, y)
    step(y, x)
    offset = pl.multiple_of(s % (TILE // CW) * CW, CW)
    prow = lax.broadcasted_iota(jnp.int32, (CW, N), 0) + offset
    pcol = lax.broadcasted_iota(jnp.int32, (CW, N), 1)
    q = jnp.dot(x[pl.ds(offset, CW), :], x[...], preferred_element_type=F32)
    part = (jnp.where(prow == pcol, 1.5, 0.0) - 0.5 * q).astype(BF16)
    z = jnp.dot(part, x[...], preferred_element_type=F32)
    dens = (jnp.where(prow == pcol, 0.5, 0.0) - 0.5 * z).astype(BF16)
    for i in range(MAXT):
        panel[i] = dens[:, i * TILE : (i + 1) * TILE]


def spread_kernel(table, panels, out, mine, sems):
    table = Table(table)
    ids, lists, orders = table.ids, table.lists, table.orders
    mine[...] = jnp.zeros_like(mine)
    for k in range(ROWS):
        s = ids[1] * ROWS + k
        for i in range(MAXT):
            group = lists[s * MAXT + i] // CT

            @pl.when((i < orders[s]) & (group // (RT // CT) == ids[0]))
            def _():
                mine[k, group % (RT // CT)] = panels[k, i]

    copies = [pltpu.make_async_copy(mine, out.at[c], sems.at[c]) for c in range(COLS)]
    for copy in copies:
        copy.start()
    for copy in copies:
        copy.wait()


def hp_kernel(table, a0, a1, a2, a3, b0, b1, b2, b3, panels, hp, pt, wide):
    table = Table(table)
    ids, lists, orders, pattern = table.ids, table.lists, table.orders, table.pattern
    half = RT * TILE // 2
    c0 = ids[1] // 4
    c1 = ids[1] % 4
    for k in range(4):
        for m in range(4):
            first = (c0 + k) % 4 * 4 + (c1 + m) % 4
            second = (c0 + m) % 4 * 4 + (c1 + k) % 4
            for part, ref, col in ((0, (a0, a1, a2, a3)[k], first), (1, (b0, b1, b2, b3)[k], second)):
                for i in range(RT // 2):
                    for j in range(CT):
                        a = part * (RT // 2) + i
                        b = col * CT + j
                        tile = ref[m, pl.ds(i * TILE, TILE), pl.ds(j * TILE, TILE)]
                        live = kept(pattern, ids[0] * RT + a, b)
                        wide[
                            pl.ds(a * TILE, TILE), pl.ds(pl.multiple_of(b * TILE, TILE), TILE)
                        ] = jnp.where(live, tile, jnp.zeros_like(tile))
    pt[...] = jnp.zeros_like(pt)
    for k in range(ROWS):
        s = ids[1] * ROWS + k
        for i in range(MAXT):

            @pl.when(i < orders[s])
            def _():
                where = pl.multiple_of(lists[s * MAXT + i] * TILE, TILE)
                pt[pl.ds(k * CW, CW), pl.ds(where, TILE)] = panels[k, i]

    hp[...] = lax.dot_general(
        wide[...], pt[...], (((1,), (1,)), ((), ())), preferred_element_type=F32
    ).astype(BF16)


def final_kernel(table, present, pieces, *refs):
    blocks = refs[:8]
    density, php, pt, hp = refs[8:]
    ids = Table(table).ids
    join_rows(ids, blocks, hp)

    def place(c, _):
        for r in range(ROWS):
            s = c * ROWS + r
            here = pl.ds(pl.multiple_of(s * CW, CW), CW)
            for g in range(RT // CT):
                piece = pieces[c, r, g]
                for a in range(g * CT, g * CT + CT):
                    live = present[s * RT + a] > 0
                    pt[here, pl.ds(a * TILE, TILE)] = jnp.where(live, piece, jnp.zeros_like(piece))
        return 0

    lax.fori_loop(0, COLS, place, 0)
    php[...] = lax.dot_general(
        pt[...], hp[...], (((0,), (0,)), ((), ())), preferred_element_type=F32
    )
    mine = pt[pl.ds(pl.multiple_of(ids[1] * WIDTH, WIDTH), WIDTH), :]
    density[...] = mine.T


def from_ring(x, axis):
    return [x] + [lax.ppermute(x, axis, [((i + k) % 4, i) for i in range(4)]) for k in range(1, 4)]


def swapped(x):
    return lax.ppermute(x, "core", [(0, 1), (1, 0)])


SMEM = pl.BlockSpec(memory_space=pltpu.SMEM)
LOCAL = pl.BlockSpec(memory_space=pltpu.VMEM)
FAR = pl.BlockSpec(memory_space=pl.ANY)


def call(kernel, outs, scratch, small, large, specs=LOCAL):
    return pl.pallas_call(
        kernel,
        out_shape=outs,
        in_specs=[SMEM] * len(small) + [LOCAL] * len(large),
        out_specs=specs,
        scratch_shapes=scratch,
        compiler_params=pltpu.CompilerParams(vmem_limit_bytes=24 << 20),
    )(*small, *[pltpu.with_memory_space_constraint(x, pltpu.VMEM) for x in large])


def call_solve(table, shift, tiles, first):
    return call(
        solve_kernel,
        pltpu.VMEM((MAXT, CW, TILE), BF16),
        [pltpu.VMEM((N, N), BF16)] * 3,
        (table, shift),
        (tiles, first),
    )


def steps(hamiltonian, pattern, tile_lists, orders, shift):
    row = lax.axis_index(ROW)
    col = lax.axis_index(COL)
    ids = jnp.stack([row, col]).astype(jnp.int32)
    table = jnp.concatenate([tile_lists.reshape(-1), orders, pattern.reshape(-1), ids])
    half = RT * TILE // 2
    top, bottom = hamiltonian[:half], hamiltonian[half:]
    strip = from_ring(hamiltonian, "z")
    ahead = jnp.stack(from_ring(top, "c1"))
    across = jnp.stack(from_ring(bottom, "c0"))
    strip = strip + [swapped(x) for x in strip]
    packed, first = call(
        pack_kernel,
        (pltpu.HBM((COLS, 4, TILE, TILE), BF16), pltpu.VMEM((MAXT, TILE, TILE), BF16)),
        [pltpu.VMEM((NB * TILE, WIDTH), BF16), pltpu.SemaphoreType.DMA((COLS, 4))],
        (table,),
        (top, bottom, *strip[1:]),
        (FAR, LOCAL),
    )
    packed, ahead, across = lax.optimization_barrier((packed, ahead, across))
    tiles = lax.all_to_all(packed, COL, 0, 0, tiled=True)
    ahead = from_ring(ahead, "c0")
    across = from_ring(across, "c1")
    panel = call_solve(table, shift, tiles, first)
    panels = lax.all_gather(panel, ROW, axis=0, tiled=False)
    spread = call(
        spread_kernel,
        pltpu.HBM((COLS, ROWS, RT // CT, CW, TILE), BF16),
        [pltpu.VMEM((ROWS, RT // CT, CW, TILE), BF16), pltpu.SemaphoreType.DMA((COLS,))],
        (table,),
        (panels,),
        FAR,
    )
    arrived = lax.all_to_all(spread, COL, 0, 0, tiled=True)
    hp = call(
        hp_kernel,
        pltpu.VMEM((RT * TILE, WIDTH), BF16),
        [pltpu.VMEM((WIDTH, NB * TILE), BF16), pltpu.VMEM((RT * TILE, NB * TILE), BF16)],
        (table,),
        (*ahead, *across, panels),
    )
    ours = from_ring(hp, "z")
    theirs = [swapped(x) for x in ours]
    own = row * RT + jnp.arange(RT, dtype=jnp.int32)
    live = jnp.arange(MAXT, dtype=jnp.int32)[None, :] < orders[:, None]
    present = jnp.any((tile_lists[:, None, :] == own[None, :, None]) & live[:, None, :], axis=2)
    density, php = call(
        final_kernel,
        (
            jax.ShapeDtypeStruct((RT * TILE, WIDTH), BF16),
            jax.ShapeDtypeStruct((RT * TILE, WIDTH), F32),
        ),
        [pltpu.VMEM((NB * TILE, RT * TILE), BF16), pltpu.VMEM((NB * TILE, WIDTH), BF16)],
        (table, present.astype(jnp.int32).reshape(-1)),
        (arrived, *ours, *theirs),
        (LOCAL, LOCAL),
    )
    return density, php


def solution(mesh):
    fine = Mesh(mesh.devices.reshape(4, 2, 4, 4), ("z", "core", "c0", "c1"))
    split = P(ROW, COL)
    return jax.shard_map(
        steps,
        mesh=fine,
        in_specs=(split, P(), P(), P(), P()),
        out_specs=(split, split),
        check_vma=False,
    )
```

profile of v0, /device:TPU:1, one launch (start us, length us, event | category | flops | bytes accessed | tf_op | source)
XLA Modules:
  0.0 182.7 jit_solution(953443198679965586)
XLA Ops:
  0.6 1.0 slice_bitcast_fusion
  1.6 3.6 %collective-permute-start.7 = (bf16[256,256]{1,0:T(8,128)(2,1)S(1)}, bf16[256,256]{1,0:T(8,128)(2,1)S(1)}, u32[]{:S(2)}, u32[]{:S(2)}) collective-permute-start(bf16[256,256]{1,0:T(8,128)(2,1)S(1)} %get-tuple-element.15.refs_0_), channel_id=1, source_target_pairs={{1,0},{2,1},{3,2},{0,3},{5,4},{6,5},{7,6},{4,7},{9,8},{10,9},{11,1... | collective-permute-start | bytes 393224 | tf_op jit(solution)/shard_map/ppermute | solution.py:277
  5.3 0.3 collective-permute-start.8
  5.6 3.8 %collective-permute-start = (bf16[512,256]{1,0:T(8,128)(2,1)}, bf16[512,256]{1,0:T(8,128)(2,1)S(1)}, u32[]{:S(2)}, u32[]{:S(2)}) collective-permute-start(bf16[512,256]{1,0:T(8,128)(2,1)} %param.5), channel_id=1, source_target_pairs={{32,0},{64,32},{96,64},{0,96},{33,1},{65,33},{97,65},{1,97},{34,2}... | collective-permute-start | bytes 786440 | tf_op jit(solution)/shard_map/ppermute | solution.py:277
  9.4 0.0 collective-permute-start.1
  9.4 0.7 collective-permute-start.2
  10.1 0.2 collective-permute-done.7
  10.3 0.5 collective-permute-start.9
  10.8 2.5 %collective-permute-start.10 = (bf16[256,256]{1,0:T(8,128)(2,1)S(1)}, bf16[256,256]{1,0:T(8,128)(2,1)S(1)}, u32[]{:S(2)}, u32[]{:S(2)}) collective-permute-start(bf16[256,256]{1,0:T(8,128)(2,1)S(1)} %get-tuple-element.14.refs_1_), channel_id=1, source_target_pairs={{4,0},{8,4},{12,8},{0,12},{5,1},{9,5},{13,9},{1,13},{6,2},{10,6},{... | collective-permute-start | bytes 393224 | tf_op jit(solution)/shard_map/ppermute | solution.py:277
  13.2 3.3 %collective-permute-done.9 = bf16[256,256]{1,0:T(8,128)(2,1)S(1)} collective-permute-done((bf16[256,256]{1,0:T(8,128)(2,1)S(1)}, bf16[256,256]{1,0:T(8,128)(2,1)S(1)}, u32[]{:S(2)}, u32[]{:S(2)}) %collective-permute-start.9) | collective-permute-done | bytes 131104 | tf_op jit(solution)/shard_map/ppermute | solution.py:277
  16.5 2.7 %collective-permute-start.11 = (bf16[256,256]{1,0:T(8,128)(2,1)S(1)}, bf16[256,256]{1,0:T(8,128)(2,1)S(1)}, u32[]{:S(2)}, u32[]{:S(2)}) collective-permute-start(bf16[256,256]{1,0:T(8,128)(2,1)S(1)} %get-tuple-element.14.refs_1_), channel_id=1, source_target_pairs={{8,0},{12,4},{0,8},{4,12},{9,1},{13,5},{1,9},{5,13},{10,2},{14,6},... | collective-permute-start | bytes 393224 | tf_op jit(solution)/shard_map/ppermute | solution.py:277
  19.2 2.2 %collective-permute-start.3 = (bf16[512,256]{1,0:T(8,128)(2,1)}, bf16[512,256]{1,0:T(8,128)(2,1)S(1)}, u32[]{:S(2)}, u32[]{:S(2)}) collective-permute-start(bf16[512,256]{1,0:T(8,128)(2,1)} %param.5), channel_id=1, source_target_pairs={{0,16},{16,0},{1,17},{17,1},{2,18},{18,2},{3,19},{19,3},{4,20},{20... | collective-permute-start | bytes 786440 | tf_op jit(solution)/shard_map/ppermute | solution.py:281
  21.4 0.0 collective-permute-done.refs_2_
  21.4 0.4 collective-permute-start.4
  21.8 0.1 collective-permute-start.5
  22.0 2.4 %collective-permute-done.2.refs_4_ = bf16[512,256]{1,0:T(8,128)(2,1)S(1)} collective-permute-done((bf16[512,256]{1,0:T(8,128)(2,1)}, bf16[512,256]{1,0:T(8,128)(2,1)S(1)}, u32[]{:S(2)}, u32[]{:S(2)}) %collective-permute-start.2) | collective-permute-done | bytes 262176 | tf_op jit(solution)/shard_map/ppermute | solution.py:277
  24.3 0.8 collective-permute-start.6
  25.1 1.2 collective-permute-start.12
  26.3 0.8 copy.12
  27.1 0.1 reshape.36
  27.2 0.8 reshape.37
  28.0 0.7 concatenate.3.table
  28.7 0.1 pad_maximum_fusion.a0
  28.8 2.7 %collective-permute-done.12 = bf16[256,256]{1,0:T(8,128)(2,1)} collective-permute-done((bf16[256,256]{1,0:T(8,128)(2,1)S(1)}, bf16[256,256]{1,0:T(8,128)(2,1)}, u32[]{:S(2)}, u32[]{:S(2)}) %collective-permute-start.12) | collective-permute-done | bytes 131104 | tf_op jit(solution)/shard_map/ppermute | solution.py:277
  31.5 1.8 pad_maximum_fusion.1.b0
  33.3 0.0 collective-permute-done.6.refs_8_
  33.3 3.3 %shard_map.68 = (bf16[16,4,128,128]{3,2,1,0:T(8,128)(2,1)}, bf16[8,128,128]{2,1,0:T(8,128)(2,1)S(1)}) custom-call(s32[2178]{0:T(1024)S(1)} %concatenate.3.table, bf16[256,256]{1,0:T(8,128)(2,1)S(1)} %get-tuple-element.15.refs_0_, bf16[256,256]{1,0:T(8,128)(2,1)S(1)} %get-tuple-element.14.refs_1_, bf16[512,256]{1,0:T(8,128)(2,1)S(1)} %collective-permute-done.refs_2_, ...), custom_call_target="tpu_custom_call" | custom-call | tf_op jit(solution)/shard_map/pallas_call | solution.py:290
  36.6 5.3 %all-to-all-start = ((bf16[16,4,128,128]{3,2,1,0:T(8,128)(2,1)}), bf16[16,4,128,128]{3,2,1,0:T(8,128)(2,1)S(1)}, u32[]{:S(2)}, u32[]{:S(2)}) async-start(bf16[16,4,128,128]{3,2,1,0:T(8,128)(2,1)} %get-tuple-element.8), calls=%async_computation | async-start | bytes 4194304 | tf_op jit(solution)/shard_map/all_to_all | solution.py:330
  42.5 26.3 %all-to-all-done.tiles = bf16[16,4,128,128]{3,2,1,0:T(8,128)(2,1)S(1)} async-done(((bf16[16,4,128,128]{3,2,1,0:T(8,128)(2,1)}), bf16[16,4,128,128]{3,2,1,0:T(8,128)(2,1)S(1)}, u32[]{:S(2)}, u32[]{:S(2)}) %all-to-all-start) | async-done | bytes 2097184 | tf_op jit(solution)/shard_map/all_to_all | solution.py:330
  68.8 8.8 %shard_map.69 = bf16[8,32,128]{2,1,0:T(8,128)(2,1)S(1)} custom-call(s32[2178]{0:T(1024)S(1)} %concatenate.3.table, f32[1]{0:T(128)S(6)} %copy.14.shift, bf16[16,4,128,128]{3,2,1,0:T(8,128)(2,1)S(1)} %all-to-all-done.tiles, bf16[8,128,128]{2,1,0:T(8,128)(2,1)S(1)} %get-tuple-element.9.first), custom_call_target="tpu_custom_call" | custom-call | tf_op jit(solution)/shard_map/pallas_call | solution.py:290
  77.6 17.2 %all-gather = bf16[64,32,128]{2,1,0:T(8,128)(2,1)S(1)} all-gather(bf16[8,32,128]{2,1,0:T(8,128)(2,1)S(1)} %shard_map.69), channel_id=2, replica_groups=mesh['z'=4,'core'=2,'c0'=4,'c1'=4] {'z','core'}, dimensions={0}, use_global_device_ids=true | all-gather | bytes 589824 | tf_op jit(solution)/shard_map/all_gather | solution.py:334
  94.8 3.6 %shard_map.70 = bf16[16,8,2,32,128]{4,3,2,1,0:T(8,128)(2,1)} custom-call(s32[2178]{0:T(1024)S(1)} %concatenate.3.table, bf16[8,8,32,128]{3,2,1,0:T(8,128)(2,1)S(1)} %bitcast.13), custom_call_target="tpu_custom_call" | custom-call | tf_op jit(solution)/shard_map/pallas_call | solution.py:290
  98.3 0.0 copy-start.2
  98.3 0.0 copy-start.1
  98.3 3.7 %all-to-all-start.1 = ((bf16[16,8,2,32,128]{4,3,2,1,0:T(8,128)(2,1)}), bf16[16,8,2,32,128]{4,3,2,1,0:T(8,128)(2,1)S(1)}, u32[]{:S(2)}, u32[]{:S(2)}) async-start(bf16[16,8,2,32,128]{4,3,2,1,0:T(8,128)(2,1)} %shard_map.70), calls=%async_computation.1 | async-start | bytes 4194304 | tf_op jit(solution)/shard_map/all_to_all | solution.py:343
  102.1 2.5 %collective-permute-start.13 = (bf16[4,256,256]{2,1,0:T(8,128)(2,1)S(1)}, bf16[4,256,256]{2,1,0:T(8,128)(2,1)S(1)}, u32[]{:S(2)}, u32[]{:S(2)}) collective-permute-start(bf16[4,256,256]{2,1,0:T(8,128)(2,1)S(1)} %pad_maximum_fusion.a0), channel_id=1, source_target_pairs={{4,0},{8,4},{12,8},{0,12},{5,1},{9,5},{13,9},{1,13},{6,2},{10,6},{... | collective-permute-start | bytes 1572872 | tf_op jit(solution)/shard_map/ppermute | solution.py:277
  104.6 0.5 collective-permute-start.14
  105.1 0.6 collective-permute-start.15
  105.7 2.4 %collective-permute-start.16 = (bf16[4,256,256]{2,1,0:T(8,128)(2,1)}, bf16[4,256,256]{2,1,0:T(8,128)(2,1)S(1)}, u32[]{:S(2)}, u32[]{:S(2)}) collective-permute-start(bf16[4,256,256]{2,1,0:T(8,128)(2,1)} %pad_maximum_fusion.1.b0), channel_id=1, source_target_pairs={{1,0},{2,1},{3,2},{0,3},{5,4},{6,5},{7,6},{4,7},{9,8},{10,9},{11,1... | collective-permute-start | bytes 1572872 | tf_op jit(solution)/shard_map/ppermute | solution.py:277
  108.2 0.6 collective-permute-start.17
  108.7 29.6 %collective-permute-done.13.a1 = bf16[4,256,256]{2,1,0:T(8,128)(2,1)S(1)} collective-permute-done((bf16[4,256,256]{2,1,0:T(8,128)(2,1)S(1)}, bf16[4,256,256]{2,1,0:T(8,128)(2,1)S(1)}, u32[]{:S(2)}, u32[]{:S(2)}) %collective-permute-start.13) | collective-permute-done | bytes 524320 | tf_op jit(solution)/shard_map/ppermute | solution.py:277
  138.4 1.3 collective-permute-start.18
  139.7 2.4 %collective-permute-done.14.a2 = bf16[4,256,256]{2,1,0:T(8,128)(2,1)S(1)} collective-permute-done((bf16[4,256,256]{2,1,0:T(8,128)(2,1)S(1)}, bf16[4,256,256]{2,1,0:T(8,128)(2,1)S(1)}, u32[]{:S(2)}, u32[]{:S(2)}) %collective-permute-start.14) | collective-permute-done | bytes 524320 | tf_op jit(solution)/shard_map/ppermute | solution.py:277
  142.1 9.1 %collective-permute-done.15.a3 = bf16[4,256,256]{2,1,0:T(8,128)(2,1)S(1)} collective-permute-done((bf16[4,256,256]{2,1,0:T(8,128)(2,1)S(1)}, bf16[4,256,256]{2,1,0:T(8,128)(2,1)S(1)}, u32[]{:S(2)}, u32[]{:S(2)}) %collective-permute-start.15) | collective-permute-done | bytes 524320 | tf_op jit(solution)/shard_map/ppermute | solution.py:277
  151.2 0.0 collective-permute-done.16.b1
  151.2 0.0 collective-permute-done.17.b2
  151.2 3.7 %collective-permute-done.18.b3 = bf16[4,256,256]{2,1,0:T(8,128)(2,1)S(1)} collective-permute-done((bf16[4,256,256]{2,1,0:T(8,128)(2,1)}, bf16[4,256,256]{2,1,0:T(8,128)(2,1)S(1)}, u32[]{:S(2)}, u32[]{:S(2)}) %collective-permute-start.18) | collective-permute-done | bytes 524320 | tf_op jit(solution)/shard_map/ppermute | solution.py:277
  154.9 1.0 copy-done
  155.9 4.7 %shard_map.71.refs_0_ = bf16[512,256]{1,0:T(8,128)(2,1)S(1)} custom-call(s32[2178]{0:T(1024)S(1)} %concatenate.3.table, bf16[4,256,256]{2,1,0:T(8,128)(2,1)S(1)} %pad_maximum_fusion.a0, bf16[4,256,256]{2,1,0:T(8,128)(2,1)S(1)} %collective-permute-done.13.a1, bf16[4,256,256]{2,1,0:T(8,128)(2,1)S(1)} %collective-permute-done.14.a2, ...), custom_call_target="tpu_custom_call" | custom-call | tf_op jit(solution)/shard_map/pallas_call | solution.py:290
  160.6 0.1 collective-permute-start.19
  160.7 1.3 collective-permute-start.20
  162.0 0.8 collective-permute-start.21
  162.7 3.3 %collective-permute-start.22 = (bf16[512,256]{1,0:T(8,128)(2,1)S(1)}, bf16[512,256]{1,0:T(8,128)(2,1)S(1)}, u32[]{:S(2)}, u32[]{:S(2)}) collective-permute-start(bf16[512,256]{1,0:T(8,128)(2,1)S(1)} %shard_map.71.refs_0_), channel_id=1, source_target_pairs={{0,16},{16,0},{1,17},{17,1},{2,18},{18,2},{3,19},{19,3},{4,20},{20... | collective-permute-start | bytes 786440 | tf_op jit(solution)/shard_map/ppermute | solution.py:281
  166.0 0.0 collective-permute-done.19.refs_1_
  166.0 6.2 %collective-permute-start.23 = (bf16[512,256]{1,0:T(8,128)(2,1)S(1)}, bf16[512,256]{1,0:T(8,128)(2,1)}, u32[]{:S(2)}, u32[]{:S(2)}) collective-permute-start(bf16[512,256]{1,0:T(8,128)(2,1)S(1)} %collective-permute-done.19.refs_1_), channel_id=1, source_target_pairs={{0,16},{16,0},{1,17},{17,1},{2,18},{18,2},{3,19},{19,3},{4,20},{20... | collective-permute-start | bytes 786440 | tf_op jit(solution)/shard_map/ppermute | solution.py:281
  172.2 0.0 collective-permute-done.20.refs_2_
  172.2 1.6 collective-permute-start.24
  173.9 1.7 collective-permute-done.21.refs_3_
  175.6 1.1 collective-permute-start.25
  176.6 0.1 and_reduce_fusion
  176.7 0.1 copy.13
  176.9 0.1 reshape.38.present
  177.0 0.9 collective-permute-done.25.refs_7_
  177.9 4.8 %shard_map.72 = (bf16[512,256]{1,0:T(8,128)(2,1)}, f32[512,256]{1,0:T(8,128)}) custom-call(s32[2178]{0:T(1024)S(1)} %concatenate.3.table, s32[512]{0:T(512)S(1)} %reshape.38.present, bf16[16,8,2,32,128]{4,3,2,1,0:T(8,128)(2,1)S(1)} %all-to-all-done.1.pieces, bf16[512,256]{1,0:T(8,128)(2,1)S(1)} %shard_map.71.refs_0_, ...), custom_call_target="tpu_custom_call" | custom-call | tf_op jit(solution)/shard_map/pallas_call | solution.py:290
  (17 shorter events, 0.1 us)
Async XLA Ops:
  1.6 8.7 %collective-permute-start.7 = (bf16[256,256]{1,0:T(8,128)(2,1)S(1)}, bf16[256,256]{1,0:T(8,128)(2,1)S(1)}, u32[]{:S(2)}, u32[]{:S(2)}) collective-permute-start(bf16[256,256]{1,0:T(8,128)(2,1)S(1)} %get-tuple-element.15.refs_0_), channel_id=1, source_target_pairs={{1,0},{2,1},{3,2},{0,3},{5,4},{6,5},{7,6},{4,7},{9,8},{10,9},{11,1... | collective-permute-start | bytes 393224 | tf_op jit(solution)/shard_map/ppermute | solution.py:277
  5.3 5.5 %collective-permute-start.8 = (bf16[256,256]{1,0:T(8,128)(2,1)S(1)}, bf16[256,256]{1,0:T(8,128)(2,1)S(1)}, u32[]{:S(2)}, u32[]{:S(2)}) collective-permute-start(bf16[256,256]{1,0:T(8,128)(2,1)S(1)} %get-tuple-element.15.refs_0_), channel_id=1, source_target_pairs={{2,0},{3,1},{0,2},{1,3},{6,4},{7,5},{4,6},{5,7},{10,8},{11,9},{8,1... | collective-permute-start | bytes 393224 | tf_op jit(solution)/shard_map/ppermute | solution.py:277
  5.6 15.8 %collective-permute-start = (bf16[512,256]{1,0:T(8,128)(2,1)}, bf16[512,256]{1,0:T(8,128)(2,1)S(1)}, u32[]{:S(2)}, u32[]{:S(2)}) collective-permute-start(bf16[512,256]{1,0:T(8,128)(2,1)} %param.5), channel_id=1, source_target_pairs={{32,0},{64,32},{96,64},{0,96},{33,1},{65,33},{97,65},{1,97},{34,2}... | collective-permute-start | bytes 786440 | tf_op jit(solution)/shard_map/ppermute | solution.py:277
  9.4 12.5 %collective-permute-start.1 = (bf16[512,256]{1,0:T(8,128)(2,1)}, bf16[512,256]{1,0:T(8,128)(2,1)S(1)}, u32[]{:S(2)}, u32[]{:S(2)}) collective-permute-start(bf16[512,256]{1,0:T(8,128)(2,1)} %param.5), channel_id=1, source_target_pairs={{64,0},{96,32},{0,64},{32,96},{65,1},{97,33},{1,65},{33,97},{66,2}... | collective-permute-start | bytes 786440 | tf_op jit(solution)/shard_map/ppermute | solution.py:277
  9.4 15.0 %collective-permute-start.2 = (bf16[512,256]{1,0:T(8,128)(2,1)}, bf16[512,256]{1,0:T(8,128)(2,1)S(1)}, u32[]{:S(2)}, u32[]{:S(2)}) collective-permute-start(bf16[512,256]{1,0:T(8,128)(2,1)} %param.5), channel_id=1, source_target_pairs={{96,0},{0,32},{32,64},{64,96},{97,1},{1,33},{33,65},{65,97},{98,2}... | collective-permute-start | bytes 786440 | tf_op jit(solution)/shard_map/ppermute | solution.py:277
  10.3 6.2 %collective-permute-start.9 = (bf16[256,256]{1,0:T(8,128)(2,1)S(1)}, bf16[256,256]{1,0:T(8,128)(2,1)S(1)}, u32[]{:S(2)}, u32[]{:S(2)}) collective-permute-start(bf16[256,256]{1,0:T(8,128)(2,1)S(1)} %get-tuple-element.15.refs_0_), channel_id=1, source_target_pairs={{3,0},{0,1},{1,2},{2,3},{7,4},{4,5},{5,6},{6,7},{11,8},{8,9},{9,10... | collective-permute-start | bytes 393224 | tf_op jit(solution)/shard_map/ppermute | solution.py:277
  10.8 8.5 %collective-permute-start.10 = (bf16[256,256]{1,0:T(8,128)(2,1)S(1)}, bf16[256,256]{1,0:T(8,128)(2,1)S(1)}, u32[]{:S(2)}, u32[]{:S(2)}) collective-permute-start(bf16[256,256]{1,0:T(8,128)(2,1)S(1)} %get-tuple-element.14.refs_1_), channel_id=1, source_target_pairs={{4,0},{8,4},{12,8},{0,12},{5,1},{9,5},{13,9},{1,13},{6,2},{10,6},{... | collective-permute-start | bytes 393224 | tf_op jit(solution)/shard_map/ppermute | solution.py:277
  16.5 8.6 %collective-permute-start.11 = (bf16[256,256]{1,0:T(8,128)(2,1)S(1)}, bf16[256,256]{1,0:T(8,128)(2,1)S(1)}, u32[]{:S(2)}, u32[]{:S(2)}) collective-permute-start(bf16[256,256]{1,0:T(8,128)(2,1)S(1)} %get-tuple-element.14.refs_1_), channel_id=1, source_target_pairs={{8,0},{12,4},{0,8},{4,12},{9,1},{13,5},{1,9},{5,13},{10,2},{14,6},... | collective-permute-start | bytes 393224 | tf_op jit(solution)/shard_map/ppermute | solution.py:277
  19.2 14.0 %collective-permute-start.3 = (bf16[512,256]{1,0:T(8,128)(2,1)}, bf16[512,256]{1,0:T(8,128)(2,1)S(1)}, u32[]{:S(2)}, u32[]{:S(2)}) collective-permute-start(bf16[512,256]{1,0:T(8,128)(2,1)} %param.5), channel_id=1, source_target_pairs={{0,16},{16,0},{1,17},{17,1},{2,18},{18,2},{3,19},{19,3},{4,20},{20... | collective-permute-start | bytes 786440 | tf_op jit(solution)/shard_map/ppermute | solution.py:281
  21.4 11.8 %collective-permute-start.4 = (bf16[512,256]{1,0:T(8,128)(2,1)S(1)}, bf16[512,256]{1,0:T(8,128)(2,1)S(1)}, u32[]{:S(2)}, u32[]{:S(2)}) collective-permute-start(bf16[512,256]{1,0:T(8,128)(2,1)S(1)} %collective-permute-done.refs_2_), channel_id=1, source_target_pairs={{0,16},{16,0},{1,17},{17,1},{2,18},{18,2},{3,19},{19,3},{4,20},{20... | collective-permute-start | bytes 786440 | tf_op jit(solution)/shard_map/ppermute | solution.py:281
  21.8 11.5 %collective-permute-start.5 = (bf16[512,256]{1,0:T(8,128)(2,1)S(1)}, bf16[512,256]{1,0:T(8,128)(2,1)S(1)}, u32[]{:S(2)}, u32[]{:S(2)}) collective-permute-start(bf16[512,256]{1,0:T(8,128)(2,1)S(1)} %collective-permute-done.1.refs_3_), channel_id=1, source_target_pairs={{0,16},{16,0},{1,17},{17,1},{2,18},{18,2},{3,19},{19,3},{4,20},{20... | collective-permute-start | bytes 786440 | tf_op jit(solution)/shard_map/ppermute | solution.py:281
  24.3 8.9 %collective-permute-start.6 = (bf16[512,256]{1,0:T(8,128)(2,1)S(1)}, bf16[512,256]{1,0:T(8,128)(2,1)S(1)}, u32[]{:S(2)}, u32[]{:S(2)}) collective-permute-start(bf16[512,256]{1,0:T(8,128)(2,1)S(1)} %collective-permute-done.2.refs_4_), channel_id=1, source_target_pairs={{0,16},{16,0},{1,17},{17,1},{2,18},{18,2},{3,19},{19,3},{4,20},{20... | collective-permute-start | bytes 786440 | tf_op jit(solution)/shard_map/ppermute | solution.py:281
  25.1 6.4 %collective-permute-start.12 = (bf16[256,256]{1,0:T(8,128)(2,1)S(1)}, bf16[256,256]{1,0:T(8,128)(2,1)}, u32[]{:S(2)}, u32[]{:S(2)}) collective-permute-start(bf16[256,256]{1,0:T(8,128)(2,1)S(1)} %get-tuple-element.14.refs_1_), channel_id=1, source_target_pairs={{12,0},{0,4},{4,8},{8,12},{13,1},{1,5},{5,9},{9,13},{14,2},{2,6},{... | collective-permute-start | bytes 393224 | tf_op jit(solution)/shard_map/ppermute | solution.py:277
  36.6 32.2 %all-to-all-start = ((bf16[16,4,128,128]{3,2,1,0:T(8,128)(2,1)}), bf16[16,4,128,128]{3,2,1,0:T(8,128)(2,1)S(1)}, u32[]{:S(2)}, u32[]{:S(2)}) async-start(bf16[16,4,128,128]{3,2,1,0:T(8,128)(2,1)} %get-tuple-element.8), calls=%async_computation | async-start | bytes 4194304 | tf_op jit(solution)/shard_map/all_to_all | solution.py:330
  98.3 78.3 %copy-start.2 = (s32[128]{0:T(128)S(1)}, s32[128]{0:T(128)}, u32[]{:S(2)}) copy-start(s32[128]{0:T(128)} %param.8) | copy-start | bytes 1540
  98.3 78.3 %copy-start.1 = (s32[128,8]{0,1:T(8,128)S(1)}, s32[128,8]{0,1:T(8,128)}, u32[]{:S(2)}) copy-start(s32[128,8]{0,1:T(8,128)} %param.7) | copy-start | bytes 12292
  98.3 79.6 %all-to-all-start.1 = ((bf16[16,8,2,32,128]{4,3,2,1,0:T(8,128)(2,1)}), bf16[16,8,2,32,128]{4,3,2,1,0:T(8,128)(2,1)S(1)}, u32[]{:S(2)}, u32[]{:S(2)}) async-start(bf16[16,8,2,32,128]{4,3,2,1,0:T(8,128)(2,1)} %shard_map.70), calls=%async_computation.1 | async-start | bytes 4194304 | tf_op jit(solution)/shard_map/all_to_all | solution.py:343
  102.1 36.3 %collective-permute-start.13 = (bf16[4,256,256]{2,1,0:T(8,128)(2,1)S(1)}, bf16[4,256,256]{2,1,0:T(8,128)(2,1)S(1)}, u32[]{:S(2)}, u32[]{:S(2)}) collective-permute-start(bf16[4,256,256]{2,1,0:T(8,128)(2,1)S(1)} %pad_maximum_fusion.a0), channel_id=1, source_target_pairs={{4,0},{8,4},{12,8},{0,12},{5,1},{9,5},{13,9},{1,13},{6,2},{10,6},{... | collective-permute-start | bytes 1572872 | tf_op jit(solution)/shard_map/ppermute | solution.py:277
  104.6 37.5 %collective-permute-start.14 = (bf16[4,256,256]{2,1,0:T(8,128)(2,1)S(1)}, bf16[4,256,256]{2,1,0:T(8,128)(2,1)S(1)}, u32[]{:S(2)}, u32[]{:S(2)}) collective-permute-start(bf16[4,256,256]{2,1,0:T(8,128)(2,1)S(1)} %pad_maximum_fusion.a0), channel_id=1, source_target_pairs={{8,0},{12,4},{0,8},{4,12},{9,1},{13,5},{1,9},{5,13},{10,2},{14,6},... | collective-permute-start | bytes 1572872 | tf_op jit(solution)/shard_map/ppermute | solution.py:277
  105.1 46.1 %collective-permute-start.15 = (bf16[4,256,256]{2,1,0:T(8,128)(2,1)S(1)}, bf16[4,256,256]{2,1,0:T(8,128)(2,1)S(1)}, u32[]{:S(2)}, u32[]{:S(2)}) collective-permute-start(bf16[4,256,256]{2,1,0:T(8,128)(2,1)S(1)} %pad_maximum_fusion.a0), channel_id=1, source_target_pairs={{12,0},{0,4},{4,8},{8,12},{13,1},{1,5},{5,9},{9,13},{14,2},{2,6},{... | collective-permute-start | bytes 1572872 | tf_op jit(solution)/shard_map/ppermute | solution.py:277
  105.7 45.5 %collective-permute-start.16 = (bf16[4,256,256]{2,1,0:T(8,128)(2,1)}, bf16[4,256,256]{2,1,0:T(8,128)(2,1)S(1)}, u32[]{:S(2)}, u32[]{:S(2)}) collective-permute-start(bf16[4,256,256]{2,1,0:T(8,128)(2,1)} %pad_maximum_fusion.1.b0), channel_id=1, source_target_pairs={{1,0},{2,1},{3,2},{0,3},{5,4},{6,5},{7,6},{4,7},{9,8},{10,9},{11,1... | collective-permute-start | bytes 1572872 | tf_op jit(solution)/shard_map/ppermute | solution.py:277
  108.2 43.0 %collective-permute-start.17 = (bf16[4,256,256]{2,1,0:T(8,128)(2,1)}, bf16[4,256,256]{2,1,0:T(8,128)(2,1)S(1)}, u32[]{:S(2)}, u32[]{:S(2)}) collective-permute-start(bf16[4,256,256]{2,1,0:T(8,128)(2,1)} %pad_maximum_fusion.1.b0), channel_id=1, source_target_pairs={{2,0},{3,1},{0,2},{1,3},{6,4},{7,5},{4,6},{5,7},{10,8},{11,9},{8,1... | collective-permute-start | bytes 1572872 | tf_op jit(solution)/shard_map/ppermute | solution.py:277
  138.4 16.5 %collective-permute-start.18 = (bf16[4,256,256]{2,1,0:T(8,128)(2,1)}, bf16[4,256,256]{2,1,0:T(8,128)(2,1)S(1)}, u32[]{:S(2)}, u32[]{:S(2)}) collective-permute-start(bf16[4,256,256]{2,1,0:T(8,128)(2,1)} %pad_maximum_fusion.1.b0), channel_id=1, source_target_pairs={{3,0},{0,1},{1,2},{2,3},{7,4},{4,5},{5,6},{6,7},{11,8},{8,9},{9,10... | collective-permute-start | bytes 1572872 | tf_op jit(solution)/shard_map/ppermute | solution.py:277
  154.9 1.0 copy-start
  160.6 5.4 %collective-permute-start.19 = (bf16[512,256]{1,0:T(8,128)(2,1)S(1)}, bf16[512,256]{1,0:T(8,128)(2,1)S(1)}, u32[]{:S(2)}, u32[]{:S(2)}) collective-permute-start(bf16[512,256]{1,0:T(8,128)(2,1)S(1)} %shard_map.71.refs_0_), channel_id=1, source_target_pairs={{32,0},{64,32},{96,64},{0,96},{33,1},{65,33},{97,65},{1,97},{34,2}... | collective-permute-start | bytes 786440 | tf_op jit(solution)/shard_map/ppermute | solution.py:277
  160.7 11.5 %collective-permute-start.20 = (bf16[512,256]{1,0:T(8,128)(2,1)S(1)}, bf16[512,256]{1,0:T(8,128)(2,1)S(1)}, u32[]{:S(2)}, u32[]{:S(2)}) collective-permute-start(bf16[512,256]{1,0:T(8,128)(2,1)S(1)} %shard_map.71.refs_0_), channel_id=1, source_target_pairs={{64,0},{96,32},{0,64},{32,96},{65,1},{97,33},{1,65},{33,97},{66,2}... | collective-permute-start | bytes 786440 | tf_op jit(solution)/shard_map/ppermute | solution.py:277
  162.0 13.6 %collective-permute-start.21 = (bf16[512,256]{1,0:T(8,128)(2,1)S(1)}, bf16[512,256]{1,0:T(8,128)(2,1)S(1)}, u32[]{:S(2)}, u32[]{:S(2)}) collective-permute-start(bf16[512,256]{1,0:T(8,128)(2,1)S(1)} %shard_map.71.refs_0_), channel_id=1, source_target_pairs={{96,0},{0,32},{32,64},{64,96},{97,1},{1,33},{33,65},{65,97},{98,2}... | collective-permute-start | bytes 786440 | tf_op jit(solution)/shard_map/ppermute | solution.py:277
  162.7 14.2 %collective-permute-start.22 = (bf16[512,256]{1,0:T(8,128)(2,1)S(1)}, bf16[512,256]{1,0:T(8,128)(2,1)S(1)}, u32[]{:S(2)}, u32[]{:S(2)}) collective-permute-start(bf16[512,256]{1,0:T(8,128)(2,1)S(1)} %shard_map.71.refs_0_), channel_id=1, source_target_pairs={{0,16},{16,0},{1,17},{17,1},{2,18},{18,2},{3,19},{19,3},{4,20},{20... | collective-permute-start | bytes 786440 | tf_op jit(solution)/shard_map/ppermute | solution.py:281
  166.0 11.0 %collective-permute-start.23 = (bf16[512,256]{1,0:T(8,128)(2,1)S(1)}, bf16[512,256]{1,0:T(8,128)(2,1)}, u32[]{:S(2)}, u32[]{:S(2)}) collective-permute-start(bf16[512,256]{1,0:T(8,128)(2,1)S(1)} %collective-permute-done.19.refs_1_), channel_id=1, source_target_pairs={{0,16},{16,0},{1,17},{17,1},{2,18},{18,2},{3,19},{19,3},{4,20},{20... | collective-permute-start | bytes 786440 | tf_op jit(solution)/shard_map/ppermute | solution.py:281
  172.2 4.8 %collective-permute-start.24 = (bf16[512,256]{1,0:T(8,128)(2,1)S(1)}, bf16[512,256]{1,0:T(8,128)(2,1)}, u32[]{:S(2)}, u32[]{:S(2)}) collective-permute-start(bf16[512,256]{1,0:T(8,128)(2,1)S(1)} %collective-permute-done.20.refs_2_), channel_id=1, source_target_pairs={{0,16},{16,0},{1,17},{17,1},{2,18},{18,2},{3,19},{19,3},{4,20},{20... | collective-permute-start | bytes 786440 | tf_op jit(solution)/shard_map/ppermute | solution.py:281
  175.6 2.4 %collective-permute-start.25 = (bf16[512,256]{1,0:T(8,128)(2,1)S(1)}, bf16[512,256]{1,0:T(8,128)(2,1)}, u32[]{:S(2)}, u32[]{:S(2)}) collective-permute-start(bf16[512,256]{1,0:T(8,128)(2,1)S(1)} %collective-permute-done.21.refs_3_), channel_id=1, source_target_pairs={{0,16},{16,0},{1,17},{17,1},{2,18},{18,2},{3,19},{19,3},{4,20},{20... | collective-permute-start | bytes 786440 | tf_op jit(solution)/shard_map/ppermute | solution.py:281
where the time goes:
time: 183 us
  waiting for transfers between devices  82.3 us (45%)
  starting transfers between devices  50.1 us (27%)
  Pallas kernels  25 us (14%)
  blocking collectives  17.2 us (9%)
  local copies, waits for them, and re-layouts  4.68 us (3%)
  other arithmetic  1.94 us (1%)
    ppermute x18, waiting for transfers between devices, from_ring(): lax.ppermute(x, axis, [((i + k) % 4, i) for i in range(4)])  55.1 us
    all_to_all x1, waiting for transfers between devices, steps(): tiles = lax.all_to_all(packed, COL, 0, 0, tiled=True)  26.3 us
    ppermute x18, starting transfers between devices, from_ring(): lax.ppermute(x, axis, [((i + k) % 4, i) for i in range(4)])  25.4 us
    pallas_call x5, Pallas kernels, call(): pl.pallas_call(kernel, out_shape=outs, in_specs=[SMEM] * len(small) + [LO...  25 us
    all_gather x1, blocking collectives, steps(): panels = lax.all_gather(panel, ROW, axis=0, tiled=False)  17.2 us
    ppermute x8, starting transfers between devices, swapped(): return lax.ppermute(x, 'core', [(0, 1), (1, 0)])  15.7 us
    all_to_all x1, starting transfers between devices, steps(): tiles = lax.all_to_all(packed, COL, 0, 0, tiled=True)  5.27 us
    all_to_all x1, starting transfers between devices, steps(): arrived = lax.all_to_all(spread, COL, 0, 0, tiled=True)  3.73 us
  transfers between devices with their start and end apart: 28, of which 11 were waited for; matrix products, arithmetic and copies ran while one was open for 2% of the time, Pallas kernels for 3%

commit v1 on v0

--- a/solution.py
+++ b/solution.py
@@ -13,6 +13,7 @@
 COLS = 16
 SUBS = 128
 CW = 32
+PAUSE = 1300
 N = MAXT * TILE
 RT = NB // ROWS
 CT = NB // COLS
@@ -89,13 +90,18 @@
 
     lax.fori_loop(0, COLS, one, 0)
 
-    def tile(a, lanes):
-        return strip[pl.ds(pl.multiple_of(a * TILE, TILE), TILE), lanes]
-
     own = (ids[1] * ROWS + ids[0]) * MAXT
-    lanes = pl.ds(pl.multiple_of(lists[own] % CT * TILE, TILE), TILE)
-    for i in range(MAXT):
-        first[i] = tile(lists[own + i], lanes)
+    side = pl.ds(pl.multiple_of(lists[own] % CT * TILE, TILE), TILE)
+    heads = [
+        pltpu.make_async_copy(
+            strip.at[pl.ds(pl.multiple_of(lists[own + i] * TILE, TILE), TILE), side],
+            first.at[i],
+            sems.at[COLS + i // 4, i % 4],
+        )
+        for i in range(MAXT)
+    ]
+    for copy in heads:
+        copy.start()
 
     def done(c, _):
         for k in range(4):
@@ -103,6 +109,8 @@
         return 0
 
     lax.fori_loop(0, COLS, done, 0)
+    for copy in heads:
+        copy.wait()
 
 
 def solve_kernel(table, shift, tiles, first, panel, x, f, y):
@@ -191,6 +199,24 @@
     dens = (jnp.where(prow == pcol, 0.5, 0.0) - 0.5 * z).astype(BF16)
     for i in range(MAXT):
         panel[i] = dens[:, i * TILE : (i + 1) * TILE]
+
+
+def stack_kernel(*refs):
+    blocks, stacks, clock, sems = refs[:8], refs[8:10], refs[10], refs[11]
+    clock[...] = jnp.zeros_like(clock)
+
+    def tick(_, carry):
+        clock[...] = clock[...] + 1.0
+        return carry
+
+    lax.fori_loop(0, PAUSE, tick, 0)
+    copies = [
+        pltpu.make_async_copy(blocks[i], stacks[i // 4].at[i % 4], sems.at[i]) for i in range(8)
+    ]
+    for copy in copies:
+        copy.start()
+    for copy in copies:
+        copy.wait()
 
 
 def spread_kernel(table, panels, out, mine, sems):
@@ -286,15 +312,15 @@
 FAR = pl.BlockSpec(memory_space=pl.ANY)
 
 
-def call(kernel, outs, scratch, small, large, specs=LOCAL):
+def call(kernel, outs, scratch, small, large, specs=LOCAL, space=pltpu.VMEM):
     return pl.pallas_call(
         kernel,
         out_shape=outs,
-        in_specs=[SMEM] * len(small) + [LOCAL] * len(large),
+        in_specs=[SMEM] * len(small) + [LOCAL if space is pltpu.VMEM else FAR] * len(large),
         out_specs=specs,
         scratch_shapes=scratch,
         compiler_params=pltpu.CompilerParams(vmem_limit_bytes=24 << 20),
-    )(*small, *[pltpu.with_memory_space_constraint(x, pltpu.VMEM) for x in large])
+    )(*small, *[pltpu.with_memory_space_constraint(x, space) for x in large])
 
 
 def call_solve(table, shift, tiles, first):
@@ -315,19 +341,27 @@
     half = RT * TILE // 2
     top, bottom = hamiltonian[:half], hamiltonian[half:]
     strip = from_ring(hamiltonian, "z")
-    ahead = jnp.stack(from_ring(top, "c1"))
-    across = jnp.stack(from_ring(bottom, "c0"))
+    ahead = from_ring(top, "c1")
+    across = from_ring(bottom, "c0")
     strip = strip + [swapped(x) for x in strip]
     packed, first = call(
         pack_kernel,
-        (pltpu.HBM((COLS, 4, TILE, TILE), BF16), pltpu.VMEM((MAXT, TILE, TILE), BF16)),
-        [pltpu.VMEM((NB * TILE, WIDTH), BF16), pltpu.SemaphoreType.DMA((COLS, 4))],
+        (pltpu.HBM((COLS, 4, TILE, TILE), BF16), pltpu.HBM((MAXT, TILE, TILE), BF16)),
+        [pltpu.VMEM((NB * TILE, WIDTH), BF16), pltpu.SemaphoreType.DMA((COLS + 2, 4))],
         (table,),
         (top, bottom, *strip[1:]),
-        (FAR, LOCAL),
-    )
-    packed, ahead, across = lax.optimization_barrier((packed, ahead, across))
+        (FAR, FAR),
+    )
     tiles = lax.all_to_all(packed, COL, 0, 0, tiled=True)
+    ahead, across = call(
+        stack_kernel,
+        (pltpu.HBM((4, half, WIDTH), BF16), pltpu.HBM((4, half, WIDTH), BF16)),
+        [pltpu.VMEM((8, TILE), F32), pltpu.SemaphoreType.DMA((8,))],
+        (),
+        (*ahead, *across),
+        (FAR, FAR),
+        pltpu.HBM,
+    )
     ahead = from_ring(ahead, "c0")
     across = from_ring(across, "c1")
     panel = call_solve(table, shift, tiles, first)

time: 183 us -> 233 us (1.27)
  Pallas kernels: 25 us -> 67.2 us
  starting transfers between devices: 50.1 us -> 57.3 us
  waiting for transfers between devices: 82.3 us -> 84.8 us
  blocking collectives: 17.2 us -> 14.8 us
  local copies, waits for them, and re-layouts: 4.68 us -> 7.05 us
    pallas_call x5 -> x6, Pallas kernels: 25 us -> 67.2 us  [call(): pl.pallas_call(kernel, out_shape=outs, in_specs=[SMEM] * len(small) + [LO...]
    ppermute x8, starting transfers between devices: 15.7 us -> 21.1 us  [swapped(): return lax.ppermute(x, 'core', [(0, 1), (1, 0)])]
    ppermute x18, waiting for transfers between devices: 55.1 us -> 58 us  [from_ring(): lax.ppermute(x, axis, [((i + k) % 4, i) for i in range(4)])]
    all_gather x1, blocking collectives: 17.2 us -> 14.8 us  [steps(): panels = lax.all_gather(panel, ROW, axis=0, tiled=False)]
    unnamed x7 -> x27, local copies, waits for them, and re-layouts: 1.84 us -> 4.24 us
  transfers between devices with their start and end apart: 28 -> 28, of which waited for: 11 -> 9; matrix products, arithmetic and copies ran while one was open for 2% -> 2% of each run, Pallas kernels for 3% -> 25%
where the time goes in v1:
time: 233 us
  waiting for transfers between devices  84.8 us (36%)
  Pallas kernels  67.2 us (29%)
  starting transfers between devices  57.3 us (25%)
  blocking collectives  14.8 us (6%)
  local copies, waits for them, and re-layouts  7.05 us (3%)
    pallas_call x6, Pallas kernels, call(): pl.pallas_call(kernel, out_shape=outs, in_specs=[SMEM] * len(small) + [LO...  67.2 us
    ppermute x18, waiting for transfers between devices, from_ring(): lax.ppermute(x, axis, [((i + k) % 4, i) for i in range(4)])  58 us
    all_to_all x1, waiting for transfers between devices, steps(): tiles = lax.all_to_all(packed, COL, 0, 0, tiled=True)  25.8 us
    ppermute x18, starting transfers between devices, from_ring(): lax.ppermute(x, axis, [((i + k) % 4, i) for i in range(4)])  23.6 us
    ppermute x8, starting transfers between devices, swapped(): return lax.ppermute(x, 'core', [(0, 1), (1, 0)])  21.1 us
    all_gather x1, blocking collectives, steps(): panels = lax.all_gather(panel, ROW, axis=0, tiled=False)  14.8 us
    all_to_all x1, starting transfers between devices, steps(): tiles = lax.all_to_all(packed, COL, 0, 0, tiled=True)  6.9 us
    all_to_all x1, starting transfers between devices, steps(): arrived = lax.all_to_all(spread, COL, 0, 0, tiled=True)  5.71 us
  transfers between devices with their start and end apart: 28, of which 9 were waited for; matrix products, arithmetic and copies ran while one was open for 2% of the time, Pallas kernels for 25%

profile of v1, /device:TPU:1, one launch (start us, length us, event | category | flops | bytes accessed | tf_op | source)
XLA Modules:
  0.0 232.7 jit_solution(12681753785169513373)
XLA Ops:
  0.6 4.6 %collective-permute-start = (bf16[512,256]{1,0:T(8,128)(2,1)}, bf16[512,256]{1,0:T(8,128)(2,1)S(1)}, u32[]{:S(2)}, u32[]{:S(2)}) collective-permute-start(bf16[512,256]{1,0:T(8,128)(2,1)} %param.5), channel_id=1, source_target_pairs={{32,0},{64,32},{96,64},{0,96},{33,1},{65,33},{97,65},{1,97},{34,2}... | collective-permute-start | bytes 786440 | tf_op jit(solution)/shard_map/ppermute | solution.py:303
  5.3 0.0 collective-permute-start.1
  5.3 0.7 collective-permute-start.2
  6.0 1.5 collective-permute-start.3
  7.5 8.6 %collective-permute-done.refs_2_ = bf16[512,256]{1,0:T(8,128)(2,1)S(1)} collective-permute-done((bf16[512,256]{1,0:T(8,128)(2,1)}, bf16[512,256]{1,0:T(8,128)(2,1)S(1)}, u32[]{:S(2)}, u32[]{:S(2)}) %collective-permute-start) | collective-permute-done | bytes 262176 | tf_op jit(solution)/shard_map/ppermute | solution.py:303
  16.1 1.7 collective-permute-start.4
  17.7 0.0 collective-permute-start.5
  17.7 2.5 %collective-permute-done.2.refs_4_ = bf16[512,256]{1,0:T(8,128)(2,1)S(1)} collective-permute-done((bf16[512,256]{1,0:T(8,128)(2,1)}, bf16[512,256]{1,0:T(8,128)(2,1)S(1)}, u32[]{:S(2)}, u32[]{:S(2)}) %collective-permute-start.2) | collective-permute-done | bytes 262176 | tf_op jit(solution)/shard_map/ppermute | solution.py:303
  20.3 0.8 collective-permute-start.6
  21.0 0.8 copy.12
  21.8 0.1 reshape.36
  21.9 0.8 reshape.37
  22.7 0.7 concatenate.3.table
  23.4 1.0 fusion
  24.5 0.0 collective-permute-done.4.refs_6_
  24.5 0.0 collective-permute-done.5.refs_7_
  24.5 3.4 %shard_map.68 = (bf16[16,4,128,128]{3,2,1,0:T(8,128)(2,1)}, bf16[8,128,128]{2,1,0:T(8,128)(2,1)}) custom-call(s32[2178]{0:T(1024)S(1)} %concatenate.3.table, bf16[256,256]{1,0:T(8,128)(2,1)S(1)} %get-tuple-element.11.refs_0_, bf16[256,256]{1,0:T(8,128)(2,1)S(1)} %get-tuple-element.10.refs_1_.refs_4_, bf16[512,256]{1,0:T(8,128)(2,1)S(1)} %collective-permute-done.refs_2_, ...), custom_call_target="tpu_custom_call" | custom-call | tf_op jit(solution)/shard_map/pallas_call | solution.py:316
  27.9 0.0 copy-start.4
  27.9 6.9 %all-to-all-start = ((bf16[16,4,128,128]{3,2,1,0:T(8,128)(2,1)}), bf16[16,4,128,128]{3,2,1,0:T(8,128)(2,1)S(1)}, u32[]{:S(2)}, u32[]{:S(2)}) async-start(bf16[16,4,128,128]{3,2,1,0:T(8,128)(2,1)} %get-tuple-element.6), calls=%async_computation | async-start | bytes 4194304 | tf_op jit(solution)/shard_map/all_to_all | solution.py:355
  34.8 2.6 %collective-permute-start.10 = (bf16[256,256]{1,0:T(8,128)(2,1)S(1)}, bf16[256,256]{1,0:T(8,128)(2,1)S(1)}, u32[]{:S(2)}, u32[]{:S(2)}) collective-permute-start(bf16[256,256]{1,0:T(8,128)(2,1)S(1)} %get-tuple-element.10.refs_1_.refs_4_), channel_id=1, source_target_pairs={{4,0},{8,4},{12,8},{0,12},{5,1},{9,5},{13,9},{1,13},{6,2},{10,6},{... | collective-permute-start | bytes 393224 | tf_op jit(solution)/shard_map/ppermute | solution.py:303
  38.0 25.8 %all-to-all-done.tiles = bf16[16,4,128,128]{3,2,1,0:T(8,128)(2,1)S(1)} async-done(((bf16[16,4,128,128]{3,2,1,0:T(8,128)(2,1)}), bf16[16,4,128,128]{3,2,1,0:T(8,128)(2,1)S(1)}, u32[]{:S(2)}, u32[]{:S(2)}) %all-to-all-start) | async-done | bytes 2097184 | tf_op jit(solution)/shard_map/all_to_all | solution.py:355
  63.9 8.8 %shard_map.69 = bf16[8,32,128]{2,1,0:T(8,128)(2,1)S(1)} custom-call(s32[2178]{0:T(1024)S(1)} %concatenate.3.table, f32[1]{0:T(128)S(6)} %copy.14.shift, bf16[16,4,128,128]{3,2,1,0:T(8,128)(2,1)S(1)} %all-to-all-done.tiles, bf16[8,128,128]{2,1,0:T(8,128)(2,1)S(1)} %copy-done.4), custom_call_target="tpu_custom_call" | custom-call | tf_op jit(solution)/shard_map/pallas_call | solution.py:316
  72.7 14.8 %all-gather = bf16[64,32,128]{2,1,0:T(8,128)(2,1)S(1)} all-gather(bf16[8,32,128]{2,1,0:T(8,128)(2,1)S(1)} %shard_map.69), channel_id=2, replica_groups=mesh['z'=4,'core'=2,'c0'=4,'c1'=4] {'z','core'}, dimensions={0}, use_global_device_ids=true | all-gather | bytes 589824 | tf_op jit(solution)/shard_map/all_gather | solution.py:368
  87.5 3.7 %shard_map.70 = bf16[16,8,2,32,128]{4,3,2,1,0:T(8,128)(2,1)} custom-call(s32[2178]{0:T(1024)S(1)} %concatenate.3.table, bf16[8,8,32,128]{3,2,1,0:T(8,128)(2,1)S(1)} %bitcast.3), custom_call_target="tpu_custom_call" | custom-call | tf_op jit(solution)/shard_map/pallas_call | solution.py:316
  91.2 5.7 %all-to-all-start.1 = ((bf16[16,8,2,32,128]{4,3,2,1,0:T(8,128)(2,1)}), bf16[16,8,2,32,128]{4,3,2,1,0:T(8,128)(2,1)S(1)}, u32[]{:S(2)}, u32[]{:S(2)}) async-start(bf16[16,8,2,32,128]{4,3,2,1,0:T(8,128)(2,1)} %shard_map.70), calls=%async_computation.1 | async-start | bytes 4194304 | tf_op jit(solution)/shard_map/all_to_all | solution.py:377
  96.9 2.9 %collective-permute-start.11 = (bf16[256,256]{1,0:T(8,128)(2,1)S(1)}, bf16[256,256]{1,0:T(8,128)(2,1)S(1)}, u32[]{:S(2)}, u32[]{:S(2)}) collective-permute-start(bf16[256,256]{1,0:T(8,128)(2,1)S(1)} %get-tuple-element.10.refs_1_.refs_4_), channel_id=1, source_target_pairs={{8,0},{12,4},{0,8},{4,12},{9,1},{13,5},{1,9},{5,13},{10,2},{14,6},... | collective-permute-start | bytes 393224 | tf_op jit(solution)/shard_map/ppermute | solution.py:303
  99.8 0.3 collective-permute-start.12
  100.1 2.4 %collective-permute-start.7 = (bf16[256,256]{1,0:T(8,128)(2,1)S(1)}, bf16[256,256]{1,0:T(8,128)(2,1)S(1)}, u32[]{:S(2)}, u32[]{:S(2)}) collective-permute-start(bf16[256,256]{1,0:T(8,128)(2,1)S(1)} %get-tuple-element.11.refs_0_), channel_id=1, source_target_pairs={{1,0},{2,1},{3,2},{0,3},{5,4},{6,5},{7,6},{4,7},{9,8},{10,9},{11,1... | collective-permute-start | bytes 393224 | tf_op jit(solution)/shard_map/ppermute | solution.py:303
  102.5 0.6 collective-permute-start.8
  103.1 0.6 collective-permute-start.9
  103.7 23.8 %collective-permute-done.11.refs_6_ = bf16[256,256]{1,0:T(8,128)(2,1)S(1)} collective-permute-done((bf16[256,256]{1,0:T(8,128)(2,1)S(1)}, bf16[256,256]{1,0:T(8,128)(2,1)S(1)}, u32[]{:S(2)}, u32[]{:S(2)}) %collective-permute-start.11) | collective-permute-done | bytes 131104 | tf_op jit(solution)/shard_map/ppermute | solution.py:303
  127.5 1.6 collective-permute-done.12.refs_7_
  129.1 0.0 collective-permute-done.7.refs_1_
  129.1 0.0 collective-permute-done.8.refs_2_
  129.1 0.6 copy-done.7
  129.7 0.0 copy-done.8
  129.8 0.0 copy-done.9
  129.8 0.7 copy-done.10
  130.5 41.8 %shard_map.71 = (bf16[4,256,256]{2,1,0:T(8,128)(2,1)}, bf16[4,256,256]{2,1,0:T(8,128)(2,1)}) custom-call(bf16[256,256]{1,0:T(8,128)(2,1)} %copy-done.1, bf16[256,256]{1,0:T(8,128)(2,1)} %copy-done.8, bf16[256,256]{1,0:T(8,128)(2,1)} %copy-done.9, bf16[256,256]{1,0:T(8,128)(2,1)} %copy-done.10, bf16[256,256]{1,0:T(8,128)(2,1)} %copy-done, ...), custom_call_target="tpu_custom_call" | custom-call | tf_op jit(solution)/shard_map/pallas_call | solution.py:316
  172.3 1.6 collective-permute-start.13
  173.9 1.0 collective-permute-start.14
  174.8 0.0 collective-permute-start.15
  174.9 2.3 collective-permute-start.16
  177.2 0.7 collective-permute-start.17
  177.8 6.8 %collective-permute-done.13.a1 = bf16[4,256,256]{2,1,0:T(8,128)(2,1)S(1)} collective-permute-done((bf16[4,256,256]{2,1,0:T(8,128)(2,1)}, bf16[4,256,256]{2,1,0:T(8,128)(2,1)S(1)}, u32[]{:S(2)}, u32[]{:S(2)}) %collective-permute-start.13) | collective-permute-done | bytes 524320 | tf_op jit(solution)/shard_map/ppermute | solution.py:303
  184.7 1.3 collective-permute-start.18
  186.0 1.6 collective-permute-done.14.a2
  187.5 13.1 %collective-permute-done.15.a3 = bf16[4,256,256]{2,1,0:T(8,128)(2,1)S(1)} collective-permute-done((bf16[4,256,256]{2,1,0:T(8,128)(2,1)}, bf16[4,256,256]{2,1,0:T(8,128)(2,1)S(1)}, u32[]{:S(2)}, u32[]{:S(2)}) %collective-permute-start.15) | collective-permute-done | bytes 524320 | tf_op jit(solution)/shard_map/ppermute | solution.py:303
  200.7 0.0 copy-start.2
  200.7 1.0 copy-done.2
  201.7 1.0 copy-done.3
  202.8 4.7 %shard_map.72.refs_0_ = bf16[512,256]{1,0:T(8,128)(2,1)S(1)} custom-call(s32[2178]{0:T(1024)S(1)} %concatenate.3.table, bf16[4,256,256]{2,1,0:T(8,128)(2,1)S(1)} %copy-done.2, bf16[4,256,256]{2,1,0:T(8,128)(2,1)S(1)} %collective-permute-done.13.a1, bf16[4,256,256]{2,1,0:T(8,128)(2,1)S(1)} %collective-permute-done.14.a2, ...), custom_call_target="tpu_custom_call" | custom-call | tf_op jit(solution)/shard_map/pallas_call | solution.py:316
  207.5 0.7 collective-permute-start.19
  208.1 0.6 collective-permute-start.20
  208.8 0.8 collective-permute-start.21
  209.5 8.4 %collective-permute-start.22 = (bf16[512,256]{1,0:T(8,128)(2,1)S(1)}, bf16[512,256]{1,0:T(8,128)(2,1)S(1)}, u32[]{:S(2)}, u32[]{:S(2)}) collective-permute-start(bf16[512,256]{1,0:T(8,128)(2,1)S(1)} %shard_map.72.refs_0_), channel_id=1, source_target_pairs={{0,16},{16,0},{1,17},{17,1},{2,18},{18,2},{3,19},{19,3},{4,20},{20... | collective-permute-start | bytes 786440 | tf_op jit(solution)/shard_map/ppermute | solution.py:307
  217.9 3.5 %collective-permute-start.23 = (bf16[512,256]{1,0:T(8,128)(2,1)S(1)}, bf16[512,256]{1,0:T(8,128)(2,1)}, u32[]{:S(2)}, u32[]{:S(2)}) collective-permute-start(bf16[512,256]{1,0:T(8,128)(2,1)S(1)} %collective-permute-done.19.refs_1_), channel_id=1, source_target_pairs={{0,16},{16,0},{1,17},{17,1},{2,18},{18,2},{3,19},{19,3},{4,20},{20... | collective-permute-start | bytes 786440 | tf_op jit(solution)/shard_map/ppermute | solution.py:307
  221.4 2.5 %collective-permute-start.24 = (bf16[512,256]{1,0:T(8,128)(2,1)S(1)}, bf16[512,256]{1,0:T(8,128)(2,1)}, u32[]{:S(2)}, u32[]{:S(2)}) collective-permute-start(bf16[512,256]{1,0:T(8,128)(2,1)S(1)} %collective-permute-done.20.refs_2_), channel_id=1, source_target_pairs={{0,16},{16,0},{1,17},{17,1},{2,18},{18,2},{3,19},{19,3},{4,20},{20... | collective-permute-start | bytes 786440 | tf_op jit(solution)/shard_map/ppermute | solution.py:307
  223.9 2.7 %collective-permute-start.25 = (bf16[512,256]{1,0:T(8,128)(2,1)S(1)}, bf16[512,256]{1,0:T(8,128)(2,1)}, u32[]{:S(2)}, u32[]{:S(2)}) collective-permute-start(bf16[512,256]{1,0:T(8,128)(2,1)S(1)} %collective-permute-done.21.refs_3_), channel_id=1, source_target_pairs={{0,16},{16,0},{1,17},{17,1},{2,18},{18,2},{3,19},{19,3},{4,20},{20... | collective-permute-start | bytes 786440 | tf_op jit(solution)/shard_map/ppermute | solution.py:307
  226.6 0.1 and_reduce_fusion
  226.7 0.1 copy.13
  226.9 0.1 reshape.38.present
  227.0 0.9 collective-permute-done.25.refs_7_
  227.9 4.8 %shard_map.73 = (bf16[512,256]{1,0:T(8,128)(2,1)}, f32[512,256]{1,0:T(8,128)}) custom-call(s32[2178]{0:T(1024)S(1)} %concatenate.3.table, s32[512]{0:T(512)S(1)} %reshape.38.present, bf16[16,8,2,32,128]{4,3,2,1,0:T(8,128)(2,1)S(1)} %all-to-all-done.1.pieces, bf16[512,256]{1,0:T(8,128)(2,1)S(1)} %shard_map.72.refs_0_, ...), custom_call_target="tpu_custom_call" | custom-call | tf_op jit(solution)/shard_map/pallas_call | solution.py:316
  (36 shorter events, 0.1 us)
Async XLA Ops:
  0.6 15.4 %collective-permute-start = (bf16[512,256]{1,0:T(8,128)(2,1)}, bf16[512,256]{1,0:T(8,128)(2,1)S(1)}, u32[]{:S(2)}, u32[]{:S(2)}) collective-permute-start(bf16[512,256]{1,0:T(8,128)(2,1)} %param.5), channel_id=1, source_target_pairs={{32,0},{64,32},{96,64},{0,96},{33,1},{65,33},{97,65},{1,97},{34,2}... | collective-permute-start | bytes 786440 | tf_op jit(solution)/shard_map/ppermute | solution.py:303
  5.3 12.5 %collective-permute-start.1 = (bf16[512,256]{1,0:T(8,128)(2,1)}, bf16[512,256]{1,0:T(8,128)(2,1)S(1)}, u32[]{:S(2)}, u32[]{:S(2)}) collective-permute-start(bf16[512,256]{1,0:T(8,128)(2,1)} %param.5), channel_id=1, source_target_pairs={{64,0},{96,32},{0,64},{32,96},{65,1},{97,33},{1,65},{33,97},{66,2}... | collective-permute-start | bytes 786440 | tf_op jit(solution)/shard_map/ppermute | solution.py:303
  5.3 15.0 %collective-permute-start.2 = (bf16[512,256]{1,0:T(8,128)(2,1)}, bf16[512,256]{1,0:T(8,128)(2,1)S(1)}, u32[]{:S(2)}, u32[]{:S(2)}) collective-permute-start(bf16[512,256]{1,0:T(8,128)(2,1)} %param.5), channel_id=1, source_target_pairs={{96,0},{0,32},{32,64},{64,96},{97,1},{1,33},{33,65},{65,97},{98,2}... | collective-permute-start | bytes 786440 | tf_op jit(solution)/shard_map/ppermute | solution.py:303
  6.0 18.5 %collective-permute-start.3 = (bf16[512,256]{1,0:T(8,128)(2,1)}, bf16[512,256]{1,0:T(8,128)(2,1)S(1)}, u32[]{:S(2)}, u32[]{:S(2)}) collective-permute-start(bf16[512,256]{1,0:T(8,128)(2,1)} %param.5), channel_id=1, source_target_pairs={{0,16},{16,0},{1,17},{17,1},{2,18},{18,2},{3,19},{19,3},{4,20},{20... | collective-permute-start | bytes 786440 | tf_op jit(solution)/shard_map/ppermute | solution.py:307
  16.1 8.4 %collective-permute-start.4 = (bf16[512,256]{1,0:T(8,128)(2,1)S(1)}, bf16[512,256]{1,0:T(8,128)(2,1)S(1)}, u32[]{:S(2)}, u32[]{:S(2)}) collective-permute-start(bf16[512,256]{1,0:T(8,128)(2,1)S(1)} %collective-permute-done.refs_2_), channel_id=1, source_target_pairs={{0,16},{16,0},{1,17},{17,1},{2,18},{18,2},{3,19},{19,3},{4,20},{20... | collective-permute-start | bytes 786440 | tf_op jit(solution)/shard_map/ppermute | solution.py:307
  17.7 6.7 %collective-permute-start.5 = (bf16[512,256]{1,0:T(8,128)(2,1)S(1)}, bf16[512,256]{1,0:T(8,128)(2,1)S(1)}, u32[]{:S(2)}, u32[]{:S(2)}) collective-permute-start(bf16[512,256]{1,0:T(8,128)(2,1)S(1)} %collective-permute-done.1.refs_3_), channel_id=1, source_target_pairs={{0,16},{16,0},{1,17},{17,1},{2,18},{18,2},{3,19},{19,3},{4,20},{20... | collective-permute-start | bytes 786440 | tf_op jit(solution)/shard_map/ppermute | solution.py:307
  20.3 4.2 %collective-permute-start.6 = (bf16[512,256]{1,0:T(8,128)(2,1)S(1)}, bf16[512,256]{1,0:T(8,128)(2,1)S(1)}, u32[]{:S(2)}, u32[]{:S(2)}) collective-permute-start(bf16[512,256]{1,0:T(8,128)(2,1)S(1)} %collective-permute-done.2.refs_4_), channel_id=1, source_target_pairs={{0,16},{16,0},{1,17},{17,1},{2,18},{18,2},{3,19},{19,3},{4,20},{20... | collective-permute-start | bytes 786440 | tf_op jit(solution)/shard_map/ppermute | solution.py:307
  24.4 75.4 %copy-start = (bf16[256,256]{1,0:T(8,128)(2,1)}, bf16[256,256]{1,0:T(8,128)(2,1)S(1)}, u32[]{:S(2)}) copy-start(bf16[256,256]{1,0:T(8,128)(2,1)S(1)} %get-tuple-element.10.refs_1_.refs_4_) | copy-start | bytes 393220
  24.4 78.6 %copy-start.1 = (bf16[256,256]{1,0:T(8,128)(2,1)}, bf16[256,256]{1,0:T(8,128)(2,1)S(1)}, u32[]{:S(2)}) copy-start(bf16[256,256]{1,0:T(8,128)(2,1)S(1)} %get-tuple-element.11.refs_0_) | copy-start | bytes 393220
  27.9 36.0 %copy-start.4 = (bf16[8,128,128]{2,1,0:T(8,128)(2,1)S(1)}, bf16[8,128,128]{2,1,0:T(8,128)(2,1)}, u32[]{:S(2)}) copy-start(bf16[8,128,128]{2,1,0:T(8,128)(2,1)} %get-tuple-element.7.first) | copy-start | bytes 786436
  27.9 36.0 %all-to-all-start = ((bf16[16,4,128,128]{3,2,1,0:T(8,128)(2,1)}), bf16[16,4,128,128]{3,2,1,0:T(8,128)(2,1)S(1)}, u32[]{:S(2)}, u32[]{:S(2)}) async-start(bf16[16,4,128,128]{3,2,1,0:T(8,128)(2,1)} %get-tuple-element.6), calls=%async_computation | async-start | bytes 4194304 | tf_op jit(solution)/shard_map/all_to_all | solution.py:355
  34.8 68.3 %collective-permute-start.10 = (bf16[256,256]{1,0:T(8,128)(2,1)S(1)}, bf16[256,256]{1,0:T(8,128)(2,1)S(1)}, u32[]{:S(2)}, u32[]{:S(2)}) collective-permute-start(bf16[256,256]{1,0:T(8,128)(2,1)S(1)} %get-tuple-element.10.refs_1_.refs_4_), channel_id=1, source_target_pairs={{4,0},{8,4},{12,8},{0,12},{5,1},{9,5},{13,9},{1,13},{6,2},{10,6},{... | collective-permute-start | bytes 393224 | tf_op jit(solution)/shard_map/ppermute | solution.py:303
  91.2 136.7 %all-to-all-start.1 = ((bf16[16,8,2,32,128]{4,3,2,1,0:T(8,128)(2,1)}), bf16[16,8,2,32,128]{4,3,2,1,0:T(8,128)(2,1)S(1)}, u32[]{:S(2)}, u32[]{:S(2)}) async-start(bf16[16,8,2,32,128]{4,3,2,1,0:T(8,128)(2,1)} %shard_map.70), calls=%async_computation.1 | async-start | bytes 4194304 | tf_op jit(solution)/shard_map/all_to_all | solution.py:377
  96.9 30.5 %collective-permute-start.11 = (bf16[256,256]{1,0:T(8,128)(2,1)S(1)}, bf16[256,256]{1,0:T(8,128)(2,1)S(1)}, u32[]{:S(2)}, u32[]{:S(2)}) collective-permute-start(bf16[256,256]{1,0:T(8,128)(2,1)S(1)} %get-tuple-element.10.refs_1_.refs_4_), channel_id=1, source_target_pairs={{8,0},{12,4},{0,8},{4,12},{9,1},{13,5},{1,9},{5,13},{10,2},{14,6},... | collective-permute-start | bytes 393224 | tf_op jit(solution)/shard_map/ppermute | solution.py:303
  99.8 29.3 %collective-permute-start.12 = (bf16[256,256]{1,0:T(8,128)(2,1)S(1)}, bf16[256,256]{1,0:T(8,128)(2,1)S(1)}, u32[]{:S(2)}, u32[]{:S(2)}) collective-permute-start(bf16[256,256]{1,0:T(8,128)(2,1)S(1)} %get-tuple-element.10.refs_1_.refs_4_), channel_id=1, source_target_pairs={{12,0},{0,4},{4,8},{8,12},{13,1},{1,5},{5,9},{9,13},{14,2},{2,6},{... | collective-permute-start | bytes 393224 | tf_op jit(solution)/shard_map/ppermute | solution.py:303
  100.1 29.0 %collective-permute-start.7 = (bf16[256,256]{1,0:T(8,128)(2,1)S(1)}, bf16[256,256]{1,0:T(8,128)(2,1)S(1)}, u32[]{:S(2)}, u32[]{:S(2)}) collective-permute-start(bf16[256,256]{1,0:T(8,128)(2,1)S(1)} %get-tuple-element.11.refs_0_), channel_id=1, source_target_pairs={{1,0},{2,1},{3,2},{0,3},{5,4},{6,5},{7,6},{4,7},{9,8},{10,9},{11,1... | collective-permute-start | bytes 393224 | tf_op jit(solution)/shard_map/ppermute | solution.py:303
  102.5 26.6 %collective-permute-start.8 = (bf16[256,256]{1,0:T(8,128)(2,1)S(1)}, bf16[256,256]{1,0:T(8,128)(2,1)S(1)}, u32[]{:S(2)}, u32[]{:S(2)}) collective-permute-start(bf16[256,256]{1,0:T(8,128)(2,1)S(1)} %get-tuple-element.11.refs_0_), channel_id=1, source_target_pairs={{2,0},{3,1},{0,2},{1,3},{6,4},{7,5},{4,6},{5,7},{10,8},{11,9},{8,1... | collective-permute-start | bytes 393224 | tf_op jit(solution)/shard_map/ppermute | solution.py:303
  103.1 26.0 %copy-start.5 = (bf16[256,256]{1,0:T(8,128)(2,1)}, bf16[256,256]{1,0:T(8,128)(2,1)S(1)}, u32[]{:S(2)}) copy-start(bf16[256,256]{1,0:T(8,128)(2,1)S(1)} %collective-permute-done.10.refs_5_) | copy-start | bytes 393220
  103.1 26.0 %collective-permute-start.9 = (bf16[256,256]{1,0:T(8,128)(2,1)S(1)}, bf16[256,256]{1,0:T(8,128)(2,1)S(1)}, u32[]{:S(2)}, u32[]{:S(2)}) collective-permute-start(bf16[256,256]{1,0:T(8,128)(2,1)S(1)} %get-tuple-element.11.refs_0_), channel_id=1, source_target_pairs={{3,0},{0,1},{1,2},{2,3},{7,4},{4,5},{5,6},{6,7},{11,8},{8,9},{9,10... | collective-permute-start | bytes 393224 | tf_op jit(solution)/shard_map/ppermute | solution.py:303
  127.5 1.6 copy-start.6
  129.1 0.7 copy-start.7
  129.1 0.7 copy-start.8
  129.1 0.7 copy-start.9
  129.8 0.7 copy-start.10
  130.5 96.2 %copy-start.11 = (s32[128,8]{0,1:T(8,128)S(1)}, s32[128,8]{0,1:T(8,128)}, u32[]{:S(2)}) copy-start(s32[128,8]{0,1:T(8,128)} %param.7) | copy-start | bytes 12292
  172.3 12.4 %collective-permute-start.13 = (bf16[4,256,256]{2,1,0:T(8,128)(2,1)}, bf16[4,256,256]{2,1,0:T(8,128)(2,1)S(1)}, u32[]{:S(2)}, u32[]{:S(2)}) collective-permute-start(bf16[4,256,256]{2,1,0:T(8,128)(2,1)} %get-tuple-element.8.a0), channel_id=1, source_target_pairs={{4,0},{8,4},{12,8},{0,12},{5,1},{9,5},{13,9},{1,13},{6,2},{10,6},{... | collective-permute-start | bytes 1572872 | tf_op jit(solution)/shard_map/ppermute | solution.py:303
  173.9 13.7 %collective-permute-start.14 = (bf16[4,256,256]{2,1,0:T(8,128)(2,1)}, bf16[4,256,256]{2,1,0:T(8,128)(2,1)S(1)}, u32[]{:S(2)}, u32[]{:S(2)}) collective-permute-start(bf16[4,256,256]{2,1,0:T(8,128)(2,1)} %get-tuple-element.8.a0), channel_id=1, source_target_pairs={{8,0},{12,4},{0,8},{4,12},{9,1},{13,5},{1,9},{5,13},{10,2},{14,6},... | collective-permute-start | bytes 1572872 | tf_op jit(solution)/shard_map/ppermute | solution.py:303
  174.8 25.8 %collective-permute-start.15 = (bf16[4,256,256]{2,1,0:T(8,128)(2,1)}, bf16[4,256,256]{2,1,0:T(8,128)(2,1)S(1)}, u32[]{:S(2)}, u32[]{:S(2)}) collective-permute-start(bf16[4,256,256]{2,1,0:T(8,128)(2,1)} %get-tuple-element.8.a0), channel_id=1, source_target_pairs={{12,0},{0,4},{4,8},{8,12},{13,1},{1,5},{5,9},{9,13},{14,2},{2,6},{... | collective-permute-start | bytes 1572872 | tf_op jit(solution)/shard_map/ppermute | solution.py:303
  174.9 51.7 %copy-start.12 = (s32[128]{0:T(128)S(1)}, s32[128]{0:T(128)}, u32[]{:S(2)}) copy-start(s32[128]{0:T(128)} %param.8) | copy-start | bytes 1540
  174.9 25.8 %collective-permute-start.16 = (bf16[4,256,256]{2,1,0:T(8,128)(2,1)}, bf16[4,256,256]{2,1,0:T(8,128)(2,1)S(1)}, u32[]{:S(2)}, u32[]{:S(2)}) collective-permute-start(bf16[4,256,256]{2,1,0:T(8,128)(2,1)} %get-tuple-element.9.b0), channel_id=1, source_target_pairs={{1,0},{2,1},{3,2},{0,3},{5,4},{6,5},{7,6},{4,7},{9,8},{10,9},{11,1... | collective-permute-start | bytes 1572872 | tf_op jit(solution)/shard_map/ppermute | solution.py:303
  177.2 23.5 %collective-permute-start.17 = (bf16[4,256,256]{2,1,0:T(8,128)(2,1)}, bf16[4,256,256]{2,1,0:T(8,128)(2,1)S(1)}, u32[]{:S(2)}, u32[]{:S(2)}) collective-permute-start(bf16[4,256,256]{2,1,0:T(8,128)(2,1)} %get-tuple-element.9.b0), channel_id=1, source_target_pairs={{2,0},{3,1},{0,2},{1,3},{6,4},{7,5},{4,6},{5,7},{10,8},{11,9},{8,1... | collective-permute-start | bytes 1572872 | tf_op jit(solution)/shard_map/ppermute | solution.py:303
  184.7 16.0 %collective-permute-start.18 = (bf16[4,256,256]{2,1,0:T(8,128)(2,1)}, bf16[4,256,256]{2,1,0:T(8,128)(2,1)S(1)}, u32[]{:S(2)}, u32[]{:S(2)}) collective-permute-start(bf16[4,256,256]{2,1,0:T(8,128)(2,1)} %get-tuple-element.9.b0), channel_id=1, source_target_pairs={{3,0},{0,1},{1,2},{2,3},{7,4},{4,5},{5,6},{6,7},{11,8},{8,9},{9,10... | collective-permute-start | bytes 1572872 | tf_op jit(solution)/shard_map/ppermute | solution.py:303
  200.7 1.0 copy-start.2
  201.7 1.0 copy-start.3
  207.5 10.4 %collective-permute-start.19 = (bf16[512,256]{1,0:T(8,128)(2,1)S(1)}, bf16[512,256]{1,0:T(8,128)(2,1)S(1)}, u32[]{:S(2)}, u32[]{:S(2)}) collective-permute-start(bf16[512,256]{1,0:T(8,128)(2,1)S(1)} %shard_map.72.refs_0_), channel_id=1, source_target_pairs={{32,0},{64,32},{96,64},{0,96},{33,1},{65,33},{97,65},{1,97},{34,2}... | collective-permute-start | bytes 786440 | tf_op jit(solution)/shard_map/ppermute | solution.py:303
  208.1 13.3 %collective-permute-start.20 = (bf16[512,256]{1,0:T(8,128)(2,1)S(1)}, bf16[512,256]{1,0:T(8,128)(2,1)S(1)}, u32[]{:S(2)}, u32[]{:S(2)}) collective-permute-start(bf16[512,256]{1,0:T(8,128)(2,1)S(1)} %shard_map.72.refs_0_), channel_id=1, source_target_pairs={{64,0},{96,32},{0,64},{32,96},{65,1},{97,33},{1,65},{33,97},{66,2}... | collective-permute-start | bytes 786440 | tf_op jit(solution)/shard_map/ppermute | solution.py:303
  208.8 15.1 %collective-permute-start.21 = (bf16[512,256]{1,0:T(8,128)(2,1)S(1)}, bf16[512,256]{1,0:T(8,128)(2,1)S(1)}, u32[]{:S(2)}, u32[]{:S(2)}) collective-permute-start(bf16[512,256]{1,0:T(8,128)(2,1)S(1)} %shard_map.72.refs_0_), channel_id=1, source_target_pairs={{96,0},{0,32},{32,64},{64,96},{97,1},{1,33},{33,65},{65,97},{98,2}... | collective-permute-start | bytes 786440 | tf_op jit(solution)/shard_map/ppermute | solution.py:303
  209.5 17.4 %collective-permute-start.22 = (bf16[512,256]{1,0:T(8,128)(2,1)S(1)}, bf16[512,256]{1,0:T(8,128)(2,1)S(1)}, u32[]{:S(2)}, u32[]{:S(2)}) collective-permute-start(bf16[512,256]{1,0:T(8,128)(2,1)S(1)} %shard_map.72.refs_0_), channel_id=1, source_target_pairs={{0,16},{16,0},{1,17},{17,1},{2,18},{18,2},{3,19},{19,3},{4,20},{20... | collective-permute-start | bytes 786440 | tf_op jit(solution)/shard_map/ppermute | solution.py:307
  217.9 9.1 %collective-permute-start.23 = (bf16[512,256]{1,0:T(8,128)(2,1)S(1)}, bf16[512,256]{1,0:T(8,128)(2,1)}, u32[]{:S(2)}, u32[]{:S(2)}) collective-permute-start(bf16[512,256]{1,0:T(8,128)(2,1)S(1)} %collective-permute-done.19.refs_1_), channel_id=1, source_target_pairs={{0,16},{16,0},{1,17},{17,1},{2,18},{18,2},{3,19},{19,3},{4,20},{20... | collective-permute-start | bytes 786440 | tf_op jit(solution)/shard_map/ppermute | solution.py:307
  221.4 5.6 %collective-permute-start.24 = (bf16[512,256]{1,0:T(8,128)(2,1)S(1)}, bf16[512,256]{1,0:T(8,128)(2,1)}, u32[]{:S(2)}, u32[]{:S(2)}) collective-permute-start(bf16[512,256]{1,0:T(8,128)(2,1)S(1)} %collective-permute-done.20.refs_2_), channel_id=1, source_target_pairs={{0,16},{16,0},{1,17},{17,1},{2,18},{18,2},{3,19},{19,3},{4,20},{20... | collective-permute-start | bytes 786440 | tf_op jit(solution)/shard_map/ppermute | solution.py:307
  223.9 4.0 %collective-permute-start.25 = (bf16[512,256]{1,0:T(8,128)(2,1)S(1)}, bf16[512,256]{1,0:T(8,128)(2,1)}, u32[]{:S(2)}, u32[]{:S(2)}) collective-permute-start(bf16[512,256]{1,0:T(8,128)(2,1)S(1)} %collective-permute-done.21.refs_3_), channel_id=1, source_target_pairs={{0,16},{16,0},{1,17},{17,1},{2,18},{18,2},{3,19},{19,3},{4,20},{20... | collective-permute-start | bytes 786440 | tf_op jit(solution)/shard_map/ppermute | solution.py:307

commit v2 on v1

--- a/solution.py
+++ b/solution.py
@@ -13,7 +13,7 @@
 COLS = 16
 SUBS = 128
 CW = 32
-PAUSE = 1300
+PAUSE = 2200
 N = MAXT * TILE
 RT = NB // ROWS
 CT = NB // COLS
@@ -201,22 +201,14 @@
         panel[i] = dens[:, i * TILE : (i + 1) * TILE]
 
 
-def stack_kernel(*refs):
-    blocks, stacks, clock, sems = refs[:8], refs[8:10], refs[10], refs[11]
-    clock[...] = jnp.zeros_like(clock)
+def pause_kernel(shift, out):
+    out[...] = jnp.full_like(out, jnp.abs(shift[0]))
 
     def tick(_, carry):
-        clock[...] = clock[...] + 1.0
+        out[...] = out[...] + 1.0
         return carry
 
     lax.fori_loop(0, PAUSE, tick, 0)
-    copies = [
-        pltpu.make_async_copy(blocks[i], stacks[i // 4].at[i % 4], sems.at[i]) for i in range(8)
-    ]
-    for copy in copies:
-        copy.start()
-    for copy in copies:
-        copy.wait()
 
 
 def spread_kernel(table, panels, out, mine, sems):
@@ -352,16 +344,12 @@
         (top, bottom, *strip[1:]),
         (FAR, FAR),
     )
+    packed, late = lax.optimization_barrier((packed, shift))
     tiles = lax.all_to_all(packed, COL, 0, 0, tiled=True)
-    ahead, across = call(
-        stack_kernel,
-        (pltpu.HBM((4, half, WIDTH), BF16), pltpu.HBM((4, half, WIDTH), BF16)),
-        [pltpu.VMEM((8, TILE), F32), pltpu.SemaphoreType.DMA((8,))],
-        (),
-        (*ahead, *across),
-        (FAR, FAR),
-        pltpu.HBM,
-    )
+    clock = call(pause_kernel, pltpu.VMEM((8, TILE), F32), [], (late,), ())
+    go = clock[0, 0] >= 0.0
+    ahead = jnp.stack(ahead[:1] + [jnp.where(go, x, jnp.zeros_like(x)) for x in ahead[1:]])
+    across = jnp.stack(across[:1] + [jnp.where(go, x, jnp.zeros_like(x)) for x in across[1:]])
     ahead = from_ring(ahead, "c0")
     across = from_ring(across, "c1")
     panel = call_solve(table, shift, tiles, first)

time: 233 us -> 181 us (0.78)
  Pallas kernels: 67.2 us -> 40.7 us
  waiting for transfers between devices: 84.8 us -> 65.7 us
  starting transfers between devices: 57.3 us -> 48.6 us
  other arithmetic: 0.11 us -> 3.96 us
    pallas_call x6, Pallas kernels: 67.2 us -> 40.7 us  [call(): pl.pallas_call(kernel, out_shape=outs, in_specs=[SMEM] * len(small) + [LO...]
    all_to_all x1, waiting for transfers between devices: 25.8 us -> 0.01 us  [steps(): tiles = lax.all_to_all(packed, COL, 0, 0, tiled=True)]
    ppermute x8, starting transfers between devices: 21.1 us -> 11.4 us  [swapped(): return lax.ppermute(x, 'core', [(0, 1), (1, 0)])]
    ppermute x18, waiting for transfers between devices: 58 us -> 64.8 us  [from_ring(): lax.ppermute(x, axis, [((i + k) % 4, i) for i in range(4)])]
    another operation x0 -> x8, other arithmetic: none -> 3.86 us  [the longest x4 2.84 us: steps(): jnp.stack(across[:1] + [jnp.where(go, x, jnp.zeros_like(x)) for x in acro...]
    unnamed x27 -> x7, local copies, waits for them, and re-layouts: 4.24 us -> 0.81 us
  transfers between devices with their start and end apart: 28 -> 28, of which waited for: 9 -> 10; matrix products, arithmetic and copies ran while one was open for 2% -> 5% of each run, Pallas kernels for 25% -> 18%
where the time goes in v2:
time: 181 us
  waiting for transfers between devices  65.7 us (36%)
  starting transfers between devices  48.6 us (27%)
  Pallas kernels  40.7 us (22%)
  blocking collectives  14.5 us (8%)
  local copies, waits for them, and re-layouts  4.84 us (3%)
  other arithmetic  3.96 us (2%)
  between operations  2.11 us (1%)
    ppermute x18, waiting for transfers between devices, from_ring(): lax.ppermute(x, axis, [((i + k) % 4, i) for i in range(4)])  64.8 us
    pallas_call x6, Pallas kernels, call(): pl.pallas_call(kernel, out_shape=outs, in_specs=[SMEM] * len(small) + [LO...  40.7 us
    ppermute x18, starting transfers between devices, from_ring(): lax.ppermute(x, axis, [((i + k) % 4, i) for i in range(4)])  25.6 us
    all_gather x1, blocking collectives, steps(): panels = lax.all_gather(panel, ROW, axis=0, tiled=False)  14.5 us
    ppermute x8, starting transfers between devices, swapped(): return lax.ppermute(x, 'core', [(0, 1), (1, 0)])  11.4 us
    all_to_all x1, starting transfers between devices, steps(): tiles = lax.all_to_all(packed, COL, 0, 0, tiled=True)  6.9 us
    all_to_all x1, starting transfers between devices, steps(): arrived = lax.all_to_all(spread, COL, 0, 0, tiled=True)  4.71 us
  transfers between devices with their start and end apart: 28, of which 10 were waited for; matrix products, arithmetic and copies ran while one was open for 5% of the time, Pallas kernels for 18%

profile of v2, /device:TPU:1, one launch (start us, length us, event | category | flops | bytes accessed | tf_op | source)
XLA Modules:
  0.0 180.5 jit_solution(14679487720038102792)
XLA Ops:
  0.6 4.6 %collective-permute-start = (bf16[512,256]{1,0:T(8,128)(2,1)}, bf16[512,256]{1,0:T(8,128)(2,1)S(1)}, u32[]{:S(2)}, u32[]{:S(2)}) collective-permute-start(bf16[512,256]{1,0:T(8,128)(2,1)} %param.5), channel_id=1, source_target_pairs={{32,0},{64,32},{96,64},{0,96},{33,1},{65,33},{97,65},{1,97},{34,2}... | collective-permute-start | bytes 786440 | tf_op jit(solution)/shard_map/ppermute | solution.py:295
  5.3 0.0 collective-permute-start.1
  5.3 0.7 collective-permute-start.2
  6.0 1.5 collective-permute-start.3
  7.5 8.6 %collective-permute-done.refs_2_ = bf16[512,256]{1,0:T(8,128)(2,1)S(1)} collective-permute-done((bf16[512,256]{1,0:T(8,128)(2,1)}, bf16[512,256]{1,0:T(8,128)(2,1)S(1)}, u32[]{:S(2)}, u32[]{:S(2)}) %collective-permute-start) | collective-permute-done | bytes 262176 | tf_op jit(solution)/shard_map/ppermute | solution.py:295
  16.1 1.7 collective-permute-start.4
  17.7 0.0 collective-permute-start.5
  17.7 2.5 %collective-permute-done.2.refs_4_ = bf16[512,256]{1,0:T(8,128)(2,1)S(1)} collective-permute-done((bf16[512,256]{1,0:T(8,128)(2,1)}, bf16[512,256]{1,0:T(8,128)(2,1)S(1)}, u32[]{:S(2)}, u32[]{:S(2)}) %collective-permute-start.2) | collective-permute-done | bytes 262176 | tf_op jit(solution)/shard_map/ppermute | solution.py:295
  20.3 0.8 collective-permute-start.6
  21.0 0.8 copy.12
  21.8 0.1 reshape.38
  21.9 0.8 reshape.39
  22.7 0.7 concatenate.3.table
  23.4 1.7 slice_bitcast_fusion
  25.1 0.0 collective-permute-done.6.refs_8_
  25.1 3.4 %shard_map.68 = (bf16[16,4,128,128]{3,2,1,0:T(8,128)(2,1)}, bf16[8,128,128]{2,1,0:T(8,128)(2,1)}) custom-call(s32[2178]{0:T(1024)S(1)} %concatenate.3.table, bf16[256,256]{1,0:T(8,128)(2,1)S(1)} %get-tuple-element.13.refs_0_, bf16[256,256]{1,0:T(8,128)(2,1)S(1)} %get-tuple-element.12.refs_1_, bf16[512,256]{1,0:T(8,128)(2,1)S(1)} %collective-permute-done.refs_2_, ...), custom_call_target="tpu_custom_call" | custom-call | tf_op jit(solution)/shard_map/pallas_call | solution.py:308
  28.5 0.0 copy-start
  28.5 6.9 %all-to-all-start = ((bf16[16,4,128,128]{3,2,1,0:T(8,128)(2,1)}), bf16[16,4,128,128]{3,2,1,0:T(8,128)(2,1)S(1)}, u32[]{:S(2)}, u32[]{:S(2)}) async-start(bf16[16,4,128,128]{3,2,1,0:T(8,128)(2,1)} %get-tuple-element.7), calls=%async_computation | async-start | bytes 4194304 | tf_op jit(solution)/shard_map/all_to_all | solution.py:348
  35.4 1.4 collective-permute-start.9
  36.8 2.4 %collective-permute-start.8 = (bf16[256,256]{1,0:T(8,128)(2,1)S(1)}, bf16[256,256]{1,0:T(8,128)(2,1)S(1)}, u32[]{:S(2)}, u32[]{:S(2)}) collective-permute-start(bf16[256,256]{1,0:T(8,128)(2,1)S(1)} %get-tuple-element.13.refs_0_), channel_id=1, source_target_pairs={{2,0},{3,1},{0,2},{1,3},{6,4},{7,5},{4,6},{5,7},{10,8},{11,9},{8,1... | collective-permute-start | bytes 393224 | tf_op jit(solution)/shard_map/ppermute | solution.py:295
  39.2 1.2 collective-permute-start.7
  40.4 1.2 collective-permute-start.15
  41.6 2.4 %collective-permute-start.14 = (bf16[256,256]{1,0:T(8,128)(2,1)S(1)}, bf16[256,256]{1,0:T(8,128)(2,1)}, u32[]{:S(2)}, u32[]{:S(2)}) collective-permute-start(bf16[256,256]{1,0:T(8,128)(2,1)S(1)} %get-tuple-element.12.refs_1_), channel_id=1, source_target_pairs={{8,0},{12,4},{0,8},{4,12},{9,1},{13,5},{1,9},{5,13},{10,2},{14,6},... | collective-permute-start | bytes 393224 | tf_op jit(solution)/shard_map/ppermute | solution.py:295
  44.6 15.1 %shard_map.71 = f32[8,128]{1,0:T(8,128)S(1)} custom-call(f32[1]{0:T(128)S(6)} %copy.14.shift), custom_call_target="tpu_custom_call" | custom-call | tf_op jit(solution)/shard_map/pallas_call | solution.py:308
  59.7 0.5 slice.11
  60.8 5.3 %collective-permute-done.9 = bf16[256,256]{1,0:T(8,128)(2,1)S(1)} collective-permute-done((bf16[256,256]{1,0:T(8,128)(2,1)S(1)}, bf16[256,256]{1,0:T(8,128)(2,1)S(1)}, u32[]{:S(2)}, u32[]{:S(2)}) %collective-permute-start.9) | collective-permute-done | bytes 131104 | tf_op jit(solution)/shard_map/ppermute | solution.py:295
  66.2 0.4 collective-permute-start.13
  66.6 0.8 collective-permute-done.8
  67.4 1.0 pad_maximum_fusion.a0
  68.4 3.2 %collective-permute-start.10 = (bf16[4,256,256]{2,1,0:T(8,128)(2,1)S(1)}, bf16[4,256,256]{2,1,0:T(8,128)(2,1)}, u32[]{:S(2)}, u32[]{:S(2)}) collective-permute-start(bf16[4,256,256]{2,1,0:T(8,128)(2,1)S(1)} %pad_maximum_fusion.a0), channel_id=1, source_target_pairs={{4,0},{8,4},{12,8},{0,12},{5,1},{9,5},{13,9},{1,13},{6,2},{10,6},{... | collective-permute-start | bytes 1572872 | tf_op jit(solution)/shard_map/ppermute | solution.py:295
  71.7 0.9 collective-permute-start.11
  72.6 0.0 all-to-all-done.tiles
  72.6 8.8 %shard_map.69 = bf16[8,32,128]{2,1,0:T(8,128)(2,1)S(1)} custom-call(s32[2178]{0:T(1024)S(1)} %concatenate.3.table, f32[1]{0:T(128)S(6)} %copy.14.shift, bf16[16,4,128,128]{3,2,1,0:T(8,128)(2,1)S(1)} %all-to-all-done.tiles, bf16[8,128,128]{2,1,0:T(8,128)(2,1)S(1)} %copy-done), custom_call_target="tpu_custom_call" | custom-call | tf_op jit(solution)/shard_map/pallas_call | solution.py:308
  81.3 14.5 %all-gather = bf16[64,32,128]{2,1,0:T(8,128)(2,1)S(1)} all-gather(bf16[8,32,128]{2,1,0:T(8,128)(2,1)S(1)} %shard_map.69), channel_id=2, replica_groups=mesh['z'=4,'core'=2,'c0'=4,'c1'=4] {'z','core'}, dimensions={0}, use_global_device_ids=true | all-gather | bytes 589824 | tf_op jit(solution)/shard_map/all_gather | solution.py:356
  95.9 3.6 %shard_map.70 = bf16[16,8,2,32,128]{4,3,2,1,0:T(8,128)(2,1)} custom-call(s32[2178]{0:T(1024)S(1)} %concatenate.3.table, bf16[8,8,32,128]{3,2,1,0:T(8,128)(2,1)S(1)} %bitcast.20), custom_call_target="tpu_custom_call" | custom-call | tf_op jit(solution)/shard_map/pallas_call | solution.py:308
  99.4 4.7 %all-to-all-start.1 = ((bf16[16,8,2,32,128]{4,3,2,1,0:T(8,128)(2,1)}), bf16[16,8,2,32,128]{4,3,2,1,0:T(8,128)(2,1)S(1)}, u32[]{:S(2)}, u32[]{:S(2)}) async-start(bf16[16,8,2,32,128]{4,3,2,1,0:T(8,128)(2,1)} %shard_map.70), calls=%async_computation.1 | async-start | bytes 4194304 | tf_op jit(solution)/shard_map/all_to_all | solution.py:365
  104.2 1.4 collective-permute-start.12
  105.6 0.9 select_bitcast_fusion
  106.5 0.9 select_bitcast_fusion.1
  107.5 0.9 select_bitcast_fusion.2
  108.4 0.1 pad_maximum_fusion.1.b0
  108.5 0.0 copy-start.2
  108.5 0.0 copy-start.1
  108.5 2.5 %collective-permute-start.16 = (bf16[4,256,256]{2,1,0:T(8,128)(2,1)S(1)}, bf16[4,256,256]{2,1,0:T(8,128)(2,1)S(1)}, u32[]{:S(2)}, u32[]{:S(2)}) collective-permute-start(bf16[4,256,256]{2,1,0:T(8,128)(2,1)S(1)} %pad_maximum_fusion.1.b0), channel_id=1, source_target_pairs={{1,0},{2,1},{3,2},{0,3},{5,4},{6,5},{7,6},{4,7},{9,8},{10,9},{11,1... | collective-permute-start | bytes 1572872 | tf_op jit(solution)/shard_map/ppermute | solution.py:295
  111.0 0.6 collective-permute-start.17
  111.5 0.6 collective-permute-start.18
  112.1 29.9 %collective-permute-done.12.a3 = bf16[4,256,256]{2,1,0:T(8,128)(2,1)S(1)} collective-permute-done((bf16[4,256,256]{2,1,0:T(8,128)(2,1)S(1)}, bf16[4,256,256]{2,1,0:T(8,128)(2,1)S(1)}, u32[]{:S(2)}, u32[]{:S(2)}) %collective-permute-start.12) | collective-permute-done | bytes 524320 | tf_op jit(solution)/shard_map/ppermute | solution.py:295
  142.0 0.1 collective-permute-done.17.b2
  142.2 10.6 %collective-permute-done.18.b3 = bf16[4,256,256]{2,1,0:T(8,128)(2,1)S(1)} collective-permute-done((bf16[4,256,256]{2,1,0:T(8,128)(2,1)S(1)}, bf16[4,256,256]{2,1,0:T(8,128)(2,1)S(1)}, u32[]{:S(2)}, u32[]{:S(2)}) %collective-permute-start.18) | collective-permute-done | bytes 524320 | tf_op jit(solution)/shard_map/ppermute | solution.py:295
  152.7 5.2 %shard_map.72.refs_0_ = bf16[512,256]{1,0:T(8,128)(2,1)S(1)} custom-call(s32[2178]{0:T(1024)S(1)} %concatenate.3.table, bf16[4,256,256]{2,1,0:T(8,128)(2,1)S(1)} %pad_maximum_fusion.a0, bf16[4,256,256]{2,1,0:T(8,128)(2,1)} %collective-permute-done.10.a1, bf16[4,256,256]{2,1,0:T(8,128)(2,1)} %collective-permute-done.11.a2, ...), custom_call_target="tpu_custom_call" | custom-call | tf_op jit(solution)/shard_map/pallas_call | solution.py:308
  157.9 0.7 collective-permute-start.19
  158.6 0.7 collective-permute-start.20
  159.3 0.8 collective-permute-start.21
  160.1 1.6 collective-permute-start.22
  161.7 3.4 %collective-permute-done.19.refs_1_ = bf16[512,256]{1,0:T(8,128)(2,1)S(1)} collective-permute-done((bf16[512,256]{1,0:T(8,128)(2,1)S(1)}, bf16[512,256]{1,0:T(8,128)(2,1)S(1)}, u32[]{:S(2)}, u32[]{:S(2)}) %collective-permute-start.19) | collective-permute-done | bytes 262176 | tf_op jit(solution)/shard_map/ppermute | solution.py:295
  165.1 2.9 %collective-permute-start.23 = (bf16[512,256]{1,0:T(8,128)(2,1)S(1)}, bf16[512,256]{1,0:T(8,128)(2,1)}, u32[]{:S(2)}, u32[]{:S(2)}) collective-permute-start(bf16[512,256]{1,0:T(8,128)(2,1)S(1)} %collective-permute-done.19.refs_1_), channel_id=1, source_target_pairs={{0,16},{16,0},{1,17},{17,1},{2,18},{18,2},{3,19},{19,3},{4,20},{20... | collective-permute-start | bytes 786440 | tf_op jit(solution)/shard_map/ppermute | solution.py:299
  168.0 2.4 %collective-permute-start.24 = (bf16[512,256]{1,0:T(8,128)(2,1)S(1)}, bf16[512,256]{1,0:T(8,128)(2,1)}, u32[]{:S(2)}, u32[]{:S(2)}) collective-permute-start(bf16[512,256]{1,0:T(8,128)(2,1)S(1)} %collective-permute-done.20.refs_2_), channel_id=1, source_target_pairs={{0,16},{16,0},{1,17},{17,1},{2,18},{18,2},{3,19},{19,3},{4,20},{20... | collective-permute-start | bytes 786440 | tf_op jit(solution)/shard_map/ppermute | solution.py:299
  170.4 3.6 %collective-permute-done.21.refs_3_ = bf16[512,256]{1,0:T(8,128)(2,1)S(1)} collective-permute-done((bf16[512,256]{1,0:T(8,128)(2,1)S(1)}, bf16[512,256]{1,0:T(8,128)(2,1)S(1)}, u32[]{:S(2)}, u32[]{:S(2)}) %collective-permute-start.21) | collective-permute-done | bytes 262176 | tf_op jit(solution)/shard_map/ppermute | solution.py:295
  174.0 0.5 collective-permute-start.25
  174.5 0.1 and_reduce_fusion
  174.6 0.1 copy.13
  174.7 0.1 reshape.40.present
  174.9 0.9 collective-permute-done.25.refs_7_
  175.8 4.8 %shard_map.73 = (bf16[512,256]{1,0:T(8,128)(2,1)}, f32[512,256]{1,0:T(8,128)}) custom-call(s32[2178]{0:T(1024)S(1)} %concatenate.3.table, s32[512]{0:T(512)S(1)} %reshape.40.present, bf16[16,8,2,32,128]{4,3,2,1,0:T(8,128)(2,1)S(1)} %all-to-all-done.1.pieces, bf16[512,256]{1,0:T(8,128)(2,1)S(1)} %shard_map.72.refs_0_, ...), custom_call_target="tpu_custom_call" | custom-call | tf_op jit(solution)/shard_map/pallas_call | solution.py:308
  (25 shorter events, 0.1 us)
Async XLA Ops:
  0.6 15.4 %collective-permute-start = (bf16[512,256]{1,0:T(8,128)(2,1)}, bf16[512,256]{1,0:T(8,128)(2,1)S(1)}, u32[]{:S(2)}, u32[]{:S(2)}) collective-permute-start(bf16[512,256]{1,0:T(8,128)(2,1)} %param.5), channel_id=1, source_target_pairs={{32,0},{64,32},{96,64},{0,96},{33,1},{65,33},{97,65},{1,97},{34,2}... | collective-permute-start | bytes 786440 | tf_op jit(solution)/shard_map/ppermute | solution.py:295
  5.3 12.5 %collective-permute-start.1 = (bf16[512,256]{1,0:T(8,128)(2,1)}, bf16[512,256]{1,0:T(8,128)(2,1)S(1)}, u32[]{:S(2)}, u32[]{:S(2)}) collective-permute-start(bf16[512,256]{1,0:T(8,128)(2,1)} %param.5), channel_id=1, source_target_pairs={{64,0},{96,32},{0,64},{32,96},{65,1},{97,33},{1,65},{33,97},{66,2}... | collective-permute-start | bytes 786440 | tf_op jit(solution)/shard_map/ppermute | solution.py:295
  5.3 15.0 %collective-permute-start.2 = (bf16[512,256]{1,0:T(8,128)(2,1)}, bf16[512,256]{1,0:T(8,128)(2,1)S(1)}, u32[]{:S(2)}, u32[]{:S(2)}) collective-permute-start(bf16[512,256]{1,0:T(8,128)(2,1)} %param.5), channel_id=1, source_target_pairs={{96,0},{0,32},{32,64},{64,96},{97,1},{1,33},{33,65},{65,97},{98,2}... | collective-permute-start | bytes 786440 | tf_op jit(solution)/shard_map/ppermute | solution.py:295
  6.0 19.1 %collective-permute-start.3 = (bf16[512,256]{1,0:T(8,128)(2,1)}, bf16[512,256]{1,0:T(8,128)(2,1)S(1)}, u32[]{:S(2)}, u32[]{:S(2)}) collective-permute-start(bf16[512,256]{1,0:T(8,128)(2,1)} %param.5), channel_id=1, source_target_pairs={{0,16},{16,0},{1,17},{17,1},{2,18},{18,2},{3,19},{19,3},{4,20},{20... | collective-permute-start | bytes 786440 | tf_op jit(solution)/shard_map/ppermute | solution.py:299
  16.1 9.0 %collective-permute-start.4 = (bf16[512,256]{1,0:T(8,128)(2,1)S(1)}, bf16[512,256]{1,0:T(8,128)(2,1)S(1)}, u32[]{:S(2)}, u32[]{:S(2)}) collective-permute-start(bf16[512,256]{1,0:T(8,128)(2,1)S(1)} %collective-permute-done.refs_2_), channel_id=1, source_target_pairs={{0,16},{16,0},{1,17},{17,1},{2,18},{18,2},{3,19},{19,3},{4,20},{20... | collective-permute-start | bytes 786440 | tf_op jit(solution)/shard_map/ppermute | solution.py:299
  17.7 7.4 %collective-permute-start.5 = (bf16[512,256]{1,0:T(8,128)(2,1)S(1)}, bf16[512,256]{1,0:T(8,128)(2,1)S(1)}, u32[]{:S(2)}, u32[]{:S(2)}) collective-permute-start(bf16[512,256]{1,0:T(8,128)(2,1)S(1)} %collective-permute-done.1.refs_3_), channel_id=1, source_target_pairs={{0,16},{16,0},{1,17},{17,1},{2,18},{18,2},{3,19},{19,3},{4,20},{20... | collective-permute-start | bytes 786440 | tf_op jit(solution)/shard_map/ppermute | solution.py:299
  20.3 4.9 %collective-permute-start.6 = (bf16[512,256]{1,0:T(8,128)(2,1)S(1)}, bf16[512,256]{1,0:T(8,128)(2,1)S(1)}, u32[]{:S(2)}, u32[]{:S(2)}) collective-permute-start(bf16[512,256]{1,0:T(8,128)(2,1)S(1)} %collective-permute-done.2.refs_4_), channel_id=1, source_target_pairs={{0,16},{16,0},{1,17},{17,1},{2,18},{18,2},{3,19},{19,3},{4,20},{20... | collective-permute-start | bytes 786440 | tf_op jit(solution)/shard_map/ppermute | solution.py:299
  28.5 44.0 %copy-start = (bf16[8,128,128]{2,1,0:T(8,128)(2,1)S(1)}, bf16[8,128,128]{2,1,0:T(8,128)(2,1)}, u32[]{:S(2)}) copy-start(bf16[8,128,128]{2,1,0:T(8,128)(2,1)} %get-tuple-element.8.first) | copy-start | bytes 786436
  28.5 44.0 %all-to-all-start = ((bf16[16,4,128,128]{3,2,1,0:T(8,128)(2,1)}), bf16[16,4,128,128]{3,2,1,0:T(8,128)(2,1)S(1)}, u32[]{:S(2)}, u32[]{:S(2)}) async-start(bf16[16,4,128,128]{3,2,1,0:T(8,128)(2,1)} %get-tuple-element.7), calls=%async_computation | async-start | bytes 4194304 | tf_op jit(solution)/shard_map/all_to_all | solution.py:348
  35.4 30.7 %collective-permute-start.9 = (bf16[256,256]{1,0:T(8,128)(2,1)S(1)}, bf16[256,256]{1,0:T(8,128)(2,1)S(1)}, u32[]{:S(2)}, u32[]{:S(2)}) collective-permute-start(bf16[256,256]{1,0:T(8,128)(2,1)S(1)} %get-tuple-element.13.refs_0_), channel_id=1, source_target_pairs={{3,0},{0,1},{1,2},{2,3},{7,4},{4,5},{5,6},{6,7},{11,8},{8,9},{9,10... | collective-permute-start | bytes 393224 | tf_op jit(solution)/shard_map/ppermute | solution.py:295
  36.8 30.6 %collective-permute-start.8 = (bf16[256,256]{1,0:T(8,128)(2,1)S(1)}, bf16[256,256]{1,0:T(8,128)(2,1)S(1)}, u32[]{:S(2)}, u32[]{:S(2)}) collective-permute-start(bf16[256,256]{1,0:T(8,128)(2,1)S(1)} %get-tuple-element.13.refs_0_), channel_id=1, source_target_pairs={{2,0},{3,1},{0,2},{1,3},{6,4},{7,5},{4,6},{5,7},{10,8},{11,9},{8,1... | collective-permute-start | bytes 393224 | tf_op jit(solution)/shard_map/ppermute | solution.py:295
  39.2 28.2 %collective-permute-start.7 = (bf16[256,256]{1,0:T(8,128)(2,1)S(1)}, bf16[256,256]{1,0:T(8,128)(2,1)S(1)}, u32[]{:S(2)}, u32[]{:S(2)}) collective-permute-start(bf16[256,256]{1,0:T(8,128)(2,1)S(1)} %get-tuple-element.13.refs_0_), channel_id=1, source_target_pairs={{1,0},{2,1},{3,2},{0,3},{5,4},{6,5},{7,6},{4,7},{9,8},{10,9},{11,1... | collective-permute-start | bytes 393224 | tf_op jit(solution)/shard_map/ppermute | solution.py:295
  40.4 63.8 %collective-permute-start.15 = (bf16[256,256]{1,0:T(8,128)(2,1)S(1)}, bf16[256,256]{1,0:T(8,128)(2,1)}, u32[]{:S(2)}, u32[]{:S(2)}) collective-permute-start(bf16[256,256]{1,0:T(8,128)(2,1)S(1)} %get-tuple-element.12.refs_1_), channel_id=1, source_target_pairs={{12,0},{0,4},{4,8},{8,12},{13,1},{1,5},{5,9},{9,13},{14,2},{2,6},{... | collective-permute-start | bytes 393224 | tf_op jit(solution)/shard_map/ppermute | solution.py:295
  41.6 65.0 %collective-permute-start.14 = (bf16[256,256]{1,0:T(8,128)(2,1)S(1)}, bf16[256,256]{1,0:T(8,128)(2,1)}, u32[]{:S(2)}, u32[]{:S(2)}) collective-permute-start(bf16[256,256]{1,0:T(8,128)(2,1)S(1)} %get-tuple-element.12.refs_1_), channel_id=1, source_target_pairs={{8,0},{12,4},{0,8},{4,12},{9,1},{13,5},{1,9},{5,13},{10,2},{14,6},... | collective-permute-start | bytes 393224 | tf_op jit(solution)/shard_map/ppermute | solution.py:295
  66.2 41.3 %collective-permute-start.13 = (bf16[256,256]{1,0:T(8,128)(2,1)S(1)}, bf16[256,256]{1,0:T(8,128)(2,1)}, u32[]{:S(2)}, u32[]{:S(2)}) collective-permute-start(bf16[256,256]{1,0:T(8,128)(2,1)S(1)} %get-tuple-element.12.refs_1_), channel_id=1, source_target_pairs={{4,0},{8,4},{12,8},{0,12},{5,1},{9,5},{13,9},{1,13},{6,2},{10,6},{... | collective-permute-start | bytes 393224 | tf_op jit(solution)/shard_map/ppermute | solution.py:295
  68.4 43.1 %collective-permute-start.10 = (bf16[4,256,256]{2,1,0:T(8,128)(2,1)S(1)}, bf16[4,256,256]{2,1,0:T(8,128)(2,1)}, u32[]{:S(2)}, u32[]{:S(2)}) collective-permute-start(bf16[4,256,256]{2,1,0:T(8,128)(2,1)S(1)} %pad_maximum_fusion.a0), channel_id=1, source_target_pairs={{4,0},{8,4},{12,8},{0,12},{5,1},{9,5},{13,9},{1,13},{6,2},{10,6},{... | collective-permute-start | bytes 1572872 | tf_op jit(solution)/shard_map/ppermute | solution.py:295
  71.7 40.5 %collective-permute-start.11 = (bf16[4,256,256]{2,1,0:T(8,128)(2,1)S(1)}, bf16[4,256,256]{2,1,0:T(8,128)(2,1)}, u32[]{:S(2)}, u32[]{:S(2)}) collective-permute-start(bf16[4,256,256]{2,1,0:T(8,128)(2,1)S(1)} %pad_maximum_fusion.a0), channel_id=1, source_target_pairs={{8,0},{12,4},{0,8},{4,12},{9,1},{13,5},{1,9},{5,13},{10,2},{14,6},... | collective-permute-start | bytes 1572872 | tf_op jit(solution)/shard_map/ppermute | solution.py:295
  99.4 76.3 %all-to-all-start.1 = ((bf16[16,8,2,32,128]{4,3,2,1,0:T(8,128)(2,1)}), bf16[16,8,2,32,128]{4,3,2,1,0:T(8,128)(2,1)S(1)}, u32[]{:S(2)}, u32[]{:S(2)}) async-start(bf16[16,8,2,32,128]{4,3,2,1,0:T(8,128)(2,1)} %shard_map.70), calls=%async_computation.1 | async-start | bytes 4194304 | tf_op jit(solution)/shard_map/all_to_all | solution.py:365
  104.2 37.9 %collective-permute-start.12 = (bf16[4,256,256]{2,1,0:T(8,128)(2,1)S(1)}, bf16[4,256,256]{2,1,0:T(8,128)(2,1)S(1)}, u32[]{:S(2)}, u32[]{:S(2)}) collective-permute-start(bf16[4,256,256]{2,1,0:T(8,128)(2,1)S(1)} %pad_maximum_fusion.a0), channel_id=1, source_target_pairs={{12,0},{0,4},{4,8},{8,12},{13,1},{1,5},{5,9},{9,13},{14,2},{2,6},{... | collective-permute-start | bytes 1572872 | tf_op jit(solution)/shard_map/ppermute | solution.py:295
  108.5 66.0 %copy-start.2 = (s32[128]{0:T(128)S(1)}, s32[128]{0:T(128)}, u32[]{:S(2)}) copy-start(s32[128]{0:T(128)} %param.8) | copy-start | bytes 1540
  108.5 66.0 %copy-start.1 = (s32[128,8]{0,1:T(8,128)S(1)}, s32[128,8]{0,1:T(8,128)}, u32[]{:S(2)}) copy-start(s32[128,8]{0,1:T(8,128)} %param.7) | copy-start | bytes 12292
  108.5 33.5 %collective-permute-start.16 = (bf16[4,256,256]{2,1,0:T(8,128)(2,1)S(1)}, bf16[4,256,256]{2,1,0:T(8,128)(2,1)S(1)}, u32[]{:S(2)}, u32[]{:S(2)}) collective-permute-start(bf16[4,256,256]{2,1,0:T(8,128)(2,1)S(1)} %pad_maximum_fusion.1.b0), channel_id=1, source_target_pairs={{1,0},{2,1},{3,2},{0,3},{5,4},{6,5},{7,6},{4,7},{9,8},{10,9},{11,1... | collective-permute-start | bytes 1572872 | tf_op jit(solution)/shard_map/ppermute | solution.py:295
  111.0 31.2 %collective-permute-start.17 = (bf16[4,256,256]{2,1,0:T(8,128)(2,1)S(1)}, bf16[4,256,256]{2,1,0:T(8,128)(2,1)S(1)}, u32[]{:S(2)}, u32[]{:S(2)}) collective-permute-start(bf16[4,256,256]{2,1,0:T(8,128)(2,1)S(1)} %pad_maximum_fusion.1.b0), channel_id=1, source_target_pairs={{2,0},{3,1},{0,2},{1,3},{6,4},{7,5},{4,6},{5,7},{10,8},{11,9},{8,1... | collective-permute-start | bytes 1572872 | tf_op jit(solution)/shard_map/ppermute | solution.py:295
  111.5 41.2 %collective-permute-start.18 = (bf16[4,256,256]{2,1,0:T(8,128)(2,1)S(1)}, bf16[4,256,256]{2,1,0:T(8,128)(2,1)S(1)}, u32[]{:S(2)}, u32[]{:S(2)}) collective-permute-start(bf16[4,256,256]{2,1,0:T(8,128)(2,1)S(1)} %pad_maximum_fusion.1.b0), channel_id=1, source_target_pairs={{3,0},{0,1},{1,2},{2,3},{7,4},{4,5},{5,6},{6,7},{11,8},{8,9},{9,10... | collective-permute-start | bytes 1572872 | tf_op jit(solution)/shard_map/ppermute | solution.py:295
  157.9 7.2 %collective-permute-start.19 = (bf16[512,256]{1,0:T(8,128)(2,1)S(1)}, bf16[512,256]{1,0:T(8,128)(2,1)S(1)}, u32[]{:S(2)}, u32[]{:S(2)}) collective-permute-start(bf16[512,256]{1,0:T(8,128)(2,1)S(1)} %shard_map.72.refs_0_), channel_id=1, source_target_pairs={{32,0},{64,32},{96,64},{0,96},{33,1},{65,33},{97,65},{1,97},{34,2}... | collective-permute-start | bytes 786440 | tf_op jit(solution)/shard_map/ppermute | solution.py:295
  158.6 9.4 %collective-permute-start.20 = (bf16[512,256]{1,0:T(8,128)(2,1)S(1)}, bf16[512,256]{1,0:T(8,128)(2,1)S(1)}, u32[]{:S(2)}, u32[]{:S(2)}) collective-permute-start(bf16[512,256]{1,0:T(8,128)(2,1)S(1)} %shard_map.72.refs_0_), channel_id=1, source_target_pairs={{64,0},{96,32},{0,64},{32,96},{65,1},{97,33},{1,65},{33,97},{66,2}... | collective-permute-start | bytes 786440 | tf_op jit(solution)/shard_map/ppermute | solution.py:295
  159.3 14.7 %collective-permute-start.21 = (bf16[512,256]{1,0:T(8,128)(2,1)S(1)}, bf16[512,256]{1,0:T(8,128)(2,1)S(1)}, u32[]{:S(2)}, u32[]{:S(2)}) collective-permute-start(bf16[512,256]{1,0:T(8,128)(2,1)S(1)} %shard_map.72.refs_0_), channel_id=1, source_target_pairs={{96,0},{0,32},{32,64},{64,96},{97,1},{1,33},{33,65},{65,97},{98,2}... | collective-permute-start | bytes 786440 | tf_op jit(solution)/shard_map/ppermute | solution.py:295
  160.1 14.8 %collective-permute-start.22 = (bf16[512,256]{1,0:T(8,128)(2,1)S(1)}, bf16[512,256]{1,0:T(8,128)(2,1)S(1)}, u32[]{:S(2)}, u32[]{:S(2)}) collective-permute-start(bf16[512,256]{1,0:T(8,128)(2,1)S(1)} %shard_map.72.refs_0_), channel_id=1, source_target_pairs={{0,16},{16,0},{1,17},{17,1},{2,18},{18,2},{3,19},{19,3},{4,20},{20... | collective-permute-start | bytes 786440 | tf_op jit(solution)/shard_map/ppermute | solution.py:299
  165.1 9.7 %collective-permute-start.23 = (bf16[512,256]{1,0:T(8,128)(2,1)S(1)}, bf16[512,256]{1,0:T(8,128)(2,1)}, u32[]{:S(2)}, u32[]{:S(2)}) collective-permute-start(bf16[512,256]{1,0:T(8,128)(2,1)S(1)} %collective-permute-done.19.refs_1_), channel_id=1, source_target_pairs={{0,16},{16,0},{1,17},{17,1},{2,18},{18,2},{3,19},{19,3},{4,20},{20... | collective-permute-start | bytes 786440 | tf_op jit(solution)/shard_map/ppermute | solution.py:299
  168.0 6.9 %collective-permute-start.24 = (bf16[512,256]{1,0:T(8,128)(2,1)S(1)}, bf16[512,256]{1,0:T(8,128)(2,1)}, u32[]{:S(2)}, u32[]{:S(2)}) collective-permute-start(bf16[512,256]{1,0:T(8,128)(2,1)S(1)} %collective-permute-done.20.refs_2_), channel_id=1, source_target_pairs={{0,16},{16,0},{1,17},{17,1},{2,18},{18,2},{3,19},{19,3},{4,20},{20... | collective-permute-start | bytes 786440 | tf_op jit(solution)/shard_map/ppermute | solution.py:299
  174.0 1.8 collective-permute-start.25

commit v3 on v2

--- a/solution.py
+++ b/solution.py
@@ -13,7 +13,6 @@
 COLS = 16
 SUBS = 128
 CW = 32
-PAUSE = 2200
 N = MAXT * TILE
 RT = NB // ROWS
 CT = NB // COLS
@@ -199,16 +198,6 @@
     dens = (jnp.where(prow == pcol, 0.5, 0.0) - 0.5 * z).astype(BF16)
     for i in range(MAXT):
         panel[i] = dens[:, i * TILE : (i + 1) * TILE]
-
-
-def pause_kernel(shift, out):
-    out[...] = jnp.full_like(out, jnp.abs(shift[0]))
-
-    def tick(_, carry):
-        out[...] = out[...] + 1.0
-        return carry
-
-    lax.fori_loop(0, PAUSE, tick, 0)
 
 
 def spread_kernel(table, panels, out, mine, sems):
@@ -333,8 +322,8 @@
     half = RT * TILE // 2
     top, bottom = hamiltonian[:half], hamiltonian[half:]
     strip = from_ring(hamiltonian, "z")
+    across = from_ring(bottom, "c0")
     ahead = from_ring(top, "c1")
-    across = from_ring(bottom, "c0")
     strip = strip + [swapped(x) for x in strip]
     packed, first = call(
         pack_kernel,
@@ -344,14 +333,10 @@
         (top, bottom, *strip[1:]),
         (FAR, FAR),
     )
-    packed, late = lax.optimization_barrier((packed, shift))
+    packed, ahead, across = lax.optimization_barrier((packed, ahead, across))
     tiles = lax.all_to_all(packed, COL, 0, 0, tiled=True)
-    clock = call(pause_kernel, pltpu.VMEM((8, TILE), F32), [], (late,), ())
-    go = clock[0, 0] >= 0.0
-    ahead = jnp.stack(ahead[:1] + [jnp.where(go, x, jnp.zeros_like(x)) for x in ahead[1:]])
-    across = jnp.stack(across[:1] + [jnp.where(go, x, jnp.zeros_like(x)) for x in across[1:]])
-    ahead = from_ring(ahead, "c0")
-    across = from_ring(across, "c1")
+    across = from_ring(jnp.stack(across), "c1")
+    ahead = from_ring(jnp.stack(ahead), "c0")
     panel = call_solve(table, shift, tiles, first)
     panels = lax.all_gather(panel, ROW, axis=0, tiled=False)
     spread = call(

time: 181 us -> 186 us (1.028)
  waiting for transfers between devices: 65.7 us -> 85.3 us
  Pallas kernels: 40.7 us -> 25.2 us
  blocking collectives: 14.5 us -> 17.8 us
  other arithmetic: 3.96 us -> 1.15 us
    all_to_all x1, waiting for transfers between devices: 0.01 us -> 25 us  [steps(): tiles = lax.all_to_all(packed, COL, 0, 0, tiled=True)]
    pallas_call x6 -> x5, Pallas kernels: 40.7 us -> 25.2 us  [call(): pl.pallas_call(kernel, out_shape=outs, in_specs=[SMEM] * len(small) + [LO...]
    ppermute x18, waiting for transfers between devices: 64.8 us -> 59.3 us  [from_ring(): lax.ppermute(x, axis, [((i + k) % 4, i) for i in range(4)])]
    all_gather x1, blocking collectives: 14.5 us -> 17.8 us  [steps(): panels = lax.all_gather(panel, ROW, axis=0, tiled=False)]
    all_to_all x1, starting transfers between devices: 6.9 us -> 3.9 us  [steps(): tiles = lax.all_to_all(packed, COL, 0, 0, tiled=True)]
    ppermute x18, starting transfers between devices: 25.6 us -> 28.5 us  [from_ring(): lax.ppermute(x, axis, [((i + k) % 4, i) for i in range(4)])]
    another operation x8 -> x2, other arithmetic: 3.86 us -> 1.04 us  [the longest x1 0.97 us: steps(): ahead = from_ring(jnp.stack(ahead), 'c0')]
  transfers between devices with their start and end apart: 28 -> 28, of which waited for: 10 -> 12; matrix products, arithmetic and copies ran while one was open for 5% -> 3% of each run, Pallas kernels for 18% -> 4%
where the time goes in v3:
time: 186 us; the launch traced here: 184 us
  waiting for transfers between devices  85.3 us (46%)
  starting transfers between devices  49.3 us (27%)
  Pallas kernels  25.2 us (14%)
  blocking collectives  17.8 us (10%)
  local copies, waits for them, and re-layouts  4.26 us (2%)
    ppermute x18, waiting for transfers between devices, from_ring(): lax.ppermute(x, axis, [((i + k) % 4, i) for i in range(4)])  59.3 us
    ppermute x18, starting transfers between devices, from_ring(): lax.ppermute(x, axis, [((i + k) % 4, i) for i in range(4)])  28.5 us
    pallas_call x5, Pallas kernels, call(): pl.pallas_call(kernel, out_shape=outs, in_specs=[SMEM] * len(small) + [LO...  25.2 us
    all_to_all x1, waiting for transfers between devices, steps(): tiles = lax.all_to_all(packed, COL, 0, 0, tiled=True)  25 us
    all_gather x1, blocking collectives, steps(): panels = lax.all_gather(panel, ROW, axis=0, tiled=False)  17.8 us
    ppermute x8, starting transfers between devices, swapped(): return lax.ppermute(x, 'core', [(0, 1), (1, 0)])  13.2 us
    all_to_all x1, starting transfers between devices, steps(): tiles = lax.all_to_all(packed, COL, 0, 0, tiled=True)  3.9 us
    all_to_all x1, starting transfers between devices, steps(): arrived = lax.all_to_all(spread, COL, 0, 0, tiled=True)  3.73 us
  transfers between devices with their start and end apart: 28, of which 12 were waited for; matrix products, arithmetic and copies ran while one was open for 3% of the time, Pallas kernels for 4%

profile of v3, /device:TPU:1, one launch (start us, length us, event | category | flops | bytes accessed | tf_op | source)
XLA Modules:
  0.0 184.5 jit_solution(5548233572174785224)
XLA Ops:
  0.6 4.6 %collective-permute-start = (bf16[512,256]{1,0:T(8,128)(2,1)}, bf16[512,256]{1,0:T(8,128)(2,1)S(1)}, u32[]{:S(2)}, u32[]{:S(2)}) collective-permute-start(bf16[512,256]{1,0:T(8,128)(2,1)} %param.5), channel_id=1, source_target_pairs={{32,0},{64,32},{96,64},{0,96},{33,1},{65,33},{97,65},{1,97},{34,2}... | collective-permute-start | bytes 786440 | tf_op jit(solution)/shard_map/ppermute | solution.py:284
  5.3 0.0 collective-permute-start.1
  5.3 0.7 collective-permute-start.2
  6.0 1.5 collective-permute-start.3
  7.5 8.6 %collective-permute-done.refs_2_ = bf16[512,256]{1,0:T(8,128)(2,1)S(1)} collective-permute-done((bf16[512,256]{1,0:T(8,128)(2,1)}, bf16[512,256]{1,0:T(8,128)(2,1)S(1)}, u32[]{:S(2)}, u32[]{:S(2)}) %collective-permute-start) | collective-permute-done | bytes 262176 | tf_op jit(solution)/shard_map/ppermute | solution.py:284
  16.1 1.7 collective-permute-start.4
  17.7 0.0 collective-permute-start.5
  17.7 2.5 %collective-permute-done.2.refs_4_ = bf16[512,256]{1,0:T(8,128)(2,1)S(1)} collective-permute-done((bf16[512,256]{1,0:T(8,128)(2,1)}, bf16[512,256]{1,0:T(8,128)(2,1)S(1)}, u32[]{:S(2)}, u32[]{:S(2)}) %collective-permute-start.2) | collective-permute-done | bytes 262176 | tf_op jit(solution)/shard_map/ppermute | solution.py:284
  20.3 0.8 collective-permute-start.6
  21.0 1.0 fusion
  22.0 1.3 collective-permute-start.12
  23.3 5.0 %collective-permute-done.12 = bf16[256,256]{1,0:T(8,128)(2,1)S(1)} collective-permute-done((bf16[256,256]{1,0:T(8,128)(2,1)S(1)}, bf16[256,256]{1,0:T(8,128)(2,1)S(1)}, u32[]{:S(2)}, u32[]{:S(2)}) %collective-permute-start.12) | collective-permute-done | bytes 131104 | tf_op jit(solution)/shard_map/ppermute | solution.py:284
  28.4 1.5 collective-permute-start.11
  29.9 0.0 collective-permute-done.3.refs_5_
  29.9 0.9 collective-permute-start.10
  30.8 1.3 collective-permute-start.9
  32.1 0.0 collective-permute-done.5.refs_7_
  32.1 2.6 %collective-permute-start.8 = (bf16[256,256]{1,0:T(8,128)(2,1)S(1)}, bf16[256,256]{1,0:T(8,128)(2,1)S(1)}, u32[]{:S(2)}, u32[]{:S(2)}) collective-permute-start(bf16[256,256]{1,0:T(8,128)(2,1)S(1)} %get-tuple-element.16.refs_0_), channel_id=1, source_target_pairs={{2,0},{3,1},{0,2},{1,3},{6,4},{7,5},{4,6},{5,7},{10,8},{11,9},{8,1... | collective-permute-start | bytes 393224 | tf_op jit(solution)/shard_map/ppermute | solution.py:284
  34.7 0.0 collective-permute-done.6.refs_8_
  34.7 1.1 collective-permute-start.7
  35.8 0.8 reshape.37
  36.5 0.8 copy.12
  37.3 0.1 reshape.36
  37.4 0.7 concatenate.3.table
  38.2 3.4 %shard_map.68 = (bf16[16,4,128,128]{3,2,1,0:T(8,128)(2,1)}, bf16[8,128,128]{2,1,0:T(8,128)(2,1)}) custom-call(s32[2178]{0:T(1024)S(1)} %concatenate.3.table, bf16[256,256]{1,0:T(8,128)(2,1)S(1)} %get-tuple-element.16.refs_0_, bf16[256,256]{1,0:T(8,128)(2,1)S(1)} %get-tuple-element.20.refs_1_, bf16[512,256]{1,0:T(8,128)(2,1)S(1)} %collective-permute-done.refs_2_, ...), custom_call_target="tpu_custom_call" | custom-call | tf_op jit(solution)/shard_map/pallas_call | solution.py:297
  41.6 0.0 copy-start.1
  41.6 0.0 copy-start
  41.6 0.6 copy-done.1
  42.3 3.9 %all-to-all-start = ((bf16[16,4,128,128]{3,2,1,0:T(8,128)(2,1)}), bf16[16,4,128,128]{3,2,1,0:T(8,128)(2,1)S(1)}, u32[]{:S(2)}, u32[]{:S(2)}) async-start(bf16[16,4,128,128]{3,2,1,0:T(8,128)(2,1)} %get-tuple-element.14), calls=%async_computation | async-start | bytes 4194304 | tf_op jit(solution)/shard_map/all_to_all | solution.py:337
  46.8 25.0 %all-to-all-done.tiles = bf16[16,4,128,128]{3,2,1,0:T(8,128)(2,1)S(1)} async-done(((bf16[16,4,128,128]{3,2,1,0:T(8,128)(2,1)}), bf16[16,4,128,128]{3,2,1,0:T(8,128)(2,1)S(1)}, u32[]{:S(2)}, u32[]{:S(2)}) %all-to-all-start) | async-done | bytes 2097184 | tf_op jit(solution)/shard_map/all_to_all | solution.py:337
  71.8 8.8 %shard_map.69 = bf16[8,32,128]{2,1,0:T(8,128)(2,1)S(1)} custom-call(s32[2178]{0:T(1024)S(1)} %concatenate.3.table, f32[1]{0:T(128)S(6)} %copy.14.shift, bf16[16,4,128,128]{3,2,1,0:T(8,128)(2,1)S(1)} %all-to-all-done.tiles, bf16[8,128,128]{2,1,0:T(8,128)(2,1)S(1)} %copy-done), custom_call_target="tpu_custom_call" | custom-call | tf_op jit(solution)/shard_map/pallas_call | solution.py:297
  80.6 17.8 %all-gather = bf16[64,32,128]{2,1,0:T(8,128)(2,1)S(1)} all-gather(bf16[8,32,128]{2,1,0:T(8,128)(2,1)S(1)} %shard_map.69), channel_id=2, replica_groups=mesh['z'=4,'core'=2,'c0'=4,'c1'=4] {'z','core'}, dimensions={0}, use_global_device_ids=true | all-gather | bytes 589824 | tf_op jit(solution)/shard_map/all_gather | solution.py:341
  98.4 3.6 %shard_map.70 = bf16[16,8,2,32,128]{4,3,2,1,0:T(8,128)(2,1)} custom-call(s32[2178]{0:T(1024)S(1)} %concatenate.3.table, bf16[8,8,32,128]{3,2,1,0:T(8,128)(2,1)S(1)} %bitcast.11), custom_call_target="tpu_custom_call" | custom-call | tf_op jit(solution)/shard_map/pallas_call | solution.py:297
  102.0 3.7 %all-to-all-start.1 = ((bf16[16,8,2,32,128]{4,3,2,1,0:T(8,128)(2,1)}), bf16[16,8,2,32,128]{4,3,2,1,0:T(8,128)(2,1)S(1)}, u32[]{:S(2)}, u32[]{:S(2)}) async-start(bf16[16,8,2,32,128]{4,3,2,1,0:T(8,128)(2,1)} %shard_map.70), calls=%async_computation.1 | async-start | bytes 4194304 | tf_op jit(solution)/shard_map/all_to_all | solution.py:350
  105.7 0.1 pad_maximum_fusion.1.b0
  105.8 1.3 collective-permute-start.18
  107.1 2.4 %collective-permute-start.17 = (bf16[4,256,256]{2,1,0:T(8,128)(2,1)S(1)}, bf16[4,256,256]{2,1,0:T(8,128)(2,1)S(1)}, u32[]{:S(2)}, u32[]{:S(2)}) collective-permute-start(bf16[4,256,256]{2,1,0:T(8,128)(2,1)S(1)} %pad_maximum_fusion.1.b0), channel_id=1, source_target_pairs={{2,0},{3,1},{0,2},{1,3},{6,4},{7,5},{4,6},{5,7},{10,8},{11,9},{8,1... | collective-permute-start | bytes 1572872 | tf_op jit(solution)/shard_map/ppermute | solution.py:284
  109.5 1.2 collective-permute-start.16
  110.7 1.0 pad_maximum_fusion.a0
  111.6 0.0 copy-start.3
  111.7 0.0 copy-start.2
  111.7 1.3 collective-permute-start.15
  112.9 2.4 %collective-permute-start.14 = (bf16[4,256,256]{2,1,0:T(8,128)(2,1)S(1)}, bf16[4,256,256]{2,1,0:T(8,128)(2,1)S(1)}, u32[]{:S(2)}, u32[]{:S(2)}) collective-permute-start(bf16[4,256,256]{2,1,0:T(8,128)(2,1)S(1)} %pad_maximum_fusion.a0), channel_id=1, source_target_pairs={{8,0},{12,4},{0,8},{4,12},{9,1},{13,5},{1,9},{5,13},{10,2},{14,6},... | collective-permute-start | bytes 1572872 | tf_op jit(solution)/shard_map/ppermute | solution.py:284
  115.4 27.5 %collective-permute-done.18.b3 = bf16[4,256,256]{2,1,0:T(8,128)(2,1)S(1)} collective-permute-done((bf16[4,256,256]{2,1,0:T(8,128)(2,1)S(1)}, bf16[4,256,256]{2,1,0:T(8,128)(2,1)S(1)}, u32[]{:S(2)}, u32[]{:S(2)}) %collective-permute-start.18) | collective-permute-done | bytes 524320 | tf_op jit(solution)/shard_map/ppermute | solution.py:284
  142.9 2.6 %collective-permute-start.13 = (bf16[4,256,256]{2,1,0:T(8,128)(2,1)S(1)}, bf16[4,256,256]{2,1,0:T(8,128)(2,1)S(1)}, u32[]{:S(2)}, u32[]{:S(2)}) collective-permute-start(bf16[4,256,256]{2,1,0:T(8,128)(2,1)S(1)} %pad_maximum_fusion.a0), channel_id=1, source_target_pairs={{4,0},{8,4},{12,8},{0,12},{5,1},{9,5},{13,9},{1,13},{6,2},{10,6},{... | collective-permute-start | bytes 1572872 | tf_op jit(solution)/shard_map/ppermute | solution.py:284
  145.5 8.7 %collective-permute-done.17.b2 = bf16[4,256,256]{2,1,0:T(8,128)(2,1)S(1)} collective-permute-done((bf16[4,256,256]{2,1,0:T(8,128)(2,1)S(1)}, bf16[4,256,256]{2,1,0:T(8,128)(2,1)S(1)}, u32[]{:S(2)}, u32[]{:S(2)}) %collective-permute-start.17) | collective-permute-done | bytes 524320 | tf_op jit(solution)/shard_map/ppermute | solution.py:284
  154.2 0.2 collective-permute-done.16.b1
  154.4 3.0 %collective-permute-done.14.a2 = bf16[4,256,256]{2,1,0:T(8,128)(2,1)S(1)} collective-permute-done((bf16[4,256,256]{2,1,0:T(8,128)(2,1)S(1)}, bf16[4,256,256]{2,1,0:T(8,128)(2,1)S(1)}, u32[]{:S(2)}, u32[]{:S(2)}) %collective-permute-start.14) | collective-permute-done | bytes 524320 | tf_op jit(solution)/shard_map/ppermute | solution.py:284
  157.4 4.7 %shard_map.71.refs_0_ = bf16[512,256]{1,0:T(8,128)(2,1)S(1)} custom-call(s32[2178]{0:T(1024)S(1)} %concatenate.3.table, bf16[4,256,256]{2,1,0:T(8,128)(2,1)S(1)} %pad_maximum_fusion.a0, bf16[4,256,256]{2,1,0:T(8,128)(2,1)S(1)} %collective-permute-done.13.a1, bf16[4,256,256]{2,1,0:T(8,128)(2,1)S(1)} %collective-permute-done.14.a2, ...), custom_call_target="tpu_custom_call" | custom-call | tf_op jit(solution)/shard_map/pallas_call | solution.py:297
  162.1 0.1 collective-permute-start.21
  162.1 1.8 collective-permute-start.20
  163.9 1.4 collective-permute-start.19
  165.4 1.9 %collective-permute-start.22 = (bf16[512,256]{1,0:T(8,128)(2,1)S(1)}, bf16[512,256]{1,0:T(8,128)(2,1)S(1)}, u32[]{:S(2)}, u32[]{:S(2)}) collective-permute-start(bf16[512,256]{1,0:T(8,128)(2,1)S(1)} %shard_map.71.refs_0_), channel_id=1, source_target_pairs={{0,16},{16,0},{1,17},{17,1},{2,18},{18,2},{3,19},{19,3},{4,20},{20... | collective-permute-start | bytes 786440 | tf_op jit(solution)/shard_map/ppermute | solution.py:288
  167.3 3.7 %collective-permute-done.21.refs_3_ = bf16[512,256]{1,0:T(8,128)(2,1)S(1)} collective-permute-done((bf16[512,256]{1,0:T(8,128)(2,1)S(1)}, bf16[512,256]{1,0:T(8,128)(2,1)S(1)}, u32[]{:S(2)}, u32[]{:S(2)}) %collective-permute-start.21) | collective-permute-done | bytes 262176 | tf_op jit(solution)/shard_map/ppermute | solution.py:284
  171.0 6.7 %collective-permute-start.25 = (bf16[512,256]{1,0:T(8,128)(2,1)S(1)}, bf16[512,256]{1,0:T(8,128)(2,1)}, u32[]{:S(2)}, u32[]{:S(2)}) collective-permute-start(bf16[512,256]{1,0:T(8,128)(2,1)S(1)} %collective-permute-done.21.refs_3_), channel_id=1, source_target_pairs={{0,16},{16,0},{1,17},{17,1},{2,18},{18,2},{3,19},{19,3},{4,20},{20... | collective-permute-start | bytes 786440 | tf_op jit(solution)/shard_map/ppermute | solution.py:288
  177.7 0.0 collective-permute-start.24
  177.7 0.6 collective-permute-start.23
  178.3 0.1 and_reduce_fusion
  178.4 0.1 copy.13
  178.5 0.1 reshape.38.present
  178.6 0.3 collective-permute-done.25.refs_7_
  179.0 0.4 collective-permute-done.24.refs_6_
  179.3 0.4 collective-permute-done.23.refs_5_
  179.7 4.8 %shard_map.72 = (bf16[512,256]{1,0:T(8,128)(2,1)}, f32[512,256]{1,0:T(8,128)}) custom-call(s32[2178]{0:T(1024)S(1)} %concatenate.3.table, s32[512]{0:T(512)S(1)} %reshape.38.present, bf16[16,8,2,32,128]{4,3,2,1,0:T(8,128)(2,1)S(1)} %all-to-all-done.1.pieces, bf16[512,256]{1,0:T(8,128)(2,1)S(1)} %shard_map.71.refs_0_, ...), custom_call_target="tpu_custom_call" | custom-call | tf_op jit(solution)/shard_map/pallas_call | solution.py:297
  (19 shorter events, 0.1 us)
Async XLA Ops:
  0.6 15.4 %collective-permute-start = (bf16[512,256]{1,0:T(8,128)(2,1)}, bf16[512,256]{1,0:T(8,128)(2,1)S(1)}, u32[]{:S(2)}, u32[]{:S(2)}) collective-permute-start(bf16[512,256]{1,0:T(8,128)(2,1)} %param.5), channel_id=1, source_target_pairs={{32,0},{64,32},{96,64},{0,96},{33,1},{65,33},{97,65},{1,97},{34,2}... | collective-permute-start | bytes 786440 | tf_op jit(solution)/shard_map/ppermute | solution.py:284
  5.3 12.5 %collective-permute-start.1 = (bf16[512,256]{1,0:T(8,128)(2,1)}, bf16[512,256]{1,0:T(8,128)(2,1)S(1)}, u32[]{:S(2)}, u32[]{:S(2)}) collective-permute-start(bf16[512,256]{1,0:T(8,128)(2,1)} %param.5), channel_id=1, source_target_pairs={{64,0},{96,32},{0,64},{32,96},{65,1},{97,33},{1,65},{33,97},{66,2}... | collective-permute-start | bytes 786440 | tf_op jit(solution)/shard_map/ppermute | solution.py:284
  5.3 15.0 %collective-permute-start.2 = (bf16[512,256]{1,0:T(8,128)(2,1)}, bf16[512,256]{1,0:T(8,128)(2,1)S(1)}, u32[]{:S(2)}, u32[]{:S(2)}) collective-permute-start(bf16[512,256]{1,0:T(8,128)(2,1)} %param.5), channel_id=1, source_target_pairs={{96,0},{0,32},{32,64},{64,96},{97,1},{1,33},{33,65},{65,97},{98,2}... | collective-permute-start | bytes 786440 | tf_op jit(solution)/shard_map/ppermute | solution.py:284
  6.0 23.9 %collective-permute-start.3 = (bf16[512,256]{1,0:T(8,128)(2,1)}, bf16[512,256]{1,0:T(8,128)(2,1)S(1)}, u32[]{:S(2)}, u32[]{:S(2)}) collective-permute-start(bf16[512,256]{1,0:T(8,128)(2,1)} %param.5), channel_id=1, source_target_pairs={{0,16},{16,0},{1,17},{17,1},{2,18},{18,2},{3,19},{19,3},{4,20},{20... | collective-permute-start | bytes 786440 | tf_op jit(solution)/shard_map/ppermute | solution.py:288
  16.1 14.7 %collective-permute-start.4 = (bf16[512,256]{1,0:T(8,128)(2,1)S(1)}, bf16[512,256]{1,0:T(8,128)(2,1)S(1)}, u32[]{:S(2)}, u32[]{:S(2)}) collective-permute-start(bf16[512,256]{1,0:T(8,128)(2,1)S(1)} %collective-permute-done.refs_2_), channel_id=1, source_target_pairs={{0,16},{16,0},{1,17},{17,1},{2,18},{18,2},{3,19},{19,3},{4,20},{20... | collective-permute-start | bytes 786440 | tf_op jit(solution)/shard_map/ppermute | solution.py:288
  17.7 14.3 %collective-permute-start.5 = (bf16[512,256]{1,0:T(8,128)(2,1)S(1)}, bf16[512,256]{1,0:T(8,128)(2,1)S(1)}, u32[]{:S(2)}, u32[]{:S(2)}) collective-permute-start(bf16[512,256]{1,0:T(8,128)(2,1)S(1)} %collective-permute-done.1.refs_3_), channel_id=1, source_target_pairs={{0,16},{16,0},{1,17},{17,1},{2,18},{18,2},{3,19},{19,3},{4,20},{20... | collective-permute-start | bytes 786440 | tf_op jit(solution)/shard_map/ppermute | solution.py:288
  20.3 14.4 %collective-permute-start.6 = (bf16[512,256]{1,0:T(8,128)(2,1)S(1)}, bf16[512,256]{1,0:T(8,128)(2,1)S(1)}, u32[]{:S(2)}, u32[]{:S(2)}) collective-permute-start(bf16[512,256]{1,0:T(8,128)(2,1)S(1)} %collective-permute-done.2.refs_4_), channel_id=1, source_target_pairs={{0,16},{16,0},{1,17},{17,1},{2,18},{18,2},{3,19},{19,3},{4,20},{20... | collective-permute-start | bytes 786440 | tf_op jit(solution)/shard_map/ppermute | solution.py:288
  22.0 6.3 %collective-permute-start.12 = (bf16[256,256]{1,0:T(8,128)(2,1)S(1)}, bf16[256,256]{1,0:T(8,128)(2,1)S(1)}, u32[]{:S(2)}, u32[]{:S(2)}) collective-permute-start(bf16[256,256]{1,0:T(8,128)(2,1)S(1)} %get-tuple-element.20.refs_1_), channel_id=1, source_target_pairs={{12,0},{0,4},{4,8},{8,12},{13,1},{1,5},{5,9},{9,13},{14,2},{2,6},{... | collective-permute-start | bytes 393224 | tf_op jit(solution)/shard_map/ppermute | solution.py:284
  28.4 13.2 %collective-permute-start.11 = (bf16[256,256]{1,0:T(8,128)(2,1)S(1)}, bf16[256,256]{1,0:T(8,128)(2,1)S(1)}, u32[]{:S(2)}, u32[]{:S(2)}) collective-permute-start(bf16[256,256]{1,0:T(8,128)(2,1)S(1)} %get-tuple-element.20.refs_1_), channel_id=1, source_target_pairs={{8,0},{12,4},{0,8},{4,12},{9,1},{13,5},{1,9},{5,13},{10,2},{14,6},... | collective-permute-start | bytes 393224 | tf_op jit(solution)/shard_map/ppermute | solution.py:284
  29.9 11.7 %collective-permute-start.10 = (bf16[256,256]{1,0:T(8,128)(2,1)S(1)}, bf16[256,256]{1,0:T(8,128)(2,1)S(1)}, u32[]{:S(2)}, u32[]{:S(2)}) collective-permute-start(bf16[256,256]{1,0:T(8,128)(2,1)S(1)} %get-tuple-element.20.refs_1_), channel_id=1, source_target_pairs={{4,0},{8,4},{12,8},{0,12},{5,1},{9,5},{13,9},{1,13},{6,2},{10,6},{... | collective-permute-start | bytes 393224 | tf_op jit(solution)/shard_map/ppermute | solution.py:284
  30.8 10.8 %collective-permute-start.9 = (bf16[256,256]{1,0:T(8,128)(2,1)S(1)}, bf16[256,256]{1,0:T(8,128)(2,1)S(1)}, u32[]{:S(2)}, u32[]{:S(2)}) collective-permute-start(bf16[256,256]{1,0:T(8,128)(2,1)S(1)} %get-tuple-element.16.refs_0_), channel_id=1, source_target_pairs={{3,0},{0,1},{1,2},{2,3},{7,4},{4,5},{5,6},{6,7},{11,8},{8,9},{9,10... | collective-permute-start | bytes 393224 | tf_op jit(solution)/shard_map/ppermute | solution.py:284
  32.1 9.5 %collective-permute-start.8 = (bf16[256,256]{1,0:T(8,128)(2,1)S(1)}, bf16[256,256]{1,0:T(8,128)(2,1)S(1)}, u32[]{:S(2)}, u32[]{:S(2)}) collective-permute-start(bf16[256,256]{1,0:T(8,128)(2,1)S(1)} %get-tuple-element.16.refs_0_), channel_id=1, source_target_pairs={{2,0},{3,1},{0,2},{1,3},{6,4},{7,5},{4,6},{5,7},{10,8},{11,9},{8,1... | collective-permute-start | bytes 393224 | tf_op jit(solution)/shard_map/ppermute | solution.py:284
  34.7 6.9 %collective-permute-start.7 = (bf16[256,256]{1,0:T(8,128)(2,1)S(1)}, bf16[256,256]{1,0:T(8,128)(2,1)S(1)}, u32[]{:S(2)}, u32[]{:S(2)}) collective-permute-start(bf16[256,256]{1,0:T(8,128)(2,1)S(1)} %get-tuple-element.16.refs_0_), channel_id=1, source_target_pairs={{1,0},{2,1},{3,2},{0,3},{5,4},{6,5},{7,6},{4,7},{9,8},{10,9},{11,1... | collective-permute-start | bytes 393224 | tf_op jit(solution)/shard_map/ppermute | solution.py:284
  41.6 0.7 copy-start.1
  41.6 30.2 %copy-start = (bf16[8,128,128]{2,1,0:T(8,128)(2,1)S(1)}, bf16[8,128,128]{2,1,0:T(8,128)(2,1)}, u32[]{:S(2)}) copy-start(bf16[8,128,128]{2,1,0:T(8,128)(2,1)} %get-tuple-element.15.first) | copy-start | bytes 786436
  42.3 29.5 %all-to-all-start = ((bf16[16,4,128,128]{3,2,1,0:T(8,128)(2,1)}), bf16[16,4,128,128]{3,2,1,0:T(8,128)(2,1)S(1)}, u32[]{:S(2)}, u32[]{:S(2)}) async-start(bf16[16,4,128,128]{3,2,1,0:T(8,128)(2,1)} %get-tuple-element.14), calls=%async_computation | async-start | bytes 4194304 | tf_op jit(solution)/shard_map/all_to_all | solution.py:337
  102.0 77.8 %all-to-all-start.1 = ((bf16[16,8,2,32,128]{4,3,2,1,0:T(8,128)(2,1)}), bf16[16,8,2,32,128]{4,3,2,1,0:T(8,128)(2,1)S(1)}, u32[]{:S(2)}, u32[]{:S(2)}) async-start(bf16[16,8,2,32,128]{4,3,2,1,0:T(8,128)(2,1)} %shard_map.70), calls=%async_computation.1 | async-start | bytes 4194304 | tf_op jit(solution)/shard_map/all_to_all | solution.py:350
  105.8 37.2 %collective-permute-start.18 = (bf16[4,256,256]{2,1,0:T(8,128)(2,1)S(1)}, bf16[4,256,256]{2,1,0:T(8,128)(2,1)S(1)}, u32[]{:S(2)}, u32[]{:S(2)}) collective-permute-start(bf16[4,256,256]{2,1,0:T(8,128)(2,1)S(1)} %pad_maximum_fusion.1.b0), channel_id=1, source_target_pairs={{3,0},{0,1},{1,2},{2,3},{7,4},{4,5},{5,6},{6,7},{11,8},{8,9},{9,10... | collective-permute-start | bytes 1572872 | tf_op jit(solution)/shard_map/ppermute | solution.py:284
  107.1 47.1 %collective-permute-start.17 = (bf16[4,256,256]{2,1,0:T(8,128)(2,1)S(1)}, bf16[4,256,256]{2,1,0:T(8,128)(2,1)S(1)}, u32[]{:S(2)}, u32[]{:S(2)}) collective-permute-start(bf16[4,256,256]{2,1,0:T(8,128)(2,1)S(1)} %pad_maximum_fusion.1.b0), channel_id=1, source_target_pairs={{2,0},{3,1},{0,2},{1,3},{6,4},{7,5},{4,6},{5,7},{10,8},{11,9},{8,1... | collective-permute-start | bytes 1572872 | tf_op jit(solution)/shard_map/ppermute | solution.py:284
  109.5 44.9 %collective-permute-start.16 = (bf16[4,256,256]{2,1,0:T(8,128)(2,1)S(1)}, bf16[4,256,256]{2,1,0:T(8,128)(2,1)S(1)}, u32[]{:S(2)}, u32[]{:S(2)}) collective-permute-start(bf16[4,256,256]{2,1,0:T(8,128)(2,1)S(1)} %pad_maximum_fusion.1.b0), channel_id=1, source_target_pairs={{1,0},{2,1},{3,2},{0,3},{5,4},{6,5},{7,6},{4,7},{9,8},{10,9},{11,1... | collective-permute-start | bytes 1572872 | tf_op jit(solution)/shard_map/ppermute | solution.py:284
  111.6 66.7 %copy-start.3 = (s32[128]{0:T(128)S(1)}, s32[128]{0:T(128)}, u32[]{:S(2)}) copy-start(s32[128]{0:T(128)} %param.8) | copy-start | bytes 1540
  111.7 66.7 %copy-start.2 = (s32[128,8]{0,1:T(8,128)S(1)}, s32[128,8]{0,1:T(8,128)}, u32[]{:S(2)}) copy-start(s32[128,8]{0,1:T(8,128)} %param.7) | copy-start | bytes 12292
  111.7 42.7 %collective-permute-start.15 = (bf16[4,256,256]{2,1,0:T(8,128)(2,1)S(1)}, bf16[4,256,256]{2,1,0:T(8,128)(2,1)S(1)}, u32[]{:S(2)}, u32[]{:S(2)}) collective-permute-start(bf16[4,256,256]{2,1,0:T(8,128)(2,1)S(1)} %pad_maximum_fusion.a0), channel_id=1, source_target_pairs={{12,0},{0,4},{4,8},{8,12},{13,1},{1,5},{5,9},{9,13},{14,2},{2,6},{... | collective-permute-start | bytes 1572872 | tf_op jit(solution)/shard_map/ppermute | solution.py:284
  112.9 44.4 %collective-permute-start.14 = (bf16[4,256,256]{2,1,0:T(8,128)(2,1)S(1)}, bf16[4,256,256]{2,1,0:T(8,128)(2,1)S(1)}, u32[]{:S(2)}, u32[]{:S(2)}) collective-permute-start(bf16[4,256,256]{2,1,0:T(8,128)(2,1)S(1)} %pad_maximum_fusion.a0), channel_id=1, source_target_pairs={{8,0},{12,4},{0,8},{4,12},{9,1},{13,5},{1,9},{5,13},{10,2},{14,6},... | collective-permute-start | bytes 1572872 | tf_op jit(solution)/shard_map/ppermute | solution.py:284
  142.9 14.4 %collective-permute-start.13 = (bf16[4,256,256]{2,1,0:T(8,128)(2,1)S(1)}, bf16[4,256,256]{2,1,0:T(8,128)(2,1)S(1)}, u32[]{:S(2)}, u32[]{:S(2)}) collective-permute-start(bf16[4,256,256]{2,1,0:T(8,128)(2,1)S(1)} %pad_maximum_fusion.a0), channel_id=1, source_target_pairs={{4,0},{8,4},{12,8},{0,12},{5,1},{9,5},{13,9},{1,13},{6,2},{10,6},{... | collective-permute-start | bytes 1572872 | tf_op jit(solution)/shard_map/ppermute | solution.py:284
  162.1 8.9 %collective-permute-start.21 = (bf16[512,256]{1,0:T(8,128)(2,1)S(1)}, bf16[512,256]{1,0:T(8,128)(2,1)S(1)}, u32[]{:S(2)}, u32[]{:S(2)}) collective-permute-start(bf16[512,256]{1,0:T(8,128)(2,1)S(1)} %shard_map.71.refs_0_), channel_id=1, source_target_pairs={{96,0},{0,32},{32,64},{64,96},{97,1},{1,33},{33,65},{65,97},{98,2}... | collective-permute-start | bytes 786440 | tf_op jit(solution)/shard_map/ppermute | solution.py:284
  162.1 15.5 %collective-permute-start.20 = (bf16[512,256]{1,0:T(8,128)(2,1)S(1)}, bf16[512,256]{1,0:T(8,128)(2,1)S(1)}, u32[]{:S(2)}, u32[]{:S(2)}) collective-permute-start(bf16[512,256]{1,0:T(8,128)(2,1)S(1)} %shard_map.71.refs_0_), channel_id=1, source_target_pairs={{64,0},{96,32},{0,64},{32,96},{65,1},{97,33},{1,65},{33,97},{66,2}... | collective-permute-start | bytes 786440 | tf_op jit(solution)/shard_map/ppermute | solution.py:284
  163.9 13.7 %collective-permute-start.19 = (bf16[512,256]{1,0:T(8,128)(2,1)S(1)}, bf16[512,256]{1,0:T(8,128)(2,1)S(1)}, u32[]{:S(2)}, u32[]{:S(2)}) collective-permute-start(bf16[512,256]{1,0:T(8,128)(2,1)S(1)} %shard_map.71.refs_0_), channel_id=1, source_target_pairs={{32,0},{64,32},{96,64},{0,96},{33,1},{65,33},{97,65},{1,97},{34,2}... | collective-permute-start | bytes 786440 | tf_op jit(solution)/shard_map/ppermute | solution.py:284
  165.4 13.3 %collective-permute-start.22 = (bf16[512,256]{1,0:T(8,128)(2,1)S(1)}, bf16[512,256]{1,0:T(8,128)(2,1)S(1)}, u32[]{:S(2)}, u32[]{:S(2)}) collective-permute-start(bf16[512,256]{1,0:T(8,128)(2,1)S(1)} %shard_map.71.refs_0_), channel_id=1, source_target_pairs={{0,16},{16,0},{1,17},{17,1},{2,18},{18,2},{3,19},{19,3},{4,20},{20... | collective-permute-start | bytes 786440 | tf_op jit(solution)/shard_map/ppermute | solution.py:288
  171.0 8.0 %collective-permute-start.25 = (bf16[512,256]{1,0:T(8,128)(2,1)S(1)}, bf16[512,256]{1,0:T(8,128)(2,1)}, u32[]{:S(2)}, u32[]{:S(2)}) collective-permute-start(bf16[512,256]{1,0:T(8,128)(2,1)S(1)} %collective-permute-done.21.refs_3_), channel_id=1, source_target_pairs={{0,16},{16,0},{1,17},{17,1},{2,18},{18,2},{3,19},{19,3},{4,20},{20... | collective-permute-start | bytes 786440 | tf_op jit(solution)/shard_map/ppermute | solution.py:288
  177.7 1.7 collective-permute-start.24
  177.7 2.0 %collective-permute-start.23 = (bf16[512,256]{1,0:T(8,128)(2,1)S(1)}, bf16[512,256]{1,0:T(8,128)(2,1)}, u32[]{:S(2)}, u32[]{:S(2)}) collective-permute-start(bf16[512,256]{1,0:T(8,128)(2,1)S(1)} %collective-permute-done.19.refs_1_), channel_id=1, source_target_pairs={{0,16},{16,0},{1,17},{17,1},{2,18},{18,2},{3,19},{19,3},{4,20},{20... | collective-permute-start | bytes 786440 | tf_op jit(solution)/shard_map/ppermute | solution.py:288

commit v4 on v3

--- a/solution.py
+++ b/solution.py
@@ -203,16 +203,17 @@
 def spread_kernel(table, panels, out, mine, sems):
     table = Table(table)
     ids, lists, orders = table.ids, table.lists, table.orders
-    mine[...] = jnp.zeros_like(mine)
     for k in range(ROWS):
         s = ids[1] * ROWS + k
+        order = orders[s]
+        where = [jnp.int32(-1)] * (RT // CT)
         for i in range(MAXT):
-            group = lists[s * MAXT + i] // CT
-
-            @pl.when((i < orders[s]) & (group // (RT // CT) == ids[0]))
-            def _():
-                mine[k, group % (RT // CT)] = panels[k, i]
-
+            group = lists[s * MAXT + i] // CT - ids[0] * (RT // CT)
+            for g in range(RT // CT):
+                where[g] = jnp.where((i < order) & (group == g), i, where[g])
+        for g in range(RT // CT):
+            piece = panels[k, jnp.maximum(where[g], 0)]
+            mine[k, g] = jnp.where(where[g] >= 0, piece, jnp.zeros_like(piece))
     copies = [pltpu.make_async_copy(mine, out.at[c], sems.at[c]) for c in range(COLS)]
     for copy in copies:
         copy.start()
@@ -333,7 +334,6 @@
         (top, bottom, *strip[1:]),
         (FAR, FAR),
     )
-    packed, ahead, across = lax.optimization_barrier((packed, ahead, across))
     tiles = lax.all_to_all(packed, COL, 0, 0, tiled=True)
     across = from_ring(jnp.stack(across), "c1")
     ahead = from_ring(jnp.stack(ahead), "c0")

time: 186 us -> 197 us (1.059)
  waiting for transfers between devices: 85.3 us -> 99.6 us
  blocking collectives: 17.8 us -> 15 us
    ppermute x18, waiting for transfers between devices: 59.3 us -> 74.8 us  [from_ring(): lax.ppermute(x, axis, [((i + k) % 4, i) for i in range(4)])]
    all_to_all x1, starting transfers between devices: 3.73 us -> 7.27 us  [steps(): arrived = lax.all_to_all(spread, COL, 0, 0, tiled=True)]
    ppermute x18, starting transfers between devices: 28.5 us -> 25.3 us  [from_ring(): lax.ppermute(x, axis, [((i + k) % 4, i) for i in range(4)])]
    all_to_all x1, starting transfers between devices: 3.9 us -> 6.9 us  [steps(): tiles = lax.all_to_all(packed, COL, 0, 0, tiled=True)]
    all_gather x1, blocking collectives: 17.8 us -> 15 us  [steps(): panels = lax.all_gather(panel, ROW, axis=0, tiled=False)]
    ppermute x8, starting transfers between devices: 13.2 us -> 10.5 us  [swapped(): return lax.ppermute(x, 'core', [(0, 1), (1, 0)])]
  transfers between devices with their start and end apart: 28 -> 28, of which waited for: 12 -> 11; matrix products, arithmetic and copies ran while one was open for 3% -> 2% of each run, Pallas kernels for 4% -> 8%
where the time goes in v4:
time: 197 us; the launch traced here: 194 us
  waiting for transfers between devices  99.6 us (51%)
  starting transfers between devices  50 us (25%)
  Pallas kernels  24.3 us (12%)
  blocking collectives  15 us (8%)
  local copies, waits for them, and re-layouts  3.64 us (2%)
    ppermute x18, waiting for transfers between devices, from_ring(): lax.ppermute(x, axis, [((i + k) % 4, i) for i in range(4)])  74.8 us
    ppermute x18, starting transfers between devices, from_ring(): lax.ppermute(x, axis, [((i + k) % 4, i) for i in range(4)])  25.3 us
    pallas_call x5, Pallas kernels, call(): pl.pallas_call(kernel, out_shape=outs, in_specs=[SMEM] * len(small) + [LO...  24.3 us
    all_to_all x1, waiting for transfers between devices, steps(): tiles = lax.all_to_all(packed, COL, 0, 0, tiled=True)  23.8 us
    all_gather x1, blocking collectives, steps(): panels = lax.all_gather(panel, ROW, axis=0, tiled=False)  15 us
    ppermute x8, starting transfers between devices, swapped(): return lax.ppermute(x, 'core', [(0, 1), (1, 0)])  10.5 us
    all_to_all x1, starting transfers between devices, steps(): arrived = lax.all_to_all(spread, COL, 0, 0, tiled=True)  7.27 us
    all_to_all x1, starting transfers between devices, steps(): tiles = lax.all_to_all(packed, COL, 0, 0, tiled=True)  6.9 us
  transfers between devices with their start and end apart: 28, of which 11 were waited for; matrix products, arithmetic and copies ran while one was open for 2% of the time, Pallas kernels for 8%

profile of v4, /device:TPU:1, one launch (start us, length us, event | category | flops | bytes accessed | tf_op | source)
XLA Modules:
  0.0 194.2 jit_solution(12939711005582994755)
XLA Ops:
  0.6 4.6 %collective-permute-start = (bf16[512,256]{1,0:T(8,128)(2,1)}, bf16[512,256]{1,0:T(8,128)(2,1)S(1)}, u32[]{:S(2)}, u32[]{:S(2)}) collective-permute-start(bf16[512,256]{1,0:T(8,128)(2,1)} %param.5), channel_id=1, source_target_pairs={{32,0},{64,32},{96,64},{0,96},{33,1},{65,33},{97,65},{1,97},{34,2}... | collective-permute-start | bytes 786440 | tf_op jit(solution)/shard_map/ppermute | solution.py:285
  5.3 0.0 collective-permute-start.1
  5.3 0.7 collective-permute-start.2
  6.0 1.5 collective-permute-start.3
  7.5 8.6 %collective-permute-done.refs_2_ = bf16[512,256]{1,0:T(8,128)(2,1)S(1)} collective-permute-done((bf16[512,256]{1,0:T(8,128)(2,1)}, bf16[512,256]{1,0:T(8,128)(2,1)S(1)}, u32[]{:S(2)}, u32[]{:S(2)}) %collective-permute-start) | collective-permute-done | bytes 262176 | tf_op jit(solution)/shard_map/ppermute | solution.py:285
  16.1 1.7 collective-permute-start.4
  17.7 0.0 collective-permute-start.5
  17.7 2.5 %collective-permute-done.2.refs_4_ = bf16[512,256]{1,0:T(8,128)(2,1)S(1)} collective-permute-done((bf16[512,256]{1,0:T(8,128)(2,1)}, bf16[512,256]{1,0:T(8,128)(2,1)S(1)}, u32[]{:S(2)}, u32[]{:S(2)}) %collective-permute-start.2) | collective-permute-done | bytes 262176 | tf_op jit(solution)/shard_map/ppermute | solution.py:285
  20.3 0.8 collective-permute-start.6
  21.0 0.8 copy.12
  21.8 0.1 reshape.36
  21.9 0.8 reshape.37
  22.7 0.7 concatenate.3.table
  23.4 1.0 slice_bitcast_fusion
  24.5 0.0 collective-permute-done.4.refs_6_
  24.5 3.4 %shard_map.68 = (bf16[16,4,128,128]{3,2,1,0:T(8,128)(2,1)}, bf16[8,128,128]{2,1,0:T(8,128)(2,1)}) custom-call(s32[2178]{0:T(1024)S(1)} %concatenate.3.table, bf16[256,256]{1,0:T(8,128)(2,1)S(1)} %get-tuple-element.9.refs_0_, bf16[256,256]{1,0:T(8,128)(2,1)S(1)} %get-tuple-element.8.refs_1_, bf16[512,256]{1,0:T(8,128)(2,1)S(1)} %collective-permute-done.refs_2_, ...), custom_call_target="tpu_custom_call" | custom-call | tf_op jit(solution)/shard_map/pallas_call | solution.py:298
  27.9 0.0 copy-start
  27.9 6.9 %all-to-all-start = ((bf16[16,4,128,128]{3,2,1,0:T(8,128)(2,1)}), bf16[16,4,128,128]{3,2,1,0:T(8,128)(2,1)S(1)}, u32[]{:S(2)}, u32[]{:S(2)}) async-start(bf16[16,4,128,128]{3,2,1,0:T(8,128)(2,1)} %get-tuple-element.4), calls=%async_computation | async-start | bytes 4194304 | tf_op jit(solution)/shard_map/all_to_all | solution.py:337
  34.8 2.6 %collective-permute-start.7 = (bf16[256,256]{1,0:T(8,128)(2,1)S(1)}, bf16[256,256]{1,0:T(8,128)(2,1)S(1)}, u32[]{:S(2)}, u32[]{:S(2)}) collective-permute-start(bf16[256,256]{1,0:T(8,128)(2,1)S(1)} %get-tuple-element.9.refs_0_), channel_id=1, source_target_pairs={{1,0},{2,1},{3,2},{0,3},{5,4},{6,5},{7,6},{4,7},{9,8},{10,9},{11,1... | collective-permute-start | bytes 393224 | tf_op jit(solution)/shard_map/ppermute | solution.py:285
  37.4 0.6 collective-permute-start.8
  38.0 0.6 collective-permute-start.9
  39.2 23.8 %all-to-all-done.tiles = bf16[16,4,128,128]{3,2,1,0:T(8,128)(2,1)S(1)} async-done(((bf16[16,4,128,128]{3,2,1,0:T(8,128)(2,1)}), bf16[16,4,128,128]{3,2,1,0:T(8,128)(2,1)S(1)}, u32[]{:S(2)}, u32[]{:S(2)}) %all-to-all-start) | async-done | bytes 2097184 | tf_op jit(solution)/shard_map/all_to_all | solution.py:337
  63.0 8.8 %shard_map.69 = bf16[8,32,128]{2,1,0:T(8,128)(2,1)S(1)} custom-call(s32[2178]{0:T(1024)S(1)} %concatenate.3.table, f32[1]{0:T(128)S(6)} %copy.14.shift, bf16[16,4,128,128]{3,2,1,0:T(8,128)(2,1)S(1)} %all-to-all-done.tiles, bf16[8,128,128]{2,1,0:T(8,128)(2,1)S(1)} %copy-done), custom_call_target="tpu_custom_call" | custom-call | tf_op jit(solution)/shard_map/pallas_call | solution.py:298
  71.8 15.0 %all-gather = bf16[64,32,128]{2,1,0:T(8,128)(2,1)S(1)} all-gather(bf16[8,32,128]{2,1,0:T(8,128)(2,1)S(1)} %shard_map.69), channel_id=2, replica_groups=mesh['z'=4,'core'=2,'c0'=4,'c1'=4] {'z','core'}, dimensions={0}, use_global_device_ids=true | all-gather | bytes 589824 | tf_op jit(solution)/shard_map/all_gather | solution.py:341
  86.8 2.7 %shard_map.70 = bf16[16,8,2,32,128]{4,3,2,1,0:T(8,128)(2,1)} custom-call(s32[2178]{0:T(1024)S(1)} %concatenate.3.table, bf16[8,8,32,128]{3,2,1,0:T(8,128)(2,1)S(1)} %bitcast.13), custom_call_target="tpu_custom_call" | custom-call | tf_op jit(solution)/shard_map/pallas_call | solution.py:298
  89.5 7.3 %all-to-all-start.1 = ((bf16[16,8,2,32,128]{4,3,2,1,0:T(8,128)(2,1)}), bf16[16,8,2,32,128]{4,3,2,1,0:T(8,128)(2,1)S(1)}, u32[]{:S(2)}, u32[]{:S(2)}) async-start(bf16[16,8,2,32,128]{4,3,2,1,0:T(8,128)(2,1)} %shard_map.70), calls=%async_computation.1 | async-start | bytes 4194304 | tf_op jit(solution)/shard_map/all_to_all | solution.py:350
  96.8 0.0 collective-permute-done.8
  96.8 0.0 collective-permute-done.9
  96.8 0.1 pad_maximum_fusion.a0
  96.9 2.6 %collective-permute-start.10 = (bf16[4,256,256]{2,1,0:T(8,128)(2,1)S(1)}, bf16[4,256,256]{2,1,0:T(8,128)(2,1)S(1)}, u32[]{:S(2)}, u32[]{:S(2)}) collective-permute-start(bf16[4,256,256]{2,1,0:T(8,128)(2,1)S(1)} %pad_maximum_fusion.a0), channel_id=1, source_target_pairs={{4,0},{8,4},{12,8},{0,12},{5,1},{9,5},{13,9},{1,13},{6,2},{10,6},{... | collective-permute-start | bytes 1572872 | tf_op jit(solution)/shard_map/ppermute | solution.py:285
  99.6 0.0 collective-permute-start.15
  99.6 2.7 %collective-permute-start.13 = (bf16[256,256]{1,0:T(8,128)(2,1)S(1)}, bf16[256,256]{1,0:T(8,128)(2,1)S(1)}, u32[]{:S(2)}, u32[]{:S(2)}) collective-permute-start(bf16[256,256]{1,0:T(8,128)(2,1)S(1)} %get-tuple-element.8.refs_1_), channel_id=1, source_target_pairs={{4,0},{8,4},{12,8},{0,12},{5,1},{9,5},{13,9},{1,13},{6,2},{10,6},{... | collective-permute-start | bytes 393224 | tf_op jit(solution)/shard_map/ppermute | solution.py:285
  102.2 3.0 %collective-permute-start.11 = (bf16[4,256,256]{2,1,0:T(8,128)(2,1)S(1)}, bf16[4,256,256]{2,1,0:T(8,128)(2,1)S(1)}, u32[]{:S(2)}, u32[]{:S(2)}) collective-permute-start(bf16[4,256,256]{2,1,0:T(8,128)(2,1)S(1)} %pad_maximum_fusion.a0), channel_id=1, source_target_pairs={{8,0},{12,4},{0,8},{4,12},{9,1},{13,5},{1,9},{5,13},{10,2},{14,6},... | collective-permute-start | bytes 1572872 | tf_op jit(solution)/shard_map/ppermute | solution.py:285
  105.2 20.9 %collective-permute-done.15 = bf16[256,256]{1,0:T(8,128)(2,1)S(1)} collective-permute-done((bf16[256,256]{1,0:T(8,128)(2,1)S(1)}, bf16[256,256]{1,0:T(8,128)(2,1)S(1)}, u32[]{:S(2)}, u32[]{:S(2)}) %collective-permute-start.15) | collective-permute-done | bytes 131104 | tf_op jit(solution)/shard_map/ppermute | solution.py:285
  126.1 0.0 collective-permute-start.12
  126.1 9.7 %collective-permute-done.13 = bf16[256,256]{1,0:T(8,128)(2,1)S(1)} collective-permute-done((bf16[256,256]{1,0:T(8,128)(2,1)S(1)}, bf16[256,256]{1,0:T(8,128)(2,1)S(1)}, u32[]{:S(2)}, u32[]{:S(2)}) %collective-permute-start.13) | collective-permute-done | bytes 131104 | tf_op jit(solution)/shard_map/ppermute | solution.py:285
  135.8 0.1 pad_maximum_fusion.1.b0
  135.9 0.0 copy-start.2
  135.9 0.0 copy-start.1
  135.9 4.5 %collective-permute-start.16 = (bf16[4,256,256]{2,1,0:T(8,128)(2,1)S(1)}, bf16[4,256,256]{2,1,0:T(8,128)(2,1)S(1)}, u32[]{:S(2)}, u32[]{:S(2)}) collective-permute-start(bf16[4,256,256]{2,1,0:T(8,128)(2,1)S(1)} %pad_maximum_fusion.1.b0), channel_id=1, source_target_pairs={{1,0},{2,1},{3,2},{0,3},{5,4},{6,5},{7,6},{4,7},{9,8},{10,9},{11,1... | collective-permute-start | bytes 1572872 | tf_op jit(solution)/shard_map/ppermute | solution.py:285
  140.4 0.6 collective-permute-start.17
  140.9 0.0 collective-permute-done.10.a1
  140.9 0.8 collective-permute-start.18
  141.7 0.0 collective-permute-done.11.a2
  141.7 11.8 %collective-permute-done.12.a3 = bf16[4,256,256]{2,1,0:T(8,128)(2,1)S(1)} collective-permute-done((bf16[4,256,256]{2,1,0:T(8,128)(2,1)S(1)}, bf16[4,256,256]{2,1,0:T(8,128)(2,1)S(1)}, u32[]{:S(2)}, u32[]{:S(2)}) %collective-permute-start.12) | collective-permute-done | bytes 524320 | tf_op jit(solution)/shard_map/ppermute | solution.py:285
  153.5 7.0 %collective-permute-done.16.b1 = bf16[4,256,256]{2,1,0:T(8,128)(2,1)S(1)} collective-permute-done((bf16[4,256,256]{2,1,0:T(8,128)(2,1)S(1)}, bf16[4,256,256]{2,1,0:T(8,128)(2,1)S(1)}, u32[]{:S(2)}, u32[]{:S(2)}) %collective-permute-start.16) | collective-permute-done | bytes 524320 | tf_op jit(solution)/shard_map/ppermute | solution.py:285
  160.6 6.4 %collective-permute-done.18.b3 = bf16[4,256,256]{2,1,0:T(8,128)(2,1)S(1)} collective-permute-done((bf16[4,256,256]{2,1,0:T(8,128)(2,1)S(1)}, bf16[4,256,256]{2,1,0:T(8,128)(2,1)S(1)}, u32[]{:S(2)}, u32[]{:S(2)}) %collective-permute-start.18) | collective-permute-done | bytes 524320 | tf_op jit(solution)/shard_map/ppermute | solution.py:285
  167.0 4.7 %shard_map.71.refs_0_ = bf16[512,256]{1,0:T(8,128)(2,1)S(1)} custom-call(s32[2178]{0:T(1024)S(1)} %concatenate.3.table, bf16[4,256,256]{2,1,0:T(8,128)(2,1)S(1)} %pad_maximum_fusion.a0, bf16[4,256,256]{2,1,0:T(8,128)(2,1)S(1)} %collective-permute-done.10.a1, bf16[4,256,256]{2,1,0:T(8,128)(2,1)S(1)} %collective-permute-done.11.a2, ...), custom_call_target="tpu_custom_call" | custom-call | tf_op jit(solution)/shard_map/pallas_call | solution.py:298
  171.7 0.7 collective-permute-start.19
  172.3 0.7 collective-permute-start.20
  173.0 0.8 collective-permute-start.21
  173.8 1.3 collective-permute-start.22
  175.1 4.0 %collective-permute-done.19.refs_1_ = bf16[512,256]{1,0:T(8,128)(2,1)S(1)} collective-permute-done((bf16[512,256]{1,0:T(8,128)(2,1)S(1)}, bf16[512,256]{1,0:T(8,128)(2,1)S(1)}, u32[]{:S(2)}, u32[]{:S(2)}) %collective-permute-start.19) | collective-permute-done | bytes 262176 | tf_op jit(solution)/shard_map/ppermute | solution.py:285
  179.1 2.3 %collective-permute-start.23 = (bf16[512,256]{1,0:T(8,128)(2,1)S(1)}, bf16[512,256]{1,0:T(8,128)(2,1)}, u32[]{:S(2)}, u32[]{:S(2)}) collective-permute-start(bf16[512,256]{1,0:T(8,128)(2,1)S(1)} %collective-permute-done.19.refs_1_), channel_id=1, source_target_pairs={{0,16},{16,0},{1,17},{17,1},{2,18},{18,2},{3,19},{19,3},{4,20},{20... | collective-permute-start | bytes 786440 | tf_op jit(solution)/shard_map/ppermute | solution.py:289
  181.4 0.0 collective-permute-done.20.refs_2_
  181.4 2.4 %collective-permute-start.24 = (bf16[512,256]{1,0:T(8,128)(2,1)S(1)}, bf16[512,256]{1,0:T(8,128)(2,1)}, u32[]{:S(2)}, u32[]{:S(2)}) collective-permute-start(bf16[512,256]{1,0:T(8,128)(2,1)S(1)} %collective-permute-done.20.refs_2_), channel_id=1, source_target_pairs={{0,16},{16,0},{1,17},{17,1},{2,18},{18,2},{3,19},{19,3},{4,20},{20... | collective-permute-start | bytes 786440 | tf_op jit(solution)/shard_map/ppermute | solution.py:289
  183.8 3.9 %collective-permute-done.21.refs_3_ = bf16[512,256]{1,0:T(8,128)(2,1)S(1)} collective-permute-done((bf16[512,256]{1,0:T(8,128)(2,1)S(1)}, bf16[512,256]{1,0:T(8,128)(2,1)S(1)}, u32[]{:S(2)}, u32[]{:S(2)}) %collective-permute-start.21) | collective-permute-done | bytes 262176 | tf_op jit(solution)/shard_map/ppermute | solution.py:285
  187.7 0.5 collective-permute-start.25
  188.2 0.1 and_reduce_fusion
  188.3 0.1 copy.13
  188.4 0.1 reshape.38.present
  188.5 0.0 collective-permute-done.22.refs_4_
  188.6 0.9 collective-permute-done.25.refs_7_
  189.5 4.8 %shard_map.72 = (bf16[512,256]{1,0:T(8,128)(2,1)}, f32[512,256]{1,0:T(8,128)}) custom-call(s32[2178]{0:T(1024)S(1)} %concatenate.3.table, s32[512]{0:T(512)S(1)} %reshape.38.present, bf16[16,8,2,32,128]{4,3,2,1,0:T(8,128)(2,1)S(1)} %all-to-all-done.1.pieces, bf16[512,256]{1,0:T(8,128)(2,1)S(1)} %shard_map.71.refs_0_, ...), custom_call_target="tpu_custom_call" | custom-call | tf_op jit(solution)/shard_map/pallas_call | solution.py:298
  (17 shorter events, 0.1 us)
Async XLA Ops:
  0.6 15.4 %collective-permute-start = (bf16[512,256]{1,0:T(8,128)(2,1)}, bf16[512,256]{1,0:T(8,128)(2,1)S(1)}, u32[]{:S(2)}, u32[]{:S(2)}) collective-permute-start(bf16[512,256]{1,0:T(8,128)(2,1)} %param.5), channel_id=1, source_target_pairs={{32,0},{64,32},{96,64},{0,96},{33,1},{65,33},{97,65},{1,97},{34,2}... | collective-permute-start | bytes 786440 | tf_op jit(solution)/shard_map/ppermute | solution.py:285
  5.3 12.5 %collective-permute-start.1 = (bf16[512,256]{1,0:T(8,128)(2,1)}, bf16[512,256]{1,0:T(8,128)(2,1)S(1)}, u32[]{:S(2)}, u32[]{:S(2)}) collective-permute-start(bf16[512,256]{1,0:T(8,128)(2,1)} %param.5), channel_id=1, source_target_pairs={{64,0},{96,32},{0,64},{32,96},{65,1},{97,33},{1,65},{33,97},{66,2}... | collective-permute-start | bytes 786440 | tf_op jit(solution)/shard_map/ppermute | solution.py:285
  5.3 15.0 %collective-permute-start.2 = (bf16[512,256]{1,0:T(8,128)(2,1)}, bf16[512,256]{1,0:T(8,128)(2,1)S(1)}, u32[]{:S(2)}, u32[]{:S(2)}) collective-permute-start(bf16[512,256]{1,0:T(8,128)(2,1)} %param.5), channel_id=1, source_target_pairs={{96,0},{0,32},{32,64},{64,96},{97,1},{1,33},{33,65},{65,97},{98,2}... | collective-permute-start | bytes 786440 | tf_op jit(solution)/shard_map/ppermute | solution.py:285
  6.0 18.5 %collective-permute-start.3 = (bf16[512,256]{1,0:T(8,128)(2,1)}, bf16[512,256]{1,0:T(8,128)(2,1)S(1)}, u32[]{:S(2)}, u32[]{:S(2)}) collective-permute-start(bf16[512,256]{1,0:T(8,128)(2,1)} %param.5), channel_id=1, source_target_pairs={{0,16},{16,0},{1,17},{17,1},{2,18},{18,2},{3,19},{19,3},{4,20},{20... | collective-permute-start | bytes 786440 | tf_op jit(solution)/shard_map/ppermute | solution.py:289
  16.1 8.4 %collective-permute-start.4 = (bf16[512,256]{1,0:T(8,128)(2,1)S(1)}, bf16[512,256]{1,0:T(8,128)(2,1)S(1)}, u32[]{:S(2)}, u32[]{:S(2)}) collective-permute-start(bf16[512,256]{1,0:T(8,128)(2,1)S(1)} %collective-permute-done.refs_2_), channel_id=1, source_target_pairs={{0,16},{16,0},{1,17},{17,1},{2,18},{18,2},{3,19},{19,3},{4,20},{20... | collective-permute-start | bytes 786440 | tf_op jit(solution)/shard_map/ppermute | solution.py:289
  17.7 6.7 %collective-permute-start.5 = (bf16[512,256]{1,0:T(8,128)(2,1)S(1)}, bf16[512,256]{1,0:T(8,128)(2,1)S(1)}, u32[]{:S(2)}, u32[]{:S(2)}) collective-permute-start(bf16[512,256]{1,0:T(8,128)(2,1)S(1)} %collective-permute-done.1.refs_3_), channel_id=1, source_target_pairs={{0,16},{16,0},{1,17},{17,1},{2,18},{18,2},{3,19},{19,3},{4,20},{20... | collective-permute-start | bytes 786440 | tf_op jit(solution)/shard_map/ppermute | solution.py:289
  20.3 4.2 %collective-permute-start.6 = (bf16[512,256]{1,0:T(8,128)(2,1)S(1)}, bf16[512,256]{1,0:T(8,128)(2,1)S(1)}, u32[]{:S(2)}, u32[]{:S(2)}) collective-permute-start(bf16[512,256]{1,0:T(8,128)(2,1)S(1)} %collective-permute-done.2.refs_4_), channel_id=1, source_target_pairs={{0,16},{16,0},{1,17},{17,1},{2,18},{18,2},{3,19},{19,3},{4,20},{20... | collective-permute-start | bytes 786440 | tf_op jit(solution)/shard_map/ppermute | solution.py:289
  27.9 35.1 %copy-start = (bf16[8,128,128]{2,1,0:T(8,128)(2,1)S(1)}, bf16[8,128,128]{2,1,0:T(8,128)(2,1)}, u32[]{:S(2)}) copy-start(bf16[8,128,128]{2,1,0:T(8,128)(2,1)} %get-tuple-element.5.first) | copy-start | bytes 786436
  27.9 35.1 %all-to-all-start = ((bf16[16,4,128,128]{3,2,1,0:T(8,128)(2,1)}), bf16[16,4,128,128]{3,2,1,0:T(8,128)(2,1)S(1)}, u32[]{:S(2)}, u32[]{:S(2)}) async-start(bf16[16,4,128,128]{3,2,1,0:T(8,128)(2,1)} %get-tuple-element.4), calls=%async_computation | async-start | bytes 4194304 | tf_op jit(solution)/shard_map/all_to_all | solution.py:337
  34.8 62.0 %collective-permute-start.7 = (bf16[256,256]{1,0:T(8,128)(2,1)S(1)}, bf16[256,256]{1,0:T(8,128)(2,1)S(1)}, u32[]{:S(2)}, u32[]{:S(2)}) collective-permute-start(bf16[256,256]{1,0:T(8,128)(2,1)S(1)} %get-tuple-element.9.refs_0_), channel_id=1, source_target_pairs={{1,0},{2,1},{3,2},{0,3},{5,4},{6,5},{7,6},{4,7},{9,8},{10,9},{11,1... | collective-permute-start | bytes 393224 | tf_op jit(solution)/shard_map/ppermute | solution.py:285
  37.4 59.4 %collective-permute-start.8 = (bf16[256,256]{1,0:T(8,128)(2,1)S(1)}, bf16[256,256]{1,0:T(8,128)(2,1)S(1)}, u32[]{:S(2)}, u32[]{:S(2)}) collective-permute-start(bf16[256,256]{1,0:T(8,128)(2,1)S(1)} %get-tuple-element.9.refs_0_), channel_id=1, source_target_pairs={{2,0},{3,1},{0,2},{1,3},{6,4},{7,5},{4,6},{5,7},{10,8},{11,9},{8,1... | collective-permute-start | bytes 393224 | tf_op jit(solution)/shard_map/ppermute | solution.py:285
  38.0 58.9 %collective-permute-start.9 = (bf16[256,256]{1,0:T(8,128)(2,1)S(1)}, bf16[256,256]{1,0:T(8,128)(2,1)S(1)}, u32[]{:S(2)}, u32[]{:S(2)}) collective-permute-start(bf16[256,256]{1,0:T(8,128)(2,1)S(1)} %get-tuple-element.9.refs_0_), channel_id=1, source_target_pairs={{3,0},{0,1},{1,2},{2,3},{7,4},{4,5},{5,6},{6,7},{11,8},{8,9},{9,10... | collective-permute-start | bytes 393224 | tf_op jit(solution)/shard_map/ppermute | solution.py:285
  89.5 100.0 %all-to-all-start.1 = ((bf16[16,8,2,32,128]{4,3,2,1,0:T(8,128)(2,1)}), bf16[16,8,2,32,128]{4,3,2,1,0:T(8,128)(2,1)S(1)}, u32[]{:S(2)}, u32[]{:S(2)}) async-start(bf16[16,8,2,32,128]{4,3,2,1,0:T(8,128)(2,1)} %shard_map.70), calls=%async_computation.1 | async-start | bytes 4194304 | tf_op jit(solution)/shard_map/all_to_all | solution.py:350
  96.9 44.0 %collective-permute-start.10 = (bf16[4,256,256]{2,1,0:T(8,128)(2,1)S(1)}, bf16[4,256,256]{2,1,0:T(8,128)(2,1)S(1)}, u32[]{:S(2)}, u32[]{:S(2)}) collective-permute-start(bf16[4,256,256]{2,1,0:T(8,128)(2,1)S(1)} %pad_maximum_fusion.a0), channel_id=1, source_target_pairs={{4,0},{8,4},{12,8},{0,12},{5,1},{9,5},{13,9},{1,13},{6,2},{10,6},{... | collective-permute-start | bytes 1572872 | tf_op jit(solution)/shard_map/ppermute | solution.py:285
  99.6 26.6 %collective-permute-start.15 = (bf16[256,256]{1,0:T(8,128)(2,1)S(1)}, bf16[256,256]{1,0:T(8,128)(2,1)S(1)}, u32[]{:S(2)}, u32[]{:S(2)}) collective-permute-start(bf16[256,256]{1,0:T(8,128)(2,1)S(1)} %get-tuple-element.8.refs_1_), channel_id=1, source_target_pairs={{12,0},{0,4},{4,8},{8,12},{13,1},{1,5},{5,9},{9,13},{14,2},{2,6},{... | collective-permute-start | bytes 393224 | tf_op jit(solution)/shard_map/ppermute | solution.py:285
  99.6 36.3 %collective-permute-start.13 = (bf16[256,256]{1,0:T(8,128)(2,1)S(1)}, bf16[256,256]{1,0:T(8,128)(2,1)S(1)}, u32[]{:S(2)}, u32[]{:S(2)}) collective-permute-start(bf16[256,256]{1,0:T(8,128)(2,1)S(1)} %get-tuple-element.8.refs_1_), channel_id=1, source_target_pairs={{4,0},{8,4},{12,8},{0,12},{5,1},{9,5},{13,9},{1,13},{6,2},{10,6},{... | collective-permute-start | bytes 393224 | tf_op jit(solution)/shard_map/ppermute | solution.py:285
  102.2 33.6 %collective-permute-start.14 = (bf16[256,256]{1,0:T(8,128)(2,1)S(1)}, bf16[256,256]{1,0:T(8,128)(2,1)S(1)}, u32[]{:S(2)}, u32[]{:S(2)}) collective-permute-start(bf16[256,256]{1,0:T(8,128)(2,1)S(1)} %get-tuple-element.8.refs_1_), channel_id=1, source_target_pairs={{8,0},{12,4},{0,8},{4,12},{9,1},{13,5},{1,9},{5,13},{10,2},{14,6},... | collective-permute-start | bytes 393224 | tf_op jit(solution)/shard_map/ppermute | solution.py:285
  102.2 39.5 %collective-permute-start.11 = (bf16[4,256,256]{2,1,0:T(8,128)(2,1)S(1)}, bf16[4,256,256]{2,1,0:T(8,128)(2,1)S(1)}, u32[]{:S(2)}, u32[]{:S(2)}) collective-permute-start(bf16[4,256,256]{2,1,0:T(8,128)(2,1)S(1)} %pad_maximum_fusion.a0), channel_id=1, source_target_pairs={{8,0},{12,4},{0,8},{4,12},{9,1},{13,5},{1,9},{5,13},{10,2},{14,6},... | collective-permute-start | bytes 1572872 | tf_op jit(solution)/shard_map/ppermute | solution.py:285
  126.1 27.4 %collective-permute-start.12 = (bf16[4,256,256]{2,1,0:T(8,128)(2,1)S(1)}, bf16[4,256,256]{2,1,0:T(8,128)(2,1)S(1)}, u32[]{:S(2)}, u32[]{:S(2)}) collective-permute-start(bf16[4,256,256]{2,1,0:T(8,128)(2,1)S(1)} %pad_maximum_fusion.a0), channel_id=1, source_target_pairs={{12,0},{0,4},{4,8},{8,12},{13,1},{1,5},{5,9},{9,13},{14,2},{2,6},{... | collective-permute-start | bytes 1572872 | tf_op jit(solution)/shard_map/ppermute | solution.py:285
  135.9 52.3 %copy-start.2 = (s32[128]{0:T(128)S(1)}, s32[128]{0:T(128)}, u32[]{:S(2)}) copy-start(s32[128]{0:T(128)} %param.8) | copy-start | bytes 1540
  135.9 52.3 %copy-start.1 = (s32[128,8]{0,1:T(8,128)S(1)}, s32[128,8]{0,1:T(8,128)}, u32[]{:S(2)}) copy-start(s32[128,8]{0,1:T(8,128)} %param.7) | copy-start | bytes 12292
  135.9 24.6 %collective-permute-start.16 = (bf16[4,256,256]{2,1,0:T(8,128)(2,1)S(1)}, bf16[4,256,256]{2,1,0:T(8,128)(2,1)S(1)}, u32[]{:S(2)}, u32[]{:S(2)}) collective-permute-start(bf16[4,256,256]{2,1,0:T(8,128)(2,1)S(1)} %pad_maximum_fusion.1.b0), channel_id=1, source_target_pairs={{1,0},{2,1},{3,2},{0,3},{5,4},{6,5},{7,6},{4,7},{9,8},{10,9},{11,1... | collective-permute-start | bytes 1572872 | tf_op jit(solution)/shard_map/ppermute | solution.py:285
  140.4 20.2 %collective-permute-start.17 = (bf16[4,256,256]{2,1,0:T(8,128)(2,1)S(1)}, bf16[4,256,256]{2,1,0:T(8,128)(2,1)S(1)}, u32[]{:S(2)}, u32[]{:S(2)}) collective-permute-start(bf16[4,256,256]{2,1,0:T(8,128)(2,1)S(1)} %pad_maximum_fusion.1.b0), channel_id=1, source_target_pairs={{2,0},{3,1},{0,2},{1,3},{6,4},{7,5},{4,6},{5,7},{10,8},{11,9},{8,1... | collective-permute-start | bytes 1572872 | tf_op jit(solution)/shard_map/ppermute | solution.py:285
  140.9 26.0 %collective-permute-start.18 = (bf16[4,256,256]{2,1,0:T(8,128)(2,1)S(1)}, bf16[4,256,256]{2,1,0:T(8,128)(2,1)S(1)}, u32[]{:S(2)}, u32[]{:S(2)}) collective-permute-start(bf16[4,256,256]{2,1,0:T(8,128)(2,1)S(1)} %pad_maximum_fusion.1.b0), channel_id=1, source_target_pairs={{3,0},{0,1},{1,2},{2,3},{7,4},{4,5},{5,6},{6,7},{11,8},{8,9},{9,10... | collective-permute-start | bytes 1572872 | tf_op jit(solution)/shard_map/ppermute | solution.py:285
  171.7 7.4 %collective-permute-start.19 = (bf16[512,256]{1,0:T(8,128)(2,1)S(1)}, bf16[512,256]{1,0:T(8,128)(2,1)S(1)}, u32[]{:S(2)}, u32[]{:S(2)}) collective-permute-start(bf16[512,256]{1,0:T(8,128)(2,1)S(1)} %shard_map.71.refs_0_), channel_id=1, source_target_pairs={{32,0},{64,32},{96,64},{0,96},{33,1},{65,33},{97,65},{1,97},{34,2}... | collective-permute-start | bytes 786440 | tf_op jit(solution)/shard_map/ppermute | solution.py:285
  172.3 9.1 %collective-permute-start.20 = (bf16[512,256]{1,0:T(8,128)(2,1)S(1)}, bf16[512,256]{1,0:T(8,128)(2,1)S(1)}, u32[]{:S(2)}, u32[]{:S(2)}) collective-permute-start(bf16[512,256]{1,0:T(8,128)(2,1)S(1)} %shard_map.71.refs_0_), channel_id=1, source_target_pairs={{64,0},{96,32},{0,64},{32,96},{65,1},{97,33},{1,65},{33,97},{66,2}... | collective-permute-start | bytes 786440 | tf_op jit(solution)/shard_map/ppermute | solution.py:285
  173.0 14.7 %collective-permute-start.21 = (bf16[512,256]{1,0:T(8,128)(2,1)S(1)}, bf16[512,256]{1,0:T(8,128)(2,1)S(1)}, u32[]{:S(2)}, u32[]{:S(2)}) collective-permute-start(bf16[512,256]{1,0:T(8,128)(2,1)S(1)} %shard_map.71.refs_0_), channel_id=1, source_target_pairs={{96,0},{0,32},{32,64},{64,96},{97,1},{1,33},{33,65},{65,97},{98,2}... | collective-permute-start | bytes 786440 | tf_op jit(solution)/shard_map/ppermute | solution.py:285
  173.8 14.8 %collective-permute-start.22 = (bf16[512,256]{1,0:T(8,128)(2,1)S(1)}, bf16[512,256]{1,0:T(8,128)(2,1)S(1)}, u32[]{:S(2)}, u32[]{:S(2)}) collective-permute-start(bf16[512,256]{1,0:T(8,128)(2,1)S(1)} %shard_map.71.refs_0_), channel_id=1, source_target_pairs={{0,16},{16,0},{1,17},{17,1},{2,18},{18,2},{3,19},{19,3},{4,20},{20... | collective-permute-start | bytes 786440 | tf_op jit(solution)/shard_map/ppermute | solution.py:289
  179.1 9.4 %collective-permute-start.23 = (bf16[512,256]{1,0:T(8,128)(2,1)S(1)}, bf16[512,256]{1,0:T(8,128)(2,1)}, u32[]{:S(2)}, u32[]{:S(2)}) collective-permute-start(bf16[512,256]{1,0:T(8,128)(2,1)S(1)} %collective-permute-done.19.refs_1_), channel_id=1, source_target_pairs={{0,16},{16,0},{1,17},{17,1},{2,18},{18,2},{3,19},{19,3},{4,20},{20... | collective-permute-start | bytes 786440 | tf_op jit(solution)/shard_map/ppermute | solution.py:289
  181.4 7.2 %collective-permute-start.24 = (bf16[512,256]{1,0:T(8,128)(2,1)S(1)}, bf16[512,256]{1,0:T(8,128)(2,1)}, u32[]{:S(2)}, u32[]{:S(2)}) collective-permute-start(bf16[512,256]{1,0:T(8,128)(2,1)S(1)} %collective-permute-done.20.refs_2_), channel_id=1, source_target_pairs={{0,16},{16,0},{1,17},{17,1},{2,18},{18,2},{3,19},{19,3},{4,20},{20... | collective-permute-start | bytes 786440 | tf_op jit(solution)/shard_map/ppermute | solution.py:289
  187.7 1.8 collective-permute-start.25
